TPU v7x, 512 devices: a whole 4x8x8 slice. The times are simulated.
512 devices in a mesh: dp: 8 (over x, core), expert: 64 (over y, z).
Axes of the slice: x: 4, y: 8, z: 8, core: 2. Of those that a mesh axis runs over, the one named last changes fastest.
Arguments:
- cotangent: bfloat16 [65536, 3584], P(('dp', 'expert')), may hold values from -0.59765625 to 0.59765625
- expert_ids: int32 [65536, 1], P(('dp', 'expert')), may hold values from 0 to 15; in each aligned block of 128 rows (0 to 127, 128 to 255, ...) at most 12 rows name the same one
- route_weights: float32 [65536, 1], P(('dp', 'expert')), may hold values from 0.1 to 1
- gate_pre: bfloat16 [6144, 16384], P('dp', 'expert'), may hold values from -5 to 5
- up_pre: bfloat16 [6144, 16384], P('dp', 'expert'), may hold values from -5 to 5
- down_weight: bfloat16 [3584, 16384], P('dp', 'expert'), may hold values from -0.1875 to 0.1875
Outputs:
- weight_grad: bfloat16 [3584, 16384], P('dp', 'expert')
- gate_grad: bfloat16 [6144, 16384], P('dp', 'expert')
- up_grad: bfloat16 [6144, 16384], P('dp', 'expert')
Inputs may be any that keep to these rules, and one draw needn't show every extreme that they name: `expert_ids`: each token names one expert. Among the tokens of one device, at most 12 name the same expert, and in every draw some expert is named by exactly 12 tokens of some device.
All inputs are finite; a program needn't handle non-finite values.
Results may differ from a plain program's by a relative error of at most 0.013.
Values may be sent and summed in bfloat16 or wider, within the bound.
No kernel may reach another device: no remote copies, remote signals or barrier semaphores. Data moves between devices by JAX's collectives and lax.ppermute only.
A program may use at most 64 MiB of HBM per device.

v0:
```python
import jax
import jax.numpy as jnp
from jax import lax
from jax.sharding import PartitionSpec as P

SPLIT = 4


def sent_to_all(array, axis):
    copies = jnp.broadcast_to(array, (lax.axis_size(axis), *array.shape))
    return lax.all_to_all(copies, axis, split_axis=0, concat_axis=0, tiled=True)


def laid_out(parts, dim):
    parts = jnp.moveaxis(parts, 0, dim)
    lengths = parts.shape
    return parts.reshape(*lengths[:dim], lengths[dim] * lengths[dim + 1], *lengths[dim + 2 :])


def gathered_copies(array, axis, dim):
    parts = sent_to_all(array, axis)
    return laid_out(parts, dim)


def split_up(array, dim, count):
    before, after = (array.shape[:dim], array.shape[dim + 1 :])
    return jnp.moveaxis(array.reshape(*before, count, -1, *after), dim, 0)


def sum_at_owner(array, axis, dim):
    parts = split_up(array, dim, lax.axis_size(axis))
    arrived = lax.all_to_all(parts, axis, split_axis=0, concat_axis=0, tiled=True)
    return arrived.astype(jnp.float32).sum(axis=0)


def slot_buffer(cotangent, expert_ids, route_weights, experts, capacity):
    columns = lax.broadcasted_iota(jnp.int32, (1, 1, experts), 2)
    onehot = (expert_ids[:, :, None] == columns).astype(jnp.int32)
    touched = jnp.sum(onehot, axis=1)
    earlier = jnp.cumsum(touched, axis=0) - touched
    position = jnp.sum(onehot * earlier[:, None, :], axis=2)
    target = expert_ids * capacity + position
    places = lax.broadcasted_iota(jnp.int32, (1, 1, experts * capacity), 2)
    chosen = (target[:, :, None] == places).astype(jnp.float32)
    picker = jnp.sum(chosen, axis=1)
    slot_scale = jnp.sum(chosen * route_weights[:, :, None], axis=(0, 1))
    picked = lax.dot_general(
        picker.astype(jnp.bfloat16),
        cotangent,
        (((0,), (0,)), ((), ())),
        preferred_element_type=jnp.float32,
    )
    return (picked * slot_scale[:, None]).astype(jnp.bfloat16)


def activations(gate_rows, up_rows, upstream):
    gate_full = gate_rows.astype(jnp.float32)
    up_full = up_rows.astype(jnp.float32)
    sigmoid = jax.nn.sigmoid(gate_full)
    active = gate_full * sigmoid
    product = (active * up_full).astype(jnp.bfloat16)
    gate_grad = (upstream * up_full * sigmoid * (1.0 + gate_full * (1.0 - sigmoid))).astype(
        jnp.bfloat16
    )
    up_grad = (upstream * active).astype(jnp.bfloat16)
    return (product, gate_grad, up_grad)


def per_device(cotangent, expert_ids, route_weights, gate_pre, up_pre, down_weight):
    devices = lax.axis_size("expert")
    experts = devices // SPLIT
    capacity = gate_pre.shape[0] // devices
    width = cotangent.shape[1]
    buffer = slot_buffer(cotangent, expert_ids, route_weights, experts, capacity)
    copies = jnp.broadcast_to(
        buffer.reshape(experts, 1, capacity, width), (experts, SPLIT, capacity, width)
    )
    arrived = lax.all_to_all(
        copies.reshape(devices, capacity, width), "expert", split_axis=0, concat_axis=0, tiled=True
    )
    routed = arrived.reshape(devices * capacity, width)
    columns = routed
    upstream = jnp.dot(
        columns, gathered_copies(down_weight, "dp", 0), preferred_element_type=jnp.float32
    )
    product, gate_grad, up_grad = activations(gate_pre, up_pre, upstream)
    columns = routed
    weight_grad = sum_at_owner(
        lax.dot_general(
            columns, product, (((0,), (0,)), ((), ())), preferred_element_type=jnp.float32
        ).astype(jnp.bfloat16),
        "dp",
        0,
    ).astype(jnp.bfloat16)
    return (weight_grad, gate_grad, up_grad)


def solution(mesh):
    placed = (
        P(("dp", "expert"), None),
        P(("dp", "expert"), None),
        P(("dp", "expert"), None),
        P("dp", "expert"),
        P("dp", "expert"),
        P("dp", "expert"),
    )
    return jax.shard_map(
        per_device,
        mesh=mesh,
        in_specs=placed,
        out_specs=(P("dp", "expert"), P("dp", "expert"), P("dp", "expert")),
        check_vma=False,
    )
```

profile of v0, /device:TPU:40, one launch (start us, length us, event | category | flops | bytes accessed | tf_op | source)
XLA Modules:
  0.0 289.3 jit_solution(12877706505439761167)
XLA Ops:
  0.6 0.0 copy-start
  0.6 3.4 %fusion.16 = s32[128]{0:T(128)S(1)} fusion(s32[128]{0:T(128)} %bitcast.19), kind=kOutput, calls=%fused_computation.30 | output fusion | flops 274304 | bytes 1024 | tf_op jit(solution)/shard_map/jit(cumsum)/reduce_window_sum | solution.py:40
  4.0 0.7 fusion.14
  4.7 0.8 select_reduce_fusion
  5.5 0.0 copy-done
  5.5 1.7 fusion
  7.2 2.3 broadcast_in_dim.6
  9.4 1.0 broadcast_in_dim.7
  10.4 0.0 copy-start.2
  10.4 219.5 %all_to_all.15 = bf16[64,12,3584]{2,1,0:T(8,128)(2,1)} all-to-all(bf16[64,12,3584]{2,1,0:T(8,128)(2,1)S(1)} %bitcast.15), channel_id=1, replica_groups=mesh['dp'=8,'expert'=64] {'expert'}, dimensions={0} | all-to-all | bytes 11010048 | tf_op jit(solution)/shard_map/all_to_all | solution.py:78
  229.9 0.0 copy-done.2
  229.9 1.4 broadcast_in_dim.8
  231.3 3.6 %all-to-all-start.2 = ((bf16[8,448,256]{2,1,0:T(8,128)(2,1)}), bf16[8,448,256]{2,1,0:T(8,128)(2,1)S(1)}, u32[]{:S(2)}, u32[]{:S(2)}) async-start(bf16[8,448,256]{2,1,0:T(8,128)(2,1)} %broadcast_in_dim.8), calls=%async_computation.2 | async-start | bytes 3670016 | tf_op jit(solution)/shard_map/all_to_all | solution.py:11
  234.9 0.0 copy-start.3
  234.9 0.0 copy-start.4
  234.9 9.4 %reshape.194 = bf16[768,3584]{1,0:T(8,128)(2,1)} reshape(bf16[64,12,3584]{2,1,0:T(8,128)(2,1)} %all_to_all.15) | data formatting | bytes 11010048 | tf_op jit(solution)/shard_map/reshape | solution.py:81
  244.4 0.0 copy-done.3
  244.4 0.0 copy-done.4
  244.4 5.6 %convolution_convert_fusion = bf16[3584,256]{1,0:T(8,128)(2,1)} fusion(bf16[768,3584]{1,0:T(8,128)(2,1)} %reshape.194, bf16[768,256]{1,0:T(8,128)(2,1)S(1)} %copy-done.3, bf16[768,256]{1,0:T(8,128)(2,1)S(1)} %copy-done.4), kind=kOutput, calls=%fused_computation.1 | convolution fusion | flops 1411776512 | bytes 8126464 | tf_op jit(solution)/shard_map/dot_general | solution.py:89
  249.9 9.2 %all-to-all-done.2 = bf16[8,448,256]{2,1,0:T(8,128)(2,1)S(1)} async-done(((bf16[8,448,256]{2,1,0:T(8,128)(2,1)}), bf16[8,448,256]{2,1,0:T(8,128)(2,1)S(1)}, u32[]{:S(2)}, u32[]{:S(2)}) %all-to-all-start.2) | async-done | bytes 1835040 | tf_op jit(solution)/shard_map/all_to_all | solution.py:11
  259.2 0.0 copy-start.1
  259.2 1.2 copy-done.1
  260.4 3.6 %all-to-all-start.1 = ((bf16[8,448,256]{2,1,0:T(8,128)(2,1)}), bf16[8,448,256]{2,1,0:T(8,128)(2,1)S(1)}, u32[]{:S(2)}, u32[]{:S(2)}) async-start(bf16[8,448,256]{2,1,0:T(8,128)(2,1)} %bitcast.17), calls=%async_computation.1 | async-start | bytes 3670016 | tf_op jit(solution)/shard_map/all_to_all | solution.py:32
  264.0 5.7 %multiply_convert_fusion = (bf16[768,256]{1,0:T(8,128)(2,1)}, bf16[768,256]{1,0:T(8,128)(2,1)}) fusion(bf16[768,256]{1,0:T(8,128)(2,1)S(1)} %copy-done.4, bf16[768,256]{1,0:T(8,128)(2,1)S(1)} %copy-done.3, bf16[768,3584]{1,0:T(8,128)(2,1)} %reshape.194, bf16[3584,256]{1,0:T(8,128)(2,1)} %bitcast.16), kind=kOutput, calls=%fused_computation.16 | convolution fusion | flops 1412235264 | bytes 8912896 | tf_op jit(solution)/shard_map/dot_general | solution.py:83
  269.8 18.5 %all-to-all-done.1 = bf16[8,448,256]{2,1,0:T(8,128)(2,1)S(1)} async-done(((bf16[8,448,256]{2,1,0:T(8,128)(2,1)}), bf16[8,448,256]{2,1,0:T(8,128)(2,1)S(1)}, u32[]{:S(2)}, u32[]{:S(2)}) %all-to-all-start.1) | async-done | bytes 1835040 | tf_op jit(solution)/shard_map/all_to_all | solution.py:32
  288.3 1.0 reduce_sum.43
Async XLA Ops:
  0.6 4.8 %copy-start = (bf16[128,3584]{1,0:T(8,128)(2,1)S(1)}, bf16[128,3584]{1,0:T(8,128)(2,1)}, u32[]{:S(2)}) copy-start(bf16[128,3584]{1,0:T(8,128)(2,1)} %param.6) | copy-start | bytes 2752516
  10.4 219.5 %copy-start.2 = (bf16[448,256]{1,0:T(8,128)(2,1)S(1)}, bf16[448,256]{1,0:T(8,128)(2,1)}, u32[]{:S(2)}) copy-start(bf16[448,256]{1,0:T(8,128)(2,1)} %param.11) | copy-start | bytes 688132
  231.3 27.9 %all-to-all-start.2 = ((bf16[8,448,256]{2,1,0:T(8,128)(2,1)}), bf16[8,448,256]{2,1,0:T(8,128)(2,1)S(1)}, u32[]{:S(2)}, u32[]{:S(2)}) async-start(bf16[8,448,256]{2,1,0:T(8,128)(2,1)} %broadcast_in_dim.8), calls=%async_computation.2 | async-start | bytes 3670016 | tf_op jit(solution)/shard_map/all_to_all | solution.py:11
  234.9 9.5 %copy-start.3 = (bf16[768,256]{1,0:T(8,128)(2,1)S(1)}, bf16[768,256]{1,0:T(8,128)(2,1)}, u32[]{:S(2)}) copy-start(bf16[768,256]{1,0:T(8,128)(2,1)} %param.10) | copy-start | bytes 1179652
  234.9 9.4 %copy-start.4 = (bf16[768,256]{1,0:T(8,128)(2,1)S(1)}, bf16[768,256]{1,0:T(8,128)(2,1)}, u32[]{:S(2)}) copy-start(bf16[768,256]{1,0:T(8,128)(2,1)} %param.9) | copy-start | bytes 1179652
  259.2 1.2 copy-start.1
  260.4 27.9 %all-to-all-start.1 = ((bf16[8,448,256]{2,1,0:T(8,128)(2,1)}), bf16[8,448,256]{2,1,0:T(8,128)(2,1)S(1)}, u32[]{:S(2)}, u32[]{:S(2)}) async-start(bf16[8,448,256]{2,1,0:T(8,128)(2,1)} %bitcast.17), calls=%async_computation.1 | async-start | bytes 3670016 | tf_op jit(solution)/shard_map/all_to_all | solution.py:32
where the time goes:
time: 290 us; the launch traced here: 289 us
  blocking collectives  220 us (76%)
  waiting for transfers between devices  27.8 us (10%)
  local copies, waits for them, and re-layouts  15.3 us (5%)
  matrix products  13 us (4%)
  starting transfers between devices  7.18 us (2%)
  other arithmetic  5.79 us (2%)
    all_to_all x1, blocking collectives, per_device(): lax.all_to_all(copies.reshape(devices, capacity, width), 'expert', split_...  220 us
    all_to_all x1, waiting for transfers between devices, sum_at_owner(): lax.all_to_all(parts, axis, split_axis=0, concat_axis=0, tiled=True)  18.5 us
    reshape x1, local copies, waits for them, and re-layouts, per_device(): routed = arrived.reshape(devices * capacity, width)  9.43 us
    all_to_all x1, waiting for transfers between devices, sent_to_all(): return lax.all_to_all(copies, axis, split_axis=0, concat_axis=0, tiled=True)  9.25 us
  transfers between devices with their start and end apart: 2, of which 2 were waited for; matrix products, arithmetic and copies ran while one was open for 7% of the time, Pallas kernels for 0%

commit v1 on v0

v1 whole, which is shorter than its diff:
```python
import jax
import jax.numpy as jnp
from jax import lax
from jax.experimental import pallas as pl
from jax.experimental.pallas import tpu as pltpu
from jax.sharding import PartitionSpec as P

CAP = 12
PART = 24
BF = jnp.bfloat16
F32 = jnp.float32
VMEM_LIMIT = 56 * 1024 * 1024


def expert_xor(value, mask):
    return lax.ppermute(value, "expert", [(i, i ^ mask) for i in range(lax.axis_size("expert"))])


def dp_xor(value, mask):
    return lax.ppermute(value, "dp", [(i, i ^ mask) for i in range(lax.axis_size("dp"))])


def swapped(value, flip):
    experts = lax.axis_size("expert")
    pairs = []
    for d in range(lax.axis_size("dp")):
        for s in range(experts):
            to_dp = (s & 1) * 4 + (d & 3)
            to_expert = (s & ~3) + (((s >> 1) & 1) ^ flip) * 2 + (d >> 2)
            pairs.append((d * experts + s, to_dp * experts + to_expert))
    return lax.ppermute(value, ("dp", "expert"), pairs)


def whole(shape):
    return pl.BlockSpec(memory_space=pltpu.VMEM)


SCALARS = pl.BlockSpec(memory_space=pltpu.SMEM)


def slots_body(ids_ref, weights_ref, cot_ref, out_ref):
    tokens = ids_ref.shape[1]
    experts = out_ref.shape[0]
    half = out_ref.shape[3]
    ids = jnp.broadcast_to(ids_ref[...].astype(F32), (tokens, tokens))
    row = lax.broadcasted_iota(jnp.int32, (tokens, tokens), 0)
    col = lax.broadcasted_iota(jnp.int32, (tokens, tokens), 1)
    ids_down = jnp.sum(jnp.where(row == col, ids, 0.0), axis=1, keepdims=True)
    earlier = jnp.where((ids_down == ids) & (row < col), 1.0, 0.0)
    position = jnp.sum(earlier, axis=0, keepdims=True)
    target = (ids_ref[...].astype(F32) * PART + position).astype(jnp.int32)
    place = lax.broadcasted_iota(jnp.int32, (experts * PART, tokens), 0)
    first = place == target
    second = place == target + CAP
    scale = jnp.sum(jnp.where(first | second, weights_ref[...], 0.0), axis=1, keepdims=True)
    picked = jnp.dot(
        first.astype(F32).astype(BF), cot_ref[:, :half], preferred_element_type=F32
    ) + jnp.dot(second.astype(F32).astype(BF), cot_ref[:, half:], preferred_element_type=F32)
    rows = picked * scale
    for x in range(experts):
        out_ref[x, 0] = rows[x * PART : (x + 1) * PART].astype(BF)


def slot_buffer(cotangent, expert_ids, route_weights, experts):
    tokens, width = cotangent.shape
    return pl.pallas_call(
        slots_body,
        grid=(2,),
        in_specs=[
            pl.BlockSpec((1, tokens), lambda k: (0, 0)),
            pl.BlockSpec((1, tokens), lambda k: (0, 0)),
            pl.BlockSpec((tokens, width // 2), lambda k: (0, k)),
        ],
        out_specs=pl.BlockSpec((experts, 1, PART, width // 4), lambda k: (0, k, 0, 0)),
        out_shape=jax.ShapeDtypeStruct((experts, 2, PART, width // 4), BF),
        compiler_params=pltpu.CompilerParams(vmem_limit_bytes=VMEM_LIMIT),
        name="slots",
    )(expert_ids.reshape(1, tokens), route_weights.reshape(1, tokens), cotangent)


def weight_body(s_ref, recv_ref, p0, p1, p2, p3, rows_ref, grad_ref):
    a1, a0, core, k = s_ref[0], s_ref[1], s_ref[2], s_ref[3]
    sources = recv_ref.shape[0]
    for b in range(2):
        for s in range(sources):
            rows_ref[b, s * CAP : (s + 1) * CAP, :] = recv_ref[s, b * CAP : (b + 1) * CAP, :]
    block = grad_ref.shape[4]
    for b in range(2):
        for q, piece in enumerate((p0, p1, p2, p3)):
            e, d = q >> 1, q & 1
            grad = lax.dot_general(
                rows_ref[b], piece[...], (((0,), (0,)), ((), ())), preferred_element_type=F32
            ).astype(BF)
            for c in range(2):
                grad_ref[c ^ core, d ^ k ^ a1, b ^ a0, e] = grad[c * block : (c + 1) * block]


def weight_partial(scalars, recv, pieces, block):
    sources, _, half = recv.shape
    count = sources * CAP
    columns = pieces[0].shape[1]
    return pl.pallas_call(
        weight_body,
        in_specs=[SCALARS, whole(recv.shape)] + [whole((count, columns))] * 4,
        out_specs=[whole((2, count, half)), whole((2, 2, 2, 2, block, columns))],
        out_shape=[
            jax.ShapeDtypeStruct((2, count, half), BF),
            jax.ShapeDtypeStruct((2, 2, 2, 2, block, columns), BF),
        ],
        compiler_params=pltpu.CompilerParams(vmem_limit_bytes=VMEM_LIMIT),
        name="weight_partial",
    )(scalars, recv, *pieces)


def upstream_body(s_ref, rows_ref, near_ref, far_ref, c0, c1, c2, c3):
    a1, a0, core, k = s_ref[0], s_ref[1], s_ref[2], s_ref[3]
    for q, out in enumerate((c0, c1, c2, c3)):
        e, d = q >> 1, q & 1
        total = None
        for b in range(2):
            near = near_ref[d ^ k ^ a1, b ^ a0, e]
            far = far_ref[d ^ k ^ a1, b ^ a0, e]
            low = jnp.where(core == 0, near, far)
            high = jnp.where(core == 0, far, near)
            part = jnp.dot(
                rows_ref[b], jnp.concatenate([low, high], axis=0), preferred_element_type=F32
            )
            total = part if total is None else total + part
        out[...] = total.astype(out.dtype)


def upstream_partial(scalars, rows, near, far):
    count = rows.shape[1]
    columns = near.shape[-1]
    return pl.pallas_call(
        upstream_body,
        in_specs=[SCALARS, whole(rows.shape), whole(near.shape), whole(far.shape)],
        out_specs=[whole((count, columns))] * 4,
        out_shape=[jax.ShapeDtypeStruct((count, columns), F32)]
        + [jax.ShapeDtypeStruct((count, columns), BF)] * 3,
        compiler_params=pltpu.CompilerParams(vmem_limit_bytes=VMEM_LIMIT),
        name="upstream_partial",
    )(scalars, rows, near, far)


def finish_body(s_ref, gate_ref, up_ref, c0, r1, r2, r3, gate_out, up_out):
    group = s_ref[4]
    for side in range(2):
        for t in range(2):
            if side == 0:
                part = c0[:, t] + r1[:, t].astype(F32)
            else:
                part = r2[:, t].astype(F32) + r3[:, t].astype(F32)
            inner = (group ^ side) == 0
            index = jnp.where(inner, 3 * t, 1 + t)
            gate = gate_ref[:, index].astype(F32)
            up = up_ref[:, index].astype(F32)
            sigmoid = jax.nn.sigmoid(gate)
            gate_out[:, index] = (part * up * sigmoid * (1.0 + gate * (1.0 - sigmoid))).astype(BF)
            up_out[:, index] = (part * (gate * sigmoid)).astype(BF)


def finish(scalars, gate, up, c0, r1, r2, r3):
    full = whole(gate.shape)
    part = whole(c0.shape)
    return pl.pallas_call(
        finish_body,
        in_specs=[SCALARS, full, full, part, part, part, part],
        out_specs=[full, full],
        out_shape=[jax.ShapeDtypeStruct(gate.shape, BF)] * 2,
        compiler_params=pltpu.CompilerParams(vmem_limit_bytes=VMEM_LIMIT),
        name="finish",
    )(scalars, gate, up, c0, r1, r2, r3)


def per_device(cotangent, expert_ids, route_weights, gate_pre, up_pre, down_weight):
    devices = lax.axis_size("expert")
    experts = devices // 4
    ys = devices // 8
    columns = gate_pre.shape[1]
    block = down_weight.shape[0]
    dp = lax.axis_index("dp")
    place = lax.axis_index("expert")
    a1, a0, core = dp >> 2, (dp >> 1) & 1, dp & 1
    half, line, k = (place >> 2) & 1, (place >> 1) & 1, place & 1
    group = half ^ line
    scalars = jnp.stack([a1, a0, core, k, group]).astype(jnp.int32)

    own = jnp.stack([swapped(down_weight, 0), swapped(down_weight, 1)])
    own, cotangent = lax.optimization_barrier((own, cotangent))

    slots = slot_buffer(cotangent, expert_ids, route_weights, experts)
    lists = [
        [y * 8 + z for y in range(ys) for z in zs] for zs in ((0, 1, 6, 7), (2, 3, 4, 5))
    ]
    recv = lax.all_to_all(
        slots.reshape(devices // 2, PART, slots.shape[3]),
        "expert",
        split_axis=0,
        concat_axis=0,
        tiled=True,
        axis_index_groups=lists,
    )

    gate4 = gate_pre.reshape(ys, 4, PART, columns)
    up4 = up_pre.reshape(ys, 4, PART, columns)
    gate_full = gate4.astype(F32)
    product = (gate_full * jax.nn.sigmoid(gate_full) * up4.astype(F32)).astype(BF)
    outer = jnp.concatenate([product[:, 0:1], product[:, 3:4]], axis=1)
    inner = product[:, 1:3]
    mine = jnp.where(group == 0, outer, inner).reshape(-1, columns)
    theirs = jnp.where(group == 0, inner, outer).reshape(-1, columns)
    pieces = [mine, expert_xor(mine, 1), expert_xor(theirs, 2), expert_xor(theirs, 3)]

    near = jnp.stack([own, dp_xor(own, 2), dp_xor(own, 4), dp_xor(own, 6)])
    far = dp_xor(near, 1)
    near = near.reshape(2, 2, 2, block, columns)
    far = far.reshape(2, 2, 2, block, columns)

    recv, near, far = lax.optimization_barrier((recv, near, far))
    rows, grad = weight_partial(scalars, recv, pieces, block)
    crossed = dp_xor(grad[1], 1)
    c0, c1, c2, c3 = upstream_partial(scalars, rows, near, far)
    summed = (grad[0].astype(F32) + crossed.astype(F32)).astype(BF)
    kept = summed[0, 0].astype(F32)
    for mask, piece in ((2, summed[0, 1]), (4, summed[1, 0]), (6, summed[1, 1])):
        kept = kept + dp_xor(piece, mask).astype(F32)
    kept = kept.astype(BF)
    weight_grad = (
        swapped(kept[0], 0).astype(F32) + swapped(kept[1], 1).astype(F32)
    ).astype(BF)

    shape = (ys, 2, PART, columns)
    r1, r2, r3 = (expert_xor(c, q) for q, c in ((1, c1), (2, c2), (3, c3)))
    gate_grad, up_grad = finish(
        scalars,
        gate4,
        up4,
        c0.reshape(shape),
        r1.reshape(shape),
        r2.reshape(shape),
        r3.reshape(shape),
    )
    return (weight_grad, gate_grad.reshape(gate_pre.shape), up_grad.reshape(up_pre.shape))


def solution(mesh):
    placed = (
        P(("dp", "expert"), None),
        P(("dp", "expert"), None),
        P(("dp", "expert"), None),
        P("dp", "expert"),
        P("dp", "expert"),
        P("dp", "expert"),
    )
    return jax.shard_map(
        per_device,
        mesh=mesh,
        in_specs=placed,
        out_specs=(P("dp", "expert"), P("dp", "expert"), P("dp", "expert")),
        check_vma=False,
    )
```

time: 290 us -> 182 us (0.63)
  the two profiles are of different devices: /device:TPU:40 before, /device:TPU:64 now
where the time goes in v1:
time: 182 us; the launch traced here: 181 us
  starting transfers between devices  80.5 us (44%)
  waiting for transfers between devices  74.6 us (41%)
  Pallas kernels  16.9 us (9%)
  other arithmetic  4.87 us (3%)
  local copies, waits for them, and re-layouts  3.27 us (2%)
    ppermute x8, waiting for transfers between devices, dp_xor(): lax.ppermute(value, 'dp', [(i, i ^ mask) for i in range(lax.axis_size('dp...  39.1 us
    ppermute x6, waiting for transfers between devices, expert_xor(): lax.ppermute(value, 'expert', [(i, i ^ mask) for i in range(lax.axis_size...  25 us
    ppermute x8, starting transfers between devices, dp_xor(): lax.ppermute(value, 'dp', [(i, i ^ mask) for i in range(lax.axis_size('dp...  23.5 us
    ppermute x4, starting transfers between devices, swapped(): return lax.ppermute(value, ('dp', 'expert'), pairs)  22 us
    ppermute x6, starting transfers between devices, expert_xor(): lax.ppermute(value, 'expert', [(i, i ^ mask) for i in range(lax.axis_size...  19.3 us
    all_to_all x1, starting transfers between devices, per_device(): lax.all_to_all(slots.reshape(devices // 2, PART, slots.shape[3]), 'expert...  15.6 us
    ppermute x4, waiting for transfers between devices, swapped(): return lax.ppermute(value, ('dp', 'expert'), pairs)  10.5 us
    pallas_call x1, Pallas kernels, weight_partial(): pl.pallas_call(weight_body, in_specs=[SCALARS, whole(recv.shape)] + [whol...  5.76 us
  transfers between devices with their start and end apart: 19, of which 12 were waited for; matrix products, arithmetic and copies ran while one was open for 2% of the time, Pallas kernels for 4%

profile of v1, /device:TPU:64, one launch (start us, length us, event | category | flops | bytes accessed | tf_op | source)
XLA Modules:
  0.0 181.0 jit_solution(8808152421652215558)
XLA Ops:
  0.6 6.7 %collective-permute-start.1 = (bf16[448,256]{1,0:T(8,128)(2,1)}, bf16[448,256]{1,0:T(8,128)(2,1)S(1)}, u32[]{:S(2)}, u32[]{:S(2)}) collective-permute-start(bf16[448,256]{1,0:T(8,128)(2,1)} %param.11), channel_id=1, source_target_pairs={{0,2},{1,258},{2,0},{3,256},{4,6},{5,262},{6,4},{7,260},{8,10},{9,... | collective-permute-start | bytes 688136 | tf_op jit(solution)/shard_map/ppermute | solution.py:31
  7.4 5.1 %collective-permute-start = (bf16[448,256]{1,0:T(8,128)(2,1)}, bf16[448,256]{1,0:T(8,128)(2,1)S(1)}, u32[]{:S(2)}, u32[]{:S(2)}) collective-permute-start(bf16[448,256]{1,0:T(8,128)(2,1)} %param.11), channel_id=1, source_target_pairs={{0,0},{1,256},{2,2},{3,258},{4,4},{5,260},{6,6},{7,262},{8,8},{9,2... | collective-permute-start | bytes 688136 | tf_op jit(solution)/shard_map/ppermute | solution.py:31
  12.5 8.0 %collective-permute-done.1 = bf16[448,256]{1,0:T(8,128)(2,1)S(1)} collective-permute-done((bf16[448,256]{1,0:T(8,128)(2,1)}, bf16[448,256]{1,0:T(8,128)(2,1)S(1)}, u32[]{:S(2)}, u32[]{:S(2)}) %collective-permute-start.1) | collective-permute-done | bytes 229408 | tf_op jit(solution)/shard_map/ppermute | solution.py:31
  20.5 2.5 %collective-permute-done = bf16[448,256]{1,0:T(8,128)(2,1)S(1)} collective-permute-done((bf16[448,256]{1,0:T(8,128)(2,1)}, bf16[448,256]{1,0:T(8,128)(2,1)S(1)}, u32[]{:S(2)}, u32[]{:S(2)}) %collective-permute-start) | collective-permute-done | bytes 229408 | tf_op jit(solution)/shard_map/ppermute | solution.py:31
  23.1 3.3 %slots.1 = bf16[16,2,24,896]{3,2,1,0:T(8,128)(2,1)} custom-call(s32[1,128]{1,0:T(1,128)} %bitcast.64, f32[1,128]{1,0:T(1,128)} %bitcast.65, bf16[128,3584]{1,0:T(8,128)(2,1)} %cot_ref), custom_call_target="tpu_custom_call" | custom-call | tf_op jit(solution)/shard_map/slots/pallas_call | solution.py:66
  26.4 15.6 %all-to-all-start = ((bf16[32,24,896]{2,1,0:T(8,128)(2,1)}), bf16[32,24,896]{2,1,0:T(8,128)(2,1)S(1)}, u32[]{:S(2)}, u32[]{:S(2)}) async-start(bf16[32,24,896]{2,1,0:T(8,128)(2,1)} %bitcast.47), calls=%async_computation | async-start | bytes 2752512 | tf_op jit(solution)/shard_map/all_to_all | solution.py:196
  42.1 2.8 %collective-permute-start.4 = (bf16[2,448,256]{2,1,0:T(8,128)(2,1)S(1)}, bf16[2,448,256]{2,1,0:T(8,128)(2,1)S(1)}, u32[]{:S(2)}, u32[]{:S(2)}) collective-permute-start(bf16[2,448,256]{2,1,0:T(8,128)(2,1)S(1)} %pad_maximum_fusion.1), channel_id=1, source_target_pairs={{0,384},{64,448},{128,256},{192,320},{256,128},{320,192},{384,0},{... | collective-permute-start | bytes 1376264 | tf_op jit(solution)/shard_map/ppermute | solution.py:20
  44.9 3.7 %collective-permute-start.3 = (bf16[2,448,256]{2,1,0:T(8,128)(2,1)S(1)}, bf16[2,448,256]{2,1,0:T(8,128)(2,1)S(1)}, u32[]{:S(2)}, u32[]{:S(2)}) collective-permute-start(bf16[2,448,256]{2,1,0:T(8,128)(2,1)S(1)} %pad_maximum_fusion.1), channel_id=1, source_target_pairs={{0,256},{64,320},{128,384},{192,448},{256,0},{320,64},{384,128},{4... | collective-permute-start | bytes 1376264 | tf_op jit(solution)/shard_map/ppermute | solution.py:20
  48.6 3.3 %collective-permute-start.2 = (bf16[2,448,256]{2,1,0:T(8,128)(2,1)S(1)}, bf16[2,448,256]{2,1,0:T(8,128)(2,1)S(1)}, u32[]{:S(2)}, u32[]{:S(2)}) collective-permute-start(bf16[2,448,256]{2,1,0:T(8,128)(2,1)S(1)} %pad_maximum_fusion.1), channel_id=1, source_target_pairs={{0,128},{64,192},{128,0},{192,64},{256,384},{320,448},{384,256},{4... | collective-permute-start | bytes 1376264 | tf_op jit(solution)/shard_map/ppermute | solution.py:20
  51.9 15.0 %collective-permute-done.4 = bf16[2,448,256]{2,1,0:T(8,128)(2,1)S(1)} collective-permute-done((bf16[2,448,256]{2,1,0:T(8,128)(2,1)S(1)}, bf16[2,448,256]{2,1,0:T(8,128)(2,1)S(1)}, u32[]{:S(2)}, u32[]{:S(2)}) %collective-permute-start.4) | collective-permute-done | bytes 458784 | tf_op jit(solution)/shard_map/ppermute | solution.py:20
  66.9 2.5 %collective-permute-done.2 = bf16[2,448,256]{2,1,0:T(8,128)(2,1)S(1)} collective-permute-done((bf16[2,448,256]{2,1,0:T(8,128)(2,1)S(1)}, bf16[2,448,256]{2,1,0:T(8,128)(2,1)S(1)}, u32[]{:S(2)}, u32[]{:S(2)}) %collective-permute-start.2) | collective-permute-done | bytes 458784 | tf_op jit(solution)/shard_map/ppermute | solution.py:20
  70.7 1.9 %collective-permute-start.5 = (bf16[4,2,448,256]{3,2,1,0:T(8,128)(2,1)S(1)}, bf16[4,2,448,256]{3,2,1,0:T(8,128)(2,1)}, u32[]{:S(2)}, u32[]{:S(2)}) collective-permute-start(bf16[4,2,448,256]{3,2,1,0:T(8,128)(2,1)S(1)} %pad_maximum_fusion), channel_id=1, source_target_pairs={{0,64},{64,0},{128,192},{192,128},{256,320},{320,256},{384,448},{4... | collective-permute-start | bytes 5505032 | tf_op jit(solution)/shard_map/ppermute | solution.py:20
  74.7 2.4 %collective-permute-start.6 = (bf16[384,256]{1,0:T(8,128)(2,1)S(1)}, bf16[384,256]{1,0:T(8,128)(2,1)}, u32[]{:S(2)}, u32[]{:S(2)}) collective-permute-start(bf16[384,256]{1,0:T(8,128)(2,1)S(1)} %bitcast.53), channel_id=1, source_target_pairs={{0,1},{1,0},{2,3},{3,2},{4,5},{5,4},{6,7},{7,6},{8,9},{9,8},{10,11... | collective-permute-start | bytes 589832 | tf_op jit(solution)/shard_map/ppermute | solution.py:16
  77.1 1.9 %collective-permute-start.8 = (bf16[384,256]{1,0:T(8,128)(2,1)}, bf16[384,256]{1,0:T(8,128)(2,1)}, u32[]{:S(2)}, u32[]{:S(2)}) collective-permute-start(bf16[384,256]{1,0:T(8,128)(2,1)} %bitcast.19), channel_id=1, source_target_pairs={{0,3},{1,2},{2,1},{3,0},{4,7},{5,6},{6,5},{7,4},{8,11},{9,10},{10,... | collective-permute-start | bytes 589832 | tf_op jit(solution)/shard_map/ppermute | solution.py:16
  79.1 5.8 %collective-permute-start.7 = (bf16[384,256]{1,0:T(8,128)(2,1)}, bf16[384,256]{1,0:T(8,128)(2,1)}, u32[]{:S(2)}, u32[]{:S(2)}) collective-permute-start(bf16[384,256]{1,0:T(8,128)(2,1)} %bitcast.19), channel_id=1, source_target_pairs={{0,2},{1,3},{2,0},{3,1},{4,6},{5,7},{6,4},{7,5},{8,10},{9,11},{10,... | collective-permute-start | bytes 589832 | tf_op jit(solution)/shard_map/ppermute | solution.py:16
  85.5 10.0 %collective-permute-done.8.p3 = bf16[384,256]{1,0:T(8,128)(2,1)} collective-permute-done((bf16[384,256]{1,0:T(8,128)(2,1)}, bf16[384,256]{1,0:T(8,128)(2,1)}, u32[]{:S(2)}, u32[]{:S(2)}) %collective-permute-start.8) | collective-permute-done | bytes 196640 | tf_op jit(solution)/shard_map/ppermute | solution.py:16
  96.8 5.8 %weight_partial.1 = (bf16[2,384,896]{2,1,0:T(8,128)(2,1)}, bf16[2,2,2,2,448,256]{5,4,3,2,1,0:T(8,128)(2,1)}) custom-call(s32[5]{0:T(128)} %stack.47.s_ref, bf16[32,24,896]{2,1,0:T(8,128)(2,1)} %copy-done.1, bf16[384,256]{1,0:T(8,128)(2,1)} %bitcast.54, bf16[384,256]{1,0:T(8,128)(2,1)} %collective-permute-done.6.p1, ...), custom_call_target="tpu_custom_call" | custom-call | tf_op jit(solution)/shard_map/weight_partial/pallas_call | solution.py:102
  104.4 1.9 %collective-permute-start.9 = (bf16[2,2,2,448,256]{4,3,2,1,0:T(8,128)(2,1)S(1)}, bf16[2,2,2,448,256]{4,3,2,1,0:T(8,128)(2,1)S(1)}, u32[]{:S(2)}, u32[]{:S(2)}) collective-permute-start(bf16[2,2,2,448,256]{4,3,2,1,0:T(8,128)(2,1)S(1)} %slice_bitcast_fusion), channel_id=1, source_target_pairs={{0,64},{64,0},{128,192},{192,128},{256,320},{320,256},{384,448},{4... | collective-permute-start | bytes 5505032 | tf_op jit(solution)/shard_map/ppermute | solution.py:20
  106.3 3.8 %collective-permute-done.9 = bf16[2,2,2,448,256]{4,3,2,1,0:T(8,128)(2,1)S(1)} collective-permute-done((bf16[2,2,2,448,256]{4,3,2,1,0:T(8,128)(2,1)S(1)}, bf16[2,2,2,448,256]{4,3,2,1,0:T(8,128)(2,1)S(1)}, u32[]{:S(2)}, u32[]{:S(2)}) %collective-permute-start.9) | collective-permute-done | bytes 1835040 | tf_op jit(solution)/shard_map/ppermute | solution.py:20
  110.7 2.5 %collective-permute-start.10 = (bf16[2,448,256]{2,1,0:T(8,128)(2,1)S(1)}, bf16[2,448,256]{2,1,0:T(8,128)(2,1)S(1)}, u32[]{:S(2)}, u32[]{:S(2)}) collective-permute-start(bf16[2,448,256]{2,1,0:T(8,128)(2,1)S(1)} %get-tuple-element.29), channel_id=1, source_target_pairs={{0,128},{64,192},{128,0},{192,64},{256,384},{320,448},{384,256},{4... | collective-permute-start | bytes 1376264 | tf_op jit(solution)/shard_map/ppermute | solution.py:20
  113.2 2.8 %collective-permute-start.12 = (bf16[2,448,256]{2,1,0:T(8,128)(2,1)S(1)}, bf16[2,448,256]{2,1,0:T(8,128)(2,1)S(1)}, u32[]{:S(2)}, u32[]{:S(2)}) collective-permute-start(bf16[2,448,256]{2,1,0:T(8,128)(2,1)S(1)} %get-tuple-element.30), channel_id=1, source_target_pairs={{0,384},{64,448},{128,256},{192,320},{256,128},{320,192},{384,0},{... | collective-permute-start | bytes 1376264 | tf_op jit(solution)/shard_map/ppermute | solution.py:20
  116.0 4.5 %collective-permute-start.11 = (bf16[2,448,256]{2,1,0:T(8,128)(2,1)S(1)}, bf16[2,448,256]{2,1,0:T(8,128)(2,1)S(1)}, u32[]{:S(2)}, u32[]{:S(2)}) collective-permute-start(bf16[2,448,256]{2,1,0:T(8,128)(2,1)S(1)} %get-tuple-element.31), channel_id=1, source_target_pairs={{0,256},{64,320},{128,384},{192,448},{256,0},{320,64},{384,128},{4... | collective-permute-start | bytes 1376264 | tf_op jit(solution)/shard_map/ppermute | solution.py:20
  120.5 5.4 %collective-permute-done.10 = bf16[2,448,256]{2,1,0:T(8,128)(2,1)S(1)} collective-permute-done((bf16[2,448,256]{2,1,0:T(8,128)(2,1)S(1)}, bf16[2,448,256]{2,1,0:T(8,128)(2,1)S(1)}, u32[]{:S(2)}, u32[]{:S(2)}) %collective-permute-start.10) | collective-permute-done | bytes 458784 | tf_op jit(solution)/shard_map/ppermute | solution.py:20
  125.9 12.4 %collective-permute-done.12 = bf16[2,448,256]{2,1,0:T(8,128)(2,1)S(1)} collective-permute-done((bf16[2,448,256]{2,1,0:T(8,128)(2,1)S(1)}, bf16[2,448,256]{2,1,0:T(8,128)(2,1)S(1)}, u32[]{:S(2)}, u32[]{:S(2)}) %collective-permute-start.12) | collective-permute-done | bytes 458784 | tf_op jit(solution)/shard_map/ppermute | solution.py:20
  138.7 5.5 %collective-permute-start.13 = (bf16[448,256]{1,0:T(8,128)(2,1)S(1)}, bf16[448,256]{1,0:T(8,128)(2,1)S(1)}, u32[]{:S(2)}, u32[]{:S(2)}) collective-permute-start(bf16[448,256]{1,0:T(8,128)(2,1)S(1)} %get-tuple-element.34), channel_id=1, source_target_pairs={{0,0},{1,256},{2,2},{3,258},{4,4},{5,260},{6,6},{7,262},{8,8},{9,2... | collective-permute-start | bytes 688136 | tf_op jit(solution)/shard_map/ppermute | solution.py:31
  144.2 4.6 %collective-permute-start.14 = (bf16[448,256]{1,0:T(8,128)(2,1)S(1)}, bf16[448,256]{1,0:T(8,128)(2,1)S(1)}, u32[]{:S(2)}, u32[]{:S(2)}) collective-permute-start(bf16[448,256]{1,0:T(8,128)(2,1)S(1)} %get-tuple-element.35), channel_id=1, source_target_pairs={{0,2},{1,258},{2,0},{3,256},{4,6},{5,262},{6,4},{7,260},{8,10},{9,... | collective-permute-start | bytes 688136 | tf_op jit(solution)/shard_map/ppermute | solution.py:31
  148.9 5.0 %upstream_partial.1 = (f32[384,256]{1,0:T(8,128)}, bf16[384,256]{1,0:T(8,128)(2,1)}, bf16[384,256]{1,0:T(8,128)(2,1)}, bf16[384,256]{1,0:T(8,128)(2,1)}) custom-call(s32[5]{0:T(128)} %stack.47.s_ref, bf16[2,384,896]{2,1,0:T(8,128)(2,1)} %get-tuple-element.20.rows_ref, bf16[2,2,2,448,256]{4,3,2,1,0:T(8,128)(2,1)} %bitcast.46, ...), custom_call_target="tpu_custom_call" | custom-call | tf_op jit(solution)/shard_map/upstream_partial/pallas_call | solution.py:135
  155.8 2.4 %collective-permute-start.16 = (bf16[384,256]{1,0:T(8,128)(2,1)}, bf16[384,256]{1,0:T(8,128)(2,1)S(1)}, u32[]{:S(2)}, u32[]{:S(2)}) collective-permute-start(bf16[384,256]{1,0:T(8,128)(2,1)} %get-tuple-element.25), channel_id=1, source_target_pairs={{0,2},{1,3},{2,0},{3,1},{4,6},{5,7},{6,4},{7,5},{8,10},{9,11},{10,... | collective-permute-start | bytes 589832 | tf_op jit(solution)/shard_map/ppermute | solution.py:16
  158.2 4.9 %collective-permute-start.17 = (bf16[384,256]{1,0:T(8,128)(2,1)}, bf16[384,256]{1,0:T(8,128)(2,1)S(1)}, u32[]{:S(2)}, u32[]{:S(2)}) collective-permute-start(bf16[384,256]{1,0:T(8,128)(2,1)} %get-tuple-element.26), channel_id=1, source_target_pairs={{0,3},{1,2},{2,1},{3,0},{4,7},{5,6},{6,5},{7,4},{8,11},{9,10},{10,... | collective-permute-start | bytes 589832 | tf_op jit(solution)/shard_map/ppermute | solution.py:16
  163.7 7.6 %collective-permute-done.16 = bf16[384,256]{1,0:T(8,128)(2,1)S(1)} collective-permute-done((bf16[384,256]{1,0:T(8,128)(2,1)}, bf16[384,256]{1,0:T(8,128)(2,1)S(1)}, u32[]{:S(2)}, u32[]{:S(2)}) %collective-permute-start.16) | collective-permute-done | bytes 196640 | tf_op jit(solution)/shard_map/ppermute | solution.py:16
  171.3 5.5 %collective-permute-done.17 = bf16[384,256]{1,0:T(8,128)(2,1)S(1)} collective-permute-done((bf16[384,256]{1,0:T(8,128)(2,1)}, bf16[384,256]{1,0:T(8,128)(2,1)S(1)}, u32[]{:S(2)}, u32[]{:S(2)}) %collective-permute-start.17) | collective-permute-done | bytes 196640 | tf_op jit(solution)/shard_map/ppermute | solution.py:16
  177.5 2.7 %finish.1 = (bf16[8,4,24,256]{3,2,1,0:T(8,128)(2,1)}, bf16[8,4,24,256]{3,2,1,0:T(8,128)(2,1)}) custom-call(s32[5]{0:T(128)} %stack.47.s_ref, bf16[8,4,24,256]{3,2,1,0:T(8,128)(2,1)} %bitcast.52, bf16[8,4,24,256]{3,2,1,0:T(8,128)(2,1)} %bitcast.50, f32[8,2,24,256]{3,2,1,0:T(8,128)} %bitcast.58, bf16[8,2,24,256]{3,2,1,0:T(8,128)(2,1)} %bitcast.61, ...), custom_call_target="tpu_custom_call" | custom-call | tf_op jit(solution)/shard_map/finish/pallas_call | solution.py:166
  (38 shorter events, 12.0 us)
Async XLA Ops:
  0.6 19.8 %collective-permute-start.1 = (bf16[448,256]{1,0:T(8,128)(2,1)}, bf16[448,256]{1,0:T(8,128)(2,1)S(1)}, u32[]{:S(2)}, u32[]{:S(2)}) collective-permute-start(bf16[448,256]{1,0:T(8,128)(2,1)} %param.11), channel_id=1, source_target_pairs={{0,2},{1,258},{2,0},{3,256},{4,6},{5,262},{6,4},{7,260},{8,10},{9,... | collective-permute-start | bytes 688136 | tf_op jit(solution)/shard_map/ppermute | solution.py:31
  7.4 15.6 %collective-permute-start = (bf16[448,256]{1,0:T(8,128)(2,1)}, bf16[448,256]{1,0:T(8,128)(2,1)S(1)}, u32[]{:S(2)}, u32[]{:S(2)}) collective-permute-start(bf16[448,256]{1,0:T(8,128)(2,1)} %param.11), channel_id=1, source_target_pairs={{0,0},{1,256},{2,2},{3,258},{4,4},{5,260},{6,6},{7,262},{8,8},{9,2... | collective-permute-start | bytes 688136 | tf_op jit(solution)/shard_map/ppermute | solution.py:31
  23.1 25.5 %copy-start.3 = (bf16[2,448,256]{2,1,0:T(8,128)(2,1)}, bf16[2,448,256]{2,1,0:T(8,128)(2,1)S(1)}, u32[]{:S(2)}) copy-start(bf16[2,448,256]{2,1,0:T(8,128)(2,1)S(1)} %pad_maximum_fusion.1) | copy-start | bytes 1376260
  26.4 59.1 %all-to-all-start = ((bf16[32,24,896]{2,1,0:T(8,128)(2,1)}), bf16[32,24,896]{2,1,0:T(8,128)(2,1)S(1)}, u32[]{:S(2)}, u32[]{:S(2)}) async-start(bf16[32,24,896]{2,1,0:T(8,128)(2,1)} %bitcast.47), calls=%async_computation | async-start | bytes 2752512 | tf_op jit(solution)/shard_map/all_to_all | solution.py:196
  42.1 24.8 %collective-permute-start.4 = (bf16[2,448,256]{2,1,0:T(8,128)(2,1)S(1)}, bf16[2,448,256]{2,1,0:T(8,128)(2,1)S(1)}, u32[]{:S(2)}, u32[]{:S(2)}) collective-permute-start(bf16[2,448,256]{2,1,0:T(8,128)(2,1)S(1)} %pad_maximum_fusion.1), channel_id=1, source_target_pairs={{0,384},{64,448},{128,256},{192,320},{256,128},{320,192},{384,0},{... | collective-permute-start | bytes 1376264 | tf_op jit(solution)/shard_map/ppermute | solution.py:20
  44.9 22.0 %collective-permute-start.3 = (bf16[2,448,256]{2,1,0:T(8,128)(2,1)S(1)}, bf16[2,448,256]{2,1,0:T(8,128)(2,1)S(1)}, u32[]{:S(2)}, u32[]{:S(2)}) collective-permute-start(bf16[2,448,256]{2,1,0:T(8,128)(2,1)S(1)} %pad_maximum_fusion.1), channel_id=1, source_target_pairs={{0,256},{64,320},{128,384},{192,448},{256,0},{320,64},{384,128},{4... | collective-permute-start | bytes 1376264 | tf_op jit(solution)/shard_map/ppermute | solution.py:20
  48.6 20.9 %collective-permute-start.2 = (bf16[2,448,256]{2,1,0:T(8,128)(2,1)S(1)}, bf16[2,448,256]{2,1,0:T(8,128)(2,1)S(1)}, u32[]{:S(2)}, u32[]{:S(2)}) collective-permute-start(bf16[2,448,256]{2,1,0:T(8,128)(2,1)S(1)} %pad_maximum_fusion.1), channel_id=1, source_target_pairs={{0,128},{64,192},{128,0},{192,64},{256,384},{320,448},{384,256},{4... | collective-permute-start | bytes 1376264 | tf_op jit(solution)/shard_map/ppermute | solution.py:20
  70.7 31.9 %copy-start = (bf16[4,2,448,256]{3,2,1,0:T(8,128)(2,1)}, bf16[4,2,448,256]{3,2,1,0:T(8,128)(2,1)S(1)}, u32[]{:S(2)}) copy-start(bf16[4,2,448,256]{3,2,1,0:T(8,128)(2,1)S(1)} %pad_maximum_fusion) | copy-start | bytes 5505028
  70.7 14.9 %collective-permute-start.5 = (bf16[4,2,448,256]{3,2,1,0:T(8,128)(2,1)S(1)}, bf16[4,2,448,256]{3,2,1,0:T(8,128)(2,1)}, u32[]{:S(2)}, u32[]{:S(2)}) collective-permute-start(bf16[4,2,448,256]{3,2,1,0:T(8,128)(2,1)S(1)} %pad_maximum_fusion), channel_id=1, source_target_pairs={{0,64},{64,0},{128,192},{192,128},{256,320},{320,256},{384,448},{4... | collective-permute-start | bytes 5505032 | tf_op jit(solution)/shard_map/ppermute | solution.py:20
  74.7 22.1 %copy-start.4 = (bf16[8,2,24,256]{3,2,1,0:T(8,128)(2,1)}, bf16[8,2,24,256]{3,2,1,0:T(8,128)(2,1)S(1)}, u32[]{:S(2)}) copy-start(bf16[8,2,24,256]{3,2,1,0:T(8,128)(2,1)S(1)} %get-tuple-element.33) | copy-start | bytes 589828
  74.7 10.8 %collective-permute-start.6 = (bf16[384,256]{1,0:T(8,128)(2,1)S(1)}, bf16[384,256]{1,0:T(8,128)(2,1)}, u32[]{:S(2)}, u32[]{:S(2)}) collective-permute-start(bf16[384,256]{1,0:T(8,128)(2,1)S(1)} %bitcast.53), channel_id=1, source_target_pairs={{0,1},{1,0},{2,3},{3,2},{4,5},{5,4},{6,7},{7,6},{8,9},{9,8},{10,11... | collective-permute-start | bytes 589832 | tf_op jit(solution)/shard_map/ppermute | solution.py:16
  77.1 18.4 %collective-permute-start.8 = (bf16[384,256]{1,0:T(8,128)(2,1)}, bf16[384,256]{1,0:T(8,128)(2,1)}, u32[]{:S(2)}, u32[]{:S(2)}) collective-permute-start(bf16[384,256]{1,0:T(8,128)(2,1)} %bitcast.19), channel_id=1, source_target_pairs={{0,3},{1,2},{2,1},{3,0},{4,7},{5,6},{6,5},{7,4},{8,11},{9,10},{10,... | collective-permute-start | bytes 589832 | tf_op jit(solution)/shard_map/ppermute | solution.py:16
  79.1 17.8 %collective-permute-start.7 = (bf16[384,256]{1,0:T(8,128)(2,1)}, bf16[384,256]{1,0:T(8,128)(2,1)}, u32[]{:S(2)}, u32[]{:S(2)}) collective-permute-start(bf16[384,256]{1,0:T(8,128)(2,1)} %bitcast.19), channel_id=1, source_target_pairs={{0,2},{1,3},{2,0},{3,1},{4,6},{5,7},{6,4},{7,5},{8,10},{9,11},{10,... | collective-permute-start | bytes 589832 | tf_op jit(solution)/shard_map/ppermute | solution.py:16
  85.5 11.3 %copy-start.1 = (bf16[32,24,896]{2,1,0:T(8,128)(2,1)}, bf16[32,24,896]{2,1,0:T(8,128)(2,1)S(1)}, u32[]{:S(2)}) copy-start(bf16[32,24,896]{2,1,0:T(8,128)(2,1)S(1)} %all-to-all-done.recv_ref) | copy-start | bytes 4128772
  102.6 7.5 %copy-start.2 = (bf16[2,2,2,2,448,256]{5,4,3,2,1,0:T(8,128)(2,1)S(1)}, bf16[2,2,2,2,448,256]{5,4,3,2,1,0:T(8,128)(2,1)}, u32[]{:S(2)}) copy-start(bf16[2,2,2,2,448,256]{5,4,3,2,1,0:T(8,128)(2,1)} %get-tuple-element.19) | copy-start | bytes 11010052
  104.4 5.7 %collective-permute-start.9 = (bf16[2,2,2,448,256]{4,3,2,1,0:T(8,128)(2,1)S(1)}, bf16[2,2,2,448,256]{4,3,2,1,0:T(8,128)(2,1)S(1)}, u32[]{:S(2)}, u32[]{:S(2)}) collective-permute-start(bf16[2,2,2,448,256]{4,3,2,1,0:T(8,128)(2,1)S(1)} %slice_bitcast_fusion), channel_id=1, source_target_pairs={{0,64},{64,0},{128,192},{192,128},{256,320},{320,256},{384,448},{4... | collective-permute-start | bytes 5505032 | tf_op jit(solution)/shard_map/ppermute | solution.py:20
  110.7 15.3 %collective-permute-start.10 = (bf16[2,448,256]{2,1,0:T(8,128)(2,1)S(1)}, bf16[2,448,256]{2,1,0:T(8,128)(2,1)S(1)}, u32[]{:S(2)}, u32[]{:S(2)}) collective-permute-start(bf16[2,448,256]{2,1,0:T(8,128)(2,1)S(1)} %get-tuple-element.29), channel_id=1, source_target_pairs={{0,128},{64,192},{128,0},{192,64},{256,384},{320,448},{384,256},{4... | collective-permute-start | bytes 1376264 | tf_op jit(solution)/shard_map/ppermute | solution.py:20
  113.2 25.2 %collective-permute-start.12 = (bf16[2,448,256]{2,1,0:T(8,128)(2,1)S(1)}, bf16[2,448,256]{2,1,0:T(8,128)(2,1)S(1)}, u32[]{:S(2)}, u32[]{:S(2)}) collective-permute-start(bf16[2,448,256]{2,1,0:T(8,128)(2,1)S(1)} %get-tuple-element.30), channel_id=1, source_target_pairs={{0,384},{64,448},{128,256},{192,320},{256,128},{320,192},{384,0},{... | collective-permute-start | bytes 1376264 | tf_op jit(solution)/shard_map/ppermute | solution.py:20
  116.0 22.4 %collective-permute-start.11 = (bf16[2,448,256]{2,1,0:T(8,128)(2,1)S(1)}, bf16[2,448,256]{2,1,0:T(8,128)(2,1)S(1)}, u32[]{:S(2)}, u32[]{:S(2)}) collective-permute-start(bf16[2,448,256]{2,1,0:T(8,128)(2,1)S(1)} %get-tuple-element.31), channel_id=1, source_target_pairs={{0,256},{64,320},{128,384},{192,448},{256,0},{320,64},{384,128},{4... | collective-permute-start | bytes 1376264 | tf_op jit(solution)/shard_map/ppermute | solution.py:20
  138.7 41.6 %collective-permute-start.13 = (bf16[448,256]{1,0:T(8,128)(2,1)S(1)}, bf16[448,256]{1,0:T(8,128)(2,1)S(1)}, u32[]{:S(2)}, u32[]{:S(2)}) collective-permute-start(bf16[448,256]{1,0:T(8,128)(2,1)S(1)} %get-tuple-element.34), channel_id=1, source_target_pairs={{0,0},{1,256},{2,2},{3,258},{4,4},{5,260},{6,6},{7,262},{8,8},{9,2... | collective-permute-start | bytes 688136 | tf_op jit(solution)/shard_map/ppermute | solution.py:31
  144.2 36.0 %collective-permute-start.14 = (bf16[448,256]{1,0:T(8,128)(2,1)S(1)}, bf16[448,256]{1,0:T(8,128)(2,1)S(1)}, u32[]{:S(2)}, u32[]{:S(2)}) collective-permute-start(bf16[448,256]{1,0:T(8,128)(2,1)S(1)} %get-tuple-element.35), channel_id=1, source_target_pairs={{0,2},{1,258},{2,0},{3,256},{4,6},{5,262},{6,4},{7,260},{8,10},{9,... | collective-permute-start | bytes 688136 | tf_op jit(solution)/shard_map/ppermute | solution.py:31
  153.9 9.8 %collective-permute-start.15 = (bf16[384,256]{1,0:T(8,128)(2,1)}, bf16[384,256]{1,0:T(8,128)(2,1)S(1)}, u32[]{:S(2)}, u32[]{:S(2)}) collective-permute-start(bf16[384,256]{1,0:T(8,128)(2,1)} %get-tuple-element.24), channel_id=1, source_target_pairs={{0,1},{1,0},{2,3},{3,2},{4,5},{5,4},{6,7},{7,6},{8,9},{9,8},{10,11... | collective-permute-start | bytes 589832 | tf_op jit(solution)/shard_map/ppermute | solution.py:16
  155.8 15.5 %collective-permute-start.16 = (bf16[384,256]{1,0:T(8,128)(2,1)}, bf16[384,256]{1,0:T(8,128)(2,1)S(1)}, u32[]{:S(2)}, u32[]{:S(2)}) collective-permute-start(bf16[384,256]{1,0:T(8,128)(2,1)} %get-tuple-element.25), channel_id=1, source_target_pairs={{0,2},{1,3},{2,0},{3,1},{4,6},{5,7},{6,4},{7,5},{8,10},{9,11},{10,... | collective-permute-start | bytes 589832 | tf_op jit(solution)/shard_map/ppermute | solution.py:16
  158.2 18.7 %collective-permute-start.17 = (bf16[384,256]{1,0:T(8,128)(2,1)}, bf16[384,256]{1,0:T(8,128)(2,1)S(1)}, u32[]{:S(2)}, u32[]{:S(2)}) collective-permute-start(bf16[384,256]{1,0:T(8,128)(2,1)} %get-tuple-element.26), channel_id=1, source_target_pairs={{0,3},{1,2},{2,1},{3,0},{4,7},{5,6},{6,5},{7,4},{8,11},{9,10},{10,... | collective-permute-start | bytes 589832 | tf_op jit(solution)/shard_map/ppermute | solution.py:16
  163.7 13.1 %copy-start.5 = (bf16[384,256]{1,0:T(8,128)(2,1)}, bf16[384,256]{1,0:T(8,128)(2,1)S(1)}, u32[]{:S(2)}) copy-start(bf16[384,256]{1,0:T(8,128)(2,1)S(1)} %collective-permute-done.15) | copy-start | bytes 589828
  171.3 5.5 %copy-start.6 = (bf16[384,256]{1,0:T(8,128)(2,1)}, bf16[384,256]{1,0:T(8,128)(2,1)S(1)}, u32[]{:S(2)}) copy-start(bf16[384,256]{1,0:T(8,128)(2,1)S(1)} %collective-permute-done.16) | copy-start | bytes 589828
  176.8 0.7 copy-start.7

commit v2 on v1

v2 whole, which is shorter than its diff:
```python
import jax
import jax.numpy as jnp
from jax import lax
from jax.experimental import pallas as pl
from jax.experimental.pallas import tpu as pltpu
from jax.sharding import PartitionSpec as P


CAP = 12
PART = 24
BF = jnp.bfloat16
F32 = jnp.float32
VMEM_LIMIT = 16 * 1024 * 1024


def expert_xor(value, mask):
    return lax.ppermute(value, "expert", [(i, i ^ mask) for i in range(lax.axis_size("expert"))])


def dp_xor(value, mask):
    return lax.ppermute(value, "dp", [(i, i ^ mask) for i in range(lax.axis_size("dp"))])


def swapped(value, flip):
    experts = lax.axis_size("expert")
    pairs = []
    for d in range(lax.axis_size("dp")):
        for s in range(experts):
            to_dp = (s & 1) * 4 + (d & 3)
            to_expert = (s & ~3) + (((s >> 1) & 1) ^ flip) * 2 + (d >> 2)
            pairs.append((d * experts + s, to_dp * experts + to_expert))
    return lax.ppermute(value, ("dp", "expert"), pairs)


SCALARS = pl.BlockSpec(memory_space=pltpu.SMEM)
WHOLE = pl.BlockSpec(memory_space=pltpu.VMEM)
PARAMS = pltpu.CompilerParams(vmem_limit_bytes=VMEM_LIMIT)


def cost(flops, size):
    return pl.CostEstimate(flops=flops, transcendentals=0, bytes_accessed=size)


def slots_body(ids_ref, weights_ref, cot_ref, out_ref):
    tokens = ids_ref.shape[1]
    experts = out_ref.shape[0]
    half = out_ref.shape[3]
    ids = jnp.broadcast_to(ids_ref[...].astype(F32), (tokens, tokens))
    row = lax.broadcasted_iota(jnp.int32, (tokens, tokens), 0)
    col = lax.broadcasted_iota(jnp.int32, (tokens, tokens), 1)
    ids_down = jnp.sum(jnp.where(row == col, ids, 0.0), axis=1, keepdims=True)
    earlier = jnp.where((ids_down == ids) & (row < col), 1.0, 0.0)
    position = jnp.sum(earlier, axis=0, keepdims=True)
    target = (ids_ref[...].astype(F32) * PART + position).astype(jnp.int32)
    place = lax.broadcasted_iota(jnp.int32, (experts * PART, tokens), 0)
    first = place == target
    second = place == target + CAP
    scale = jnp.sum(jnp.where(first | second, weights_ref[...], 0.0), axis=1, keepdims=True)
    picked = jnp.dot(
        first.astype(F32).astype(BF), cot_ref[:, :half], preferred_element_type=F32
    ) + jnp.dot(second.astype(F32).astype(BF), cot_ref[:, half:], preferred_element_type=F32)
    rows = picked * scale
    for x in range(experts):
        out_ref[x, 0] = rows[x * PART : (x + 1) * PART].astype(BF)


def slot_buffer(cotangent, expert_ids, route_weights, experts):
    tokens, width = cotangent.shape
    return pl.pallas_call(
        slots_body,
        grid=(2,),
        in_specs=[
            pl.BlockSpec((1, tokens), lambda k: (0, 0)),
            pl.BlockSpec((1, tokens), lambda k: (0, 0)),
            pl.BlockSpec((tokens, width // 2), lambda k: (0, k)),
        ],
        out_specs=pl.BlockSpec((experts, 1, PART, width // 4), lambda k: (0, k, 0, 0)),
        out_shape=jax.ShapeDtypeStruct((experts, 2, PART, width // 4), BF),
        compiler_params=PARAMS,
        cost_estimate=cost(4 * tokens * experts * PART * width, 4 * tokens * width),
        name="slots",
    )(
        *(
            pltpu.with_memory_space_constraint(value, pltpu.HBM)
            for value in (
                expert_ids.reshape(1, tokens),
                route_weights.reshape(1, tokens),
                cotangent,
            )
        )
    )


def product_body(s_ref, gate_ref, up_ref, out_ref):
    group = s_ref[4]
    for t in range(4):
        gate = gate_ref[:, t].astype(F32)
        value = (gate * jax.nn.sigmoid(gate) * up_ref[:, t].astype(F32)).astype(BF)
        side = group ^ (0 if t in (0, 3) else 1)
        out_ref[side, :, t >> 1] = value


def products(scalars, gate, up):
    ys, _, part, columns = gate.shape
    return pl.pallas_call(
        product_body,
        in_specs=[SCALARS, WHOLE, WHOLE],
        out_specs=WHOLE,
        out_shape=jax.ShapeDtypeStruct((2, ys, 2, part, columns), BF),
        compiler_params=PARAMS,
        cost_estimate=cost(gate.size * 200, gate.size * 8),
        name="products",
    )(scalars, gate, up)


def slot_of(e, r1, r0):
    near, far = ((4, 0), (1, 5)) if e == 0 else ((6, 7), (3, 2))
    return jnp.where(r1 == 0, jnp.where(r0 == 0, *near), jnp.where(r0 == 0, *far))


def weight_body(s_ref, recv_ref, p0, p1, p2, p3, rows_ref, keep_ref, send_ref):
    core, k, a1, a0 = s_ref[0], s_ref[1], s_ref[2], s_ref[3]
    sources = recv_ref.shape[0]
    block = keep_ref.shape[1]
    for b in range(2):
        for s in range(sources):
            rows_ref[b, s * CAP : (s + 1) * CAP, :] = recv_ref[s, b * CAP : (b + 1) * CAP, :]
    for b in range(2):
        for q, piece in enumerate((p0, p1, p2, p3)):
            grad = lax.dot_general(
                rows_ref[b], piece[...], (((0,), (0,)), ((), ())), preferred_element_type=F32
            ).astype(BF)
            low, high = grad[:block], grad[block:]
            place = slot_of(q >> 1, (q & 1) ^ k ^ a1, b ^ a0)
            keep_ref[place] = jnp.where(core == 0, low, high)
            send_ref[place] = jnp.where(core == 0, high, low)


def weight_partial(scalars, recv, pieces, block):
    sources, _, half = recv.shape
    count = sources * CAP
    columns = pieces[0].shape[1]
    grad = jax.ShapeDtypeStruct((8, block, columns), BF)
    return pl.pallas_call(
        weight_body,
        in_specs=[SCALARS] + [WHOLE] * 5,
        out_specs=[WHOLE] * 3,
        out_shape=[jax.ShapeDtypeStruct((2, count, half), BF), grad, grad],
        compiler_params=PARAMS,
        cost_estimate=cost(16 * count * half * columns, 8 * count * half),
        name="weight_partial",
    )(scalars, recv, *pieces)


def upstream_body(s_ref, rows_ref, near_ref, far_ref, *out_refs):
    core, k, a1, a0 = s_ref[0], s_ref[1], s_ref[2], s_ref[3]
    for q in range(4):
        total = None
        for b in range(2):
            near = near_ref[((q & 1) ^ k ^ a1) * 2 + (b ^ a0), q >> 1]
            far = far_ref[((q & 1) ^ k ^ a1) * 2 + (b ^ a0), q >> 1]
            low = jnp.where(core == 0, near, far)
            high = jnp.where(core == 0, far, near)
            part = jnp.dot(
                rows_ref[b], jnp.concatenate([low, high], axis=0), preferred_element_type=F32
            )
            total = part if total is None else total + part
        out_refs[q][...] = total.astype(BF)


def upstream_partial(scalars, rows, near, far):
    _, count, half = rows.shape
    columns = near.shape[-1]
    return pl.pallas_call(
        upstream_body,
        in_specs=[SCALARS, WHOLE, WHOLE, WHOLE],
        out_specs=[WHOLE] * 4,
        out_shape=[jax.ShapeDtypeStruct((count, columns), BF)] * 4,
        compiler_params=PARAMS,
        cost_estimate=cost(16 * count * half * columns, 8 * count * half),
        name="upstream_partial",
    )(scalars, rows, near, far)


def finish_body(s_ref, gate_ref, up_ref, c0, c1, c2, c3, gate_out, up_out):
    group = s_ref[4]
    for side in range(2):
        for t in range(2):
            left, right = ((c0, c1), (c2, c3))[side]
            part = left[:, t].astype(F32) + right[:, t].astype(F32)
            index = jnp.where((group ^ side) == 0, 3 * t, 1 + t)
            gate = gate_ref[:, index].astype(F32)
            up = up_ref[:, index].astype(F32)
            sigmoid = jax.nn.sigmoid(gate)
            gate_out[:, index] = (part * up * sigmoid * (1.0 + gate * (1.0 - sigmoid))).astype(BF)
            up_out[:, index] = (part * (gate * sigmoid)).astype(BF)


def finish(scalars, gate, up, parts):
    return pl.pallas_call(
        finish_body,
        in_specs=[SCALARS] + [WHOLE] * 6,
        out_specs=[WHOLE] * 2,
        out_shape=[jax.ShapeDtypeStruct(gate.shape, BF)] * 2,
        compiler_params=PARAMS,
        cost_estimate=cost(gate.size * 200, gate.size * 12),
        name="finish",
    )(scalars, gate, up, *parts)


def added(left, right):
    return (left.astype(F32) + right.astype(F32)).astype(BF)


def dispatched(slots):
    ys = lax.axis_size("expert") // 8
    lists = [[y * 8 + z for y in range(ys) for z in zs] for zs in ((0, 1, 6, 7), (2, 3, 4, 5))]
    return lax.all_to_all(
        slots, "expert", split_axis=0, concat_axis=0, tiled=True, axis_index_groups=lists
    )


def per_device(cotangent, expert_ids, route_weights, gate_pre, up_pre, down_weight):
    devices = lax.axis_size("expert")
    experts = devices // 4
    ys = devices // 8
    columns = gate_pre.shape[1]
    block = down_weight.shape[0]
    dp = lax.axis_index("dp")
    place = lax.axis_index("expert")
    group = ((place >> 2) ^ (place >> 1)) & 1
    scalars = jnp.stack([dp & 1, place & 1, dp >> 2, (dp >> 1) & 1, group]).astype(jnp.int32)
    gate4 = gate_pre.reshape(ys, 4, PART, columns)
    up4 = up_pre.reshape(ys, 4, PART, columns)

    own = [swapped(down_weight, flip) for flip in range(2)]
    sent = products(scalars, gate4, up4).reshape(2, -1, columns)
    slots = slot_buffer(cotangent, expert_ids, route_weights, experts)
    recv = dispatched(slots.reshape(devices // 2, PART, slots.shape[3]))
    pieces = [sent[0]] + [expert_xor(sent[q >> 1], q) for q in (1, 2, 3)]
    own = jnp.stack(own)
    near = jnp.stack([own] + [dp_xor(own, mask) for mask in (2, 4, 6)])
    far = dp_xor(near, 1)

    recv, near, far = lax.optimization_barrier((recv, near, far))
    rows, keep, send = weight_partial(scalars, recv, pieces, block)
    crossed = dp_xor(send, 1)
    parts = upstream_partial(scalars, rows, near, far)
    summed = added(keep, crossed)
    first = [dp_xor(summed[0:2], 2), dp_xor(summed[2:4], 6)]
    parts = [parts[0]] + [expert_xor(parts[q], q) for q in (1, 2, 3)]
    parts = [part.reshape(ys, 2, PART, columns) for part in parts]
    first = [added(summed[4:6], first[0]), added(summed[6:8], first[1])]
    second = [dp_xor(first[0][1], 6), dp_xor(first[1][1], 2)]
    kept = [added(first[e][0], second[e]) for e in range(2)]
    weight_grad = added(swapped(kept[0], 0), swapped(kept[1], 1))
    gate_grad, up_grad = finish(scalars, gate4, up4, parts)
    return (
        weight_grad,
        gate_grad.reshape(gate_pre.shape),
        up_grad.reshape(up_pre.shape),
    )


def solution(mesh):
    placed = (
        P(("dp", "expert"), None),
        P(("dp", "expert"), None),
        P(("dp", "expert"), None),
        P("dp", "expert"),
        P("dp", "expert"),
        P("dp", "expert"),
    )
    return jax.shard_map(
        per_device,
        mesh=mesh,
        in_specs=placed,
        out_specs=(P("dp", "expert"), P("dp", "expert"), P("dp", "expert")),
        check_vma=False,
    )
```

time: 182 us -> 158 us (0.87)
  waiting for transfers between devices: 74.6 us -> 62.5 us
  Pallas kernels: 16.9 us -> 12.7 us
  other arithmetic: 4.87 us -> 1.93 us
  local copies, waits for them, and re-layouts: 3.27 us -> 0.89 us
  starting transfers between devices: 80.5 us -> 78.2 us
    ppermute x4, waiting for transfers between devices: 10.5 us -> 0.01 us  [swapped(): return lax.ppermute(value, ('dp', 'expert'), pairs)]
    all_to_all x1, starting transfers between devices: 15.6 us -> 10.9 us  [dispatched(): lax.all_to_all(slots, 'expert', split_axis=0, concat_axis=0, tiled=True,...]
    ppermute x8 -> x9, waiting for transfers between devices: 39.1 us -> 34.9 us  [dp_xor(): lax.ppermute(value, 'dp', [(i, i ^ mask) for i in range(lax.axis_size('dp...]
    pallas_call x3 -> x4, Pallas kernels: 13.5 us -> 9.5 us  [the longest x1 3.55 us: weight_partial(): pl.pallas_call(weight_body, in_specs=[SCALARS] + [WHOLE] * 5, out_specs=[...]
    ppermute x6, waiting for transfers between devices: 25 us -> 27.5 us  [expert_xor(): lax.ppermute(value, 'expert', [(i, i ^ mask) for i in range(lax.axis_size...]
    ppermute x8 -> x9, starting transfers between devices: 23.5 us -> 25.7 us  [dp_xor(): lax.ppermute(value, 'dp', [(i, i ^ mask) for i in range(lax.axis_size('dp...]
    squeeze x3 -> x2, local copies, waits for them, and re-layouts: 1.89 us -> 0.03 us  [per_device(): second = [dp_xor(first[0][1], 6), dp_xor(first[1][1], 2)]]
  transfers between devices with their start and end apart: 19 -> 20, of which waited for: 12 -> 12; matrix products, arithmetic and copies ran while one was open for 2% -> 1% of each run, Pallas kernels for 4% -> 6%
where the time goes in v2:
time: 158 us; the launch traced here: 157 us
  starting transfers between devices  78.2 us (49%)
  waiting for transfers between devices  62.5 us (40%)
  Pallas kernels  12.7 us (8%)
  other arithmetic  1.93 us (1%)
    ppermute x9, waiting for transfers between devices, dp_xor(): lax.ppermute(value, 'dp', [(i, i ^ mask) for i in range(lax.axis_size('dp...  34.9 us
    ppermute x6, waiting for transfers between devices, expert_xor(): lax.ppermute(value, 'expert', [(i, i ^ mask) for i in range(lax.axis_size...  27.5 us
    ppermute x9, starting transfers between devices, dp_xor(): lax.ppermute(value, 'dp', [(i, i ^ mask) for i in range(lax.axis_size('dp...  25.7 us
    ppermute x4, starting transfers between devices, swapped(): return lax.ppermute(value, ('dp', 'expert'), pairs)  22.3 us
    ppermute x6, starting transfers between devices, expert_xor(): lax.ppermute(value, 'expert', [(i, i ^ mask) for i in range(lax.axis_size...  19.3 us
    all_to_all x1, starting transfers between devices, dispatched(): lax.all_to_all(slots, 'expert', split_axis=0, concat_axis=0, tiled=True,...  10.9 us
    pallas_call x1, Pallas kernels, weight_partial(): pl.pallas_call(weight_body, in_specs=[SCALARS] + [WHOLE] * 5, out_specs=[...  3.55 us
    pallas_call x1, Pallas kernels, upstream_partial(): pl.pallas_call(upstream_body, in_specs=[SCALARS, WHOLE, WHOLE, WHOLE], ou...  3.39 us
  transfers between devices with their start and end apart: 20, of which 12 were waited for; matrix products, arithmetic and copies ran while one was open for 1% of the time, Pallas kernels for 6%

profile of v2, /device:TPU:64, one launch (start us, length us, event | category | flops | bytes accessed | tf_op | source)
XLA Modules:
  0.0 157.1 jit_solution(16096700217005340786)
XLA Ops:
  0.6 6.7 %collective-permute-start.1 = (bf16[448,256]{1,0:T(8,128)(2,1)}, bf16[448,256]{1,0:T(8,128)(2,1)S(1)}, u32[]{:S(2)}, u32[]{:S(2)}) collective-permute-start(bf16[448,256]{1,0:T(8,128)(2,1)} %param.11), channel_id=1, source_target_pairs={{0,2},{1,258},{2,0},{3,256},{4,6},{5,262},{6,4},{7,260},{8,10},{9,... | collective-permute-start | bytes 688136 | tf_op jit(solution)/shard_map/ppermute | solution.py:32
  7.4 5.1 %collective-permute-start = (bf16[448,256]{1,0:T(8,128)(2,1)}, bf16[448,256]{1,0:T(8,128)(2,1)S(1)}, u32[]{:S(2)}, u32[]{:S(2)}) collective-permute-start(bf16[448,256]{1,0:T(8,128)(2,1)} %param.11), channel_id=1, source_target_pairs={{0,0},{1,256},{2,2},{3,258},{4,4},{5,260},{6,6},{7,262},{8,8},{9,2... | collective-permute-start | bytes 688136 | tf_op jit(solution)/shard_map/ppermute | solution.py:32
  12.5 3.2 %slots.1 = bf16[16,2,24,896]{3,2,1,0:T(8,128)(2,1)} custom-call(s32[1,128]{1,0:T(1,128)} %bitcast.56, f32[1,128]{1,0:T(1,128)} %bitcast.57, bf16[128,3584]{1,0:T(8,128)(2,1)} %cot_ref.1), custom_call_target="tpu_custom_call" | custom-call | flops 704643072 | bytes 1835008 | tf_op jit(solution)/shard_map/slots/pallas_call | solution.py:69
  15.7 10.9 %all-to-all-start = ((bf16[32,24,896]{2,1,0:T(8,128)(2,1)}), bf16[32,24,896]{2,1,0:T(8,128)(2,1)}, u32[]{:S(2)}, u32[]{:S(2)}) async-start(bf16[32,24,896]{2,1,0:T(8,128)(2,1)} %bitcast.7), calls=%async_computation | async-start | bytes 2752512 | tf_op jit(solution)/shard_map/all_to_all | solution.py:218
  26.7 5.8 %collective-permute-start.3 = (bf16[2,448,256]{2,1,0:T(8,128)(2,1)S(1)}, bf16[2,448,256]{2,1,0:T(8,128)(2,1)S(1)}, u32[]{:S(2)}, u32[]{:S(2)}) collective-permute-start(bf16[2,448,256]{2,1,0:T(8,128)(2,1)S(1)} %get-tuple-element.32), channel_id=1, source_target_pairs={{0,256},{64,320},{128,384},{192,448},{256,0},{320,64},{384,128},{4... | collective-permute-start | bytes 1376264 | tf_op jit(solution)/shard_map/ppermute | solution.py:21
  32.5 2.5 %collective-permute-start.2 = (bf16[2,448,256]{2,1,0:T(8,128)(2,1)S(1)}, bf16[2,448,256]{2,1,0:T(8,128)(2,1)S(1)}, u32[]{:S(2)}, u32[]{:S(2)}) collective-permute-start(bf16[2,448,256]{2,1,0:T(8,128)(2,1)S(1)} %get-tuple-element.32), channel_id=1, source_target_pairs={{0,128},{64,192},{128,0},{192,64},{256,384},{320,448},{384,256},{4... | collective-permute-start | bytes 1376264 | tf_op jit(solution)/shard_map/ppermute | solution.py:21
  35.0 1.9 %collective-permute-start.4 = (bf16[2,448,256]{2,1,0:T(8,128)(2,1)S(1)}, bf16[2,448,256]{2,1,0:T(8,128)(2,1)S(1)}, u32[]{:S(2)}, u32[]{:S(2)}) collective-permute-start(bf16[2,448,256]{2,1,0:T(8,128)(2,1)S(1)} %get-tuple-element.32), channel_id=1, source_target_pairs={{0,384},{64,448},{128,256},{192,320},{256,128},{320,192},{384,0},{... | collective-permute-start | bytes 1376264 | tf_op jit(solution)/shard_map/ppermute | solution.py:21
  36.9 6.9 %collective-permute-done.3 = bf16[2,448,256]{2,1,0:T(8,128)(2,1)S(1)} collective-permute-done((bf16[2,448,256]{2,1,0:T(8,128)(2,1)S(1)}, bf16[2,448,256]{2,1,0:T(8,128)(2,1)S(1)}, u32[]{:S(2)}, u32[]{:S(2)}) %collective-permute-start.3) | collective-permute-done | bytes 458784 | tf_op jit(solution)/shard_map/ppermute | solution.py:21
  43.9 8.2 %collective-permute-done.2 = bf16[2,448,256]{2,1,0:T(8,128)(2,1)S(1)} collective-permute-done((bf16[2,448,256]{2,1,0:T(8,128)(2,1)S(1)}, bf16[2,448,256]{2,1,0:T(8,128)(2,1)S(1)}, u32[]{:S(2)}, u32[]{:S(2)}) %collective-permute-start.2) | collective-permute-done | bytes 458784 | tf_op jit(solution)/shard_map/ppermute | solution.py:21
  52.3 1.9 %collective-permute-start.5 = (bf16[4,2,448,256]{3,2,1,0:T(8,128)(2,1)S(1)}, bf16[4,2,448,256]{3,2,1,0:T(8,128)(2,1)}, u32[]{:S(2)}, u32[]{:S(2)}) collective-permute-start(bf16[4,2,448,256]{3,2,1,0:T(8,128)(2,1)S(1)} %pad_maximum_fusion.near_ref), channel_id=1, source_target_pairs={{0,64},{64,0},{128,192},{192,128},{256,320},{320,256},{384,448},{4... | collective-permute-start | bytes 5505032 | tf_op jit(solution)/shard_map/ppermute | solution.py:21
  55.8 2.5 %collective-permute-start.6 = (bf16[384,256]{1,0:T(8,128)(2,1)S(1)}, bf16[384,256]{1,0:T(8,128)(2,1)S(1)}, u32[]{:S(2)}, u32[]{:S(2)}) collective-permute-start(bf16[384,256]{1,0:T(8,128)(2,1)S(1)} %bitcast.43), channel_id=1, source_target_pairs={{0,1},{1,0},{2,3},{3,2},{4,5},{5,4},{6,7},{7,6},{8,9},{9,8},{10,11... | collective-permute-start | bytes 589832 | tf_op jit(solution)/shard_map/ppermute | solution.py:17
  58.2 5.2 %collective-permute-start.8 = (bf16[384,256]{1,0:T(8,128)(2,1)}, bf16[384,256]{1,0:T(8,128)(2,1)S(1)}, u32[]{:S(2)}, u32[]{:S(2)}) collective-permute-start(bf16[384,256]{1,0:T(8,128)(2,1)} %bitcast.17), channel_id=1, source_target_pairs={{0,3},{1,2},{2,1},{3,0},{4,7},{5,6},{6,5},{7,4},{8,11},{9,10},{10,... | collective-permute-start | bytes 589832 | tf_op jit(solution)/shard_map/ppermute | solution.py:17
  63.4 2.5 %collective-permute-start.7 = (bf16[384,256]{1,0:T(8,128)(2,1)}, bf16[384,256]{1,0:T(8,128)(2,1)S(1)}, u32[]{:S(2)}, u32[]{:S(2)}) collective-permute-start(bf16[384,256]{1,0:T(8,128)(2,1)} %bitcast.17), channel_id=1, source_target_pairs={{0,2},{1,3},{2,0},{3,1},{4,6},{5,7},{6,4},{7,5},{8,10},{9,11},{10,... | collective-permute-start | bytes 589832 | tf_op jit(solution)/shard_map/ppermute | solution.py:17
  65.9 11.9 %collective-permute-done.8.p3 = bf16[384,256]{1,0:T(8,128)(2,1)S(1)} collective-permute-done((bf16[384,256]{1,0:T(8,128)(2,1)}, bf16[384,256]{1,0:T(8,128)(2,1)S(1)}, u32[]{:S(2)}, u32[]{:S(2)}) %collective-permute-start.8) | collective-permute-done | bytes 196640 | tf_op jit(solution)/shard_map/ppermute | solution.py:17
  77.8 3.0 %collective-permute-done.7.p2 = bf16[384,256]{1,0:T(8,128)(2,1)S(1)} collective-permute-done((bf16[384,256]{1,0:T(8,128)(2,1)}, bf16[384,256]{1,0:T(8,128)(2,1)S(1)}, u32[]{:S(2)}, u32[]{:S(2)}) %collective-permute-start.7) | collective-permute-done | bytes 196640 | tf_op jit(solution)/shard_map/ppermute | solution.py:17
  80.8 3.6 %weight_partial.1 = (bf16[2,384,896]{2,1,0:T(8,128)(2,1)S(1)}, bf16[8,448,256]{2,1,0:T(8,128)(2,1)S(1)}, bf16[8,448,256]{2,1,0:T(8,128)(2,1)S(1)}) custom-call(s32[5]{0:T(128)S(1)} %stack.47.s_ref, bf16[32,24,896]{2,1,0:T(8,128)(2,1)} %all-to-all-done.recv_ref, bf16[384,256]{1,0:T(8,128)(2,1)S(1)} %bitcast.44, ...), custom_call_target="tpu_custom_call" | custom-call | flops 1409286144 | bytes 2752512 | tf_op jit(solution)/shard_map/weight_partial/pallas_call | solution.py:144
  84.3 1.9 %collective-permute-start.9 = (bf16[8,448,256]{2,1,0:T(8,128)(2,1)S(1)}, bf16[8,448,256]{2,1,0:T(8,128)(2,1)S(1)}, u32[]{:S(2)}, u32[]{:S(2)}) collective-permute-start(bf16[8,448,256]{2,1,0:T(8,128)(2,1)S(1)} %get-tuple-element.17), channel_id=1, source_target_pairs={{0,64},{64,0},{128,192},{192,128},{256,320},{320,256},{384,448},{4... | collective-permute-start | bytes 5505032 | tf_op jit(solution)/shard_map/ppermute | solution.py:21
  86.3 3.8 %collective-permute-done.9 = bf16[8,448,256]{2,1,0:T(8,128)(2,1)S(1)} collective-permute-done((bf16[8,448,256]{2,1,0:T(8,128)(2,1)S(1)}, bf16[8,448,256]{2,1,0:T(8,128)(2,1)S(1)}, u32[]{:S(2)}, u32[]{:S(2)}) %collective-permute-start.9) | collective-permute-done | bytes 1835040 | tf_op jit(solution)/shard_map/ppermute | solution.py:21
  90.6 3.4 %collective-permute-start.10 = (bf16[2,448,256]{2,1,0:T(8,128)(2,1)S(1)}, bf16[2,448,256]{2,1,0:T(8,128)(2,1)S(1)}, u32[]{:S(2)}, u32[]{:S(2)}) collective-permute-start(bf16[2,448,256]{2,1,0:T(8,128)(2,1)S(1)} %get-tuple-element.29), channel_id=1, source_target_pairs={{0,128},{64,192},{128,0},{192,64},{256,384},{320,448},{384,256},{4... | collective-permute-start | bytes 1376264 | tf_op jit(solution)/shard_map/ppermute | solution.py:21
  94.0 3.1 %collective-permute-start.13 = (bf16[2,448,256]{2,1,0:T(8,128)(2,1)S(1)}, bf16[2,448,256]{2,1,0:T(8,128)(2,1)S(1)}, u32[]{:S(2)}, u32[]{:S(2)}) collective-permute-start(bf16[2,448,256]{2,1,0:T(8,128)(2,1)S(1)} %get-tuple-element.30), channel_id=1, source_target_pairs={{0,384},{64,448},{128,256},{192,320},{256,128},{320,192},{384,0},{... | collective-permute-start | bytes 1376264 | tf_op jit(solution)/shard_map/ppermute | solution.py:21
  97.1 7.9 %collective-permute-done.10 = bf16[2,448,256]{2,1,0:T(8,128)(2,1)S(1)} collective-permute-done((bf16[2,448,256]{2,1,0:T(8,128)(2,1)S(1)}, bf16[2,448,256]{2,1,0:T(8,128)(2,1)S(1)}, u32[]{:S(2)}, u32[]{:S(2)}) %collective-permute-start.10) | collective-permute-done | bytes 458784 | tf_op jit(solution)/shard_map/ppermute | solution.py:21
  105.1 4.3 %collective-permute-done.13 = bf16[2,448,256]{2,1,0:T(8,128)(2,1)S(1)} collective-permute-done((bf16[2,448,256]{2,1,0:T(8,128)(2,1)S(1)}, bf16[2,448,256]{2,1,0:T(8,128)(2,1)S(1)}, u32[]{:S(2)}, u32[]{:S(2)}) %collective-permute-start.13) | collective-permute-done | bytes 458784 | tf_op jit(solution)/shard_map/ppermute | solution.py:21
  111.6 3.1 %collective-permute-start.11 = (bf16[448,256]{1,0:T(8,128)(2,1)S(1)}, bf16[448,256]{1,0:T(8,128)(2,1)S(1)}, u32[]{:S(2)}, u32[]{:S(2)}) collective-permute-start(bf16[448,256]{1,0:T(8,128)(2,1)S(1)} %slice_bitcast_fusion.2), channel_id=1, source_target_pairs={{0,384},{64,448},{128,256},{192,320},{256,128},{320,192},{384,0},{... | collective-permute-start | bytes 688136 | tf_op jit(solution)/shard_map/ppermute | solution.py:21
  114.8 3.3 %collective-permute-done.14 = bf16[448,256]{1,0:T(8,128)(2,1)S(1)} collective-permute-done((bf16[448,256]{1,0:T(8,128)(2,1)S(1)}, bf16[448,256]{1,0:T(8,128)(2,1)S(1)}, u32[]{:S(2)}, u32[]{:S(2)}) %collective-permute-start.14) | collective-permute-done | bytes 229408 | tf_op jit(solution)/shard_map/ppermute | solution.py:21
  118.1 2.6 %collective-permute-start.15 = (bf16[448,256]{1,0:T(8,128)(2,1)S(1)}, bf16[448,256]{1,0:T(8,128)(2,1)S(1)}, u32[]{:S(2)}, u32[]{:S(2)}) collective-permute-start(bf16[448,256]{1,0:T(8,128)(2,1)S(1)} %fusion), channel_id=1, source_target_pairs={{0,2},{1,258},{2,0},{3,256},{4,6},{5,262},{6,4},{7,260},{8,10},{9,... | collective-permute-start | bytes 688136 | tf_op jit(solution)/shard_map/ppermute | solution.py:32
  121.3 7.9 %collective-permute-start.12 = (bf16[448,256]{1,0:T(8,128)(2,1)S(1)}, bf16[448,256]{1,0:T(8,128)(2,1)S(1)}, u32[]{:S(2)}, u32[]{:S(2)}) collective-permute-start(bf16[448,256]{1,0:T(8,128)(2,1)S(1)} %fusion.1), channel_id=1, source_target_pairs={{0,0},{1,256},{2,2},{3,258},{4,4},{5,260},{6,6},{7,262},{8,8},{9,2... | collective-permute-start | bytes 688136 | tf_op jit(solution)/shard_map/ppermute | solution.py:32
  129.2 3.4 %upstream_partial.1 = (bf16[384,256]{1,0:T(8,128)(2,1)S(1)}, bf16[384,256]{1,0:T(8,128)(2,1)S(1)}, bf16[384,256]{1,0:T(8,128)(2,1)S(1)}, bf16[384,256]{1,0:T(8,128)(2,1)S(1)}) custom-call(s32[5]{0:T(128)S(1)} %stack.47.s_ref, bf16[2,384,896]{2,1,0:T(8,128)(2,1)S(1)} %get-tuple-element.18.rows_ref, bf16[4,2,448,256]{3,2,1,0:T(8,128)(2,1)S(1)} %pad_maximum_fusion.near_ref, ...), custom_call_target="tpu_custom_call" | custom-call | flops 1409286144 | bytes 2752512 | tf_op jit(solution)/shard_map/upstream_partial/pallas_call | solution.py:174
  132.6 1.9 %collective-permute-start.16 = (bf16[384,256]{1,0:T(8,128)(2,1)S(1)}, bf16[384,256]{1,0:T(8,128)(2,1)S(1)}, u32[]{:S(2)}, u32[]{:S(2)}) collective-permute-start(bf16[384,256]{1,0:T(8,128)(2,1)S(1)} %get-tuple-element.22), channel_id=1, source_target_pairs={{0,1},{1,0},{2,3},{3,2},{4,5},{5,4},{6,7},{7,6},{8,9},{9,8},{10,11... | collective-permute-start | bytes 589832 | tf_op jit(solution)/shard_map/ppermute | solution.py:17
  134.5 1.9 %collective-permute-start.17 = (bf16[384,256]{1,0:T(8,128)(2,1)S(1)}, bf16[384,256]{1,0:T(8,128)(2,1)S(1)}, u32[]{:S(2)}, u32[]{:S(2)}) collective-permute-start(bf16[384,256]{1,0:T(8,128)(2,1)S(1)} %get-tuple-element.23), channel_id=1, source_target_pairs={{0,2},{1,3},{2,0},{3,1},{4,6},{5,7},{6,4},{7,5},{8,10},{9,11},{10,... | collective-permute-start | bytes 589832 | tf_op jit(solution)/shard_map/ppermute | solution.py:17
  136.5 5.4 %collective-permute-start.18 = (bf16[384,256]{1,0:T(8,128)(2,1)S(1)}, bf16[384,256]{1,0:T(8,128)(2,1)S(1)}, u32[]{:S(2)}, u32[]{:S(2)}) collective-permute-start(bf16[384,256]{1,0:T(8,128)(2,1)S(1)} %get-tuple-element.24), channel_id=1, source_target_pairs={{0,3},{1,2},{2,1},{3,0},{4,7},{5,6},{6,5},{7,4},{8,11},{9,10},{10,... | collective-permute-start | bytes 589832 | tf_op jit(solution)/shard_map/ppermute | solution.py:17
  142.8 5.9 %collective-permute-done.17 = bf16[384,256]{1,0:T(8,128)(2,1)S(1)} collective-permute-done((bf16[384,256]{1,0:T(8,128)(2,1)S(1)}, bf16[384,256]{1,0:T(8,128)(2,1)S(1)}, u32[]{:S(2)}, u32[]{:S(2)}) %collective-permute-start.17) | collective-permute-done | bytes 196640 | tf_op jit(solution)/shard_map/ppermute | solution.py:17
  148.7 5.8 %collective-permute-done.18 = bf16[384,256]{1,0:T(8,128)(2,1)S(1)} collective-permute-done((bf16[384,256]{1,0:T(8,128)(2,1)S(1)}, bf16[384,256]{1,0:T(8,128)(2,1)S(1)}, u32[]{:S(2)}, u32[]{:S(2)}) %collective-permute-start.18) | collective-permute-done | bytes 196640 | tf_op jit(solution)/shard_map/ppermute | solution.py:17
  (29 shorter events, 8.8 us)
Async XLA Ops:
  0.6 26.0 %collective-permute-start.1 = (bf16[448,256]{1,0:T(8,128)(2,1)}, bf16[448,256]{1,0:T(8,128)(2,1)S(1)}, u32[]{:S(2)}, u32[]{:S(2)}) collective-permute-start(bf16[448,256]{1,0:T(8,128)(2,1)} %param.11), channel_id=1, source_target_pairs={{0,2},{1,258},{2,0},{3,256},{4,6},{5,262},{6,4},{7,260},{8,10},{9,... | collective-permute-start | bytes 688136 | tf_op jit(solution)/shard_map/ppermute | solution.py:32
  7.4 19.2 %collective-permute-start = (bf16[448,256]{1,0:T(8,128)(2,1)}, bf16[448,256]{1,0:T(8,128)(2,1)S(1)}, u32[]{:S(2)}, u32[]{:S(2)}) collective-permute-start(bf16[448,256]{1,0:T(8,128)(2,1)} %param.11), channel_id=1, source_target_pairs={{0,0},{1,256},{2,2},{3,258},{4,4},{5,260},{6,6},{7,262},{8,8},{9,2... | collective-permute-start | bytes 688136 | tf_op jit(solution)/shard_map/ppermute | solution.py:32
  15.7 50.2 %all-to-all-start = ((bf16[32,24,896]{2,1,0:T(8,128)(2,1)}), bf16[32,24,896]{2,1,0:T(8,128)(2,1)}, u32[]{:S(2)}, u32[]{:S(2)}) async-start(bf16[32,24,896]{2,1,0:T(8,128)(2,1)} %bitcast.7), calls=%async_computation | async-start | bytes 2752512 | tf_op jit(solution)/shard_map/all_to_all | solution.py:218
  26.7 17.2 %collective-permute-start.3 = (bf16[2,448,256]{2,1,0:T(8,128)(2,1)S(1)}, bf16[2,448,256]{2,1,0:T(8,128)(2,1)S(1)}, u32[]{:S(2)}, u32[]{:S(2)}) collective-permute-start(bf16[2,448,256]{2,1,0:T(8,128)(2,1)S(1)} %get-tuple-element.32), channel_id=1, source_target_pairs={{0,256},{64,320},{128,384},{192,448},{256,0},{320,64},{384,128},{4... | collective-permute-start | bytes 1376264 | tf_op jit(solution)/shard_map/ppermute | solution.py:21
  32.5 19.6 %collective-permute-start.2 = (bf16[2,448,256]{2,1,0:T(8,128)(2,1)S(1)}, bf16[2,448,256]{2,1,0:T(8,128)(2,1)S(1)}, u32[]{:S(2)}, u32[]{:S(2)}) collective-permute-start(bf16[2,448,256]{2,1,0:T(8,128)(2,1)S(1)} %get-tuple-element.32), channel_id=1, source_target_pairs={{0,128},{64,192},{128,0},{192,64},{256,384},{320,448},{384,256},{4... | collective-permute-start | bytes 1376264 | tf_op jit(solution)/shard_map/ppermute | solution.py:21
  35.0 17.1 %collective-permute-start.4 = (bf16[2,448,256]{2,1,0:T(8,128)(2,1)S(1)}, bf16[2,448,256]{2,1,0:T(8,128)(2,1)S(1)}, u32[]{:S(2)}, u32[]{:S(2)}) collective-permute-start(bf16[2,448,256]{2,1,0:T(8,128)(2,1)S(1)} %get-tuple-element.32), channel_id=1, source_target_pairs={{0,384},{64,448},{128,256},{192,320},{256,128},{320,192},{384,0},{... | collective-permute-start | bytes 1376264 | tf_op jit(solution)/shard_map/ppermute | solution.py:21
  52.1 2.3 %copy-start = (bf16[768,256]{1,0:T(8,128)(2,1)S(1)}, bf16[768,256]{1,0:T(8,128)(2,1)}, u32[]{:S(2)}) copy-start(bf16[768,256]{1,0:T(8,128)(2,1)} %param.9) | copy-start | bytes 1179652
  52.1 2.3 %copy-start.1 = (bf16[768,256]{1,0:T(8,128)(2,1)S(1)}, bf16[768,256]{1,0:T(8,128)(2,1)}, u32[]{:S(2)}) copy-start(bf16[768,256]{1,0:T(8,128)(2,1)} %param.10) | copy-start | bytes 1179652
  52.3 13.6 %collective-permute-start.5 = (bf16[4,2,448,256]{3,2,1,0:T(8,128)(2,1)S(1)}, bf16[4,2,448,256]{3,2,1,0:T(8,128)(2,1)}, u32[]{:S(2)}, u32[]{:S(2)}) collective-permute-start(bf16[4,2,448,256]{3,2,1,0:T(8,128)(2,1)S(1)} %pad_maximum_fusion.near_ref), channel_id=1, source_target_pairs={{0,64},{64,0},{128,192},{192,128},{256,320},{320,256},{384,448},{4... | collective-permute-start | bytes 5505032 | tf_op jit(solution)/shard_map/ppermute | solution.py:21
  55.8 10.1 %collective-permute-start.6 = (bf16[384,256]{1,0:T(8,128)(2,1)S(1)}, bf16[384,256]{1,0:T(8,128)(2,1)S(1)}, u32[]{:S(2)}, u32[]{:S(2)}) collective-permute-start(bf16[384,256]{1,0:T(8,128)(2,1)S(1)} %bitcast.43), channel_id=1, source_target_pairs={{0,1},{1,0},{2,3},{3,2},{4,5},{5,4},{6,7},{7,6},{8,9},{9,8},{10,11... | collective-permute-start | bytes 589832 | tf_op jit(solution)/shard_map/ppermute | solution.py:17
  58.2 19.5 %collective-permute-start.8 = (bf16[384,256]{1,0:T(8,128)(2,1)}, bf16[384,256]{1,0:T(8,128)(2,1)S(1)}, u32[]{:S(2)}, u32[]{:S(2)}) collective-permute-start(bf16[384,256]{1,0:T(8,128)(2,1)} %bitcast.17), channel_id=1, source_target_pairs={{0,3},{1,2},{2,1},{3,0},{4,7},{5,6},{6,5},{7,4},{8,11},{9,10},{10,... | collective-permute-start | bytes 589832 | tf_op jit(solution)/shard_map/ppermute | solution.py:17
  63.4 17.4 %collective-permute-start.7 = (bf16[384,256]{1,0:T(8,128)(2,1)}, bf16[384,256]{1,0:T(8,128)(2,1)S(1)}, u32[]{:S(2)}, u32[]{:S(2)}) collective-permute-start(bf16[384,256]{1,0:T(8,128)(2,1)} %bitcast.17), channel_id=1, source_target_pairs={{0,2},{1,3},{2,0},{3,1},{4,6},{5,7},{6,4},{7,5},{8,10},{9,11},{10,... | collective-permute-start | bytes 589832 | tf_op jit(solution)/shard_map/ppermute | solution.py:17
  84.3 5.7 %collective-permute-start.9 = (bf16[8,448,256]{2,1,0:T(8,128)(2,1)S(1)}, bf16[8,448,256]{2,1,0:T(8,128)(2,1)S(1)}, u32[]{:S(2)}, u32[]{:S(2)}) collective-permute-start(bf16[8,448,256]{2,1,0:T(8,128)(2,1)S(1)} %get-tuple-element.17), channel_id=1, source_target_pairs={{0,64},{64,0},{128,192},{192,128},{256,320},{320,256},{384,448},{4... | collective-permute-start | bytes 5505032 | tf_op jit(solution)/shard_map/ppermute | solution.py:21
  90.6 14.5 %collective-permute-start.10 = (bf16[2,448,256]{2,1,0:T(8,128)(2,1)S(1)}, bf16[2,448,256]{2,1,0:T(8,128)(2,1)S(1)}, u32[]{:S(2)}, u32[]{:S(2)}) collective-permute-start(bf16[2,448,256]{2,1,0:T(8,128)(2,1)S(1)} %get-tuple-element.29), channel_id=1, source_target_pairs={{0,128},{64,192},{128,0},{192,64},{256,384},{320,448},{384,256},{4... | collective-permute-start | bytes 1376264 | tf_op jit(solution)/shard_map/ppermute | solution.py:21
  94.0 15.4 %collective-permute-start.13 = (bf16[2,448,256]{2,1,0:T(8,128)(2,1)S(1)}, bf16[2,448,256]{2,1,0:T(8,128)(2,1)S(1)}, u32[]{:S(2)}, u32[]{:S(2)}) collective-permute-start(bf16[2,448,256]{2,1,0:T(8,128)(2,1)S(1)} %get-tuple-element.30), channel_id=1, source_target_pairs={{0,384},{64,448},{128,256},{192,320},{256,128},{320,192},{384,0},{... | collective-permute-start | bytes 1376264 | tf_op jit(solution)/shard_map/ppermute | solution.py:21
  109.7 8.4 %collective-permute-start.14 = (bf16[448,256]{1,0:T(8,128)(2,1)S(1)}, bf16[448,256]{1,0:T(8,128)(2,1)S(1)}, u32[]{:S(2)}, u32[]{:S(2)}) collective-permute-start(bf16[448,256]{1,0:T(8,128)(2,1)S(1)} %slice_bitcast_fusion), channel_id=1, source_target_pairs={{0,128},{64,192},{128,0},{192,64},{256,384},{320,448},{384,256},{4... | collective-permute-start | bytes 688136 | tf_op jit(solution)/shard_map/ppermute | solution.py:21
  111.6 9.6 %collective-permute-start.11 = (bf16[448,256]{1,0:T(8,128)(2,1)S(1)}, bf16[448,256]{1,0:T(8,128)(2,1)S(1)}, u32[]{:S(2)}, u32[]{:S(2)}) collective-permute-start(bf16[448,256]{1,0:T(8,128)(2,1)S(1)} %slice_bitcast_fusion.2), channel_id=1, source_target_pairs={{0,384},{64,448},{128,256},{192,320},{256,128},{320,192},{384,0},{... | collective-permute-start | bytes 688136 | tf_op jit(solution)/shard_map/ppermute | solution.py:21
  118.1 38.2 %collective-permute-start.15 = (bf16[448,256]{1,0:T(8,128)(2,1)S(1)}, bf16[448,256]{1,0:T(8,128)(2,1)S(1)}, u32[]{:S(2)}, u32[]{:S(2)}) collective-permute-start(bf16[448,256]{1,0:T(8,128)(2,1)S(1)} %fusion), channel_id=1, source_target_pairs={{0,2},{1,258},{2,0},{3,256},{4,6},{5,262},{6,4},{7,260},{8,10},{9,... | collective-permute-start | bytes 688136 | tf_op jit(solution)/shard_map/ppermute | solution.py:32
  121.3 35.0 %collective-permute-start.12 = (bf16[448,256]{1,0:T(8,128)(2,1)S(1)}, bf16[448,256]{1,0:T(8,128)(2,1)S(1)}, u32[]{:S(2)}, u32[]{:S(2)}) collective-permute-start(bf16[448,256]{1,0:T(8,128)(2,1)S(1)} %fusion.1), channel_id=1, source_target_pairs={{0,0},{1,256},{2,2},{3,258},{4,4},{5,260},{6,6},{7,262},{8,8},{9,2... | collective-permute-start | bytes 688136 | tf_op jit(solution)/shard_map/ppermute | solution.py:32
  132.6 10.2 %collective-permute-start.16 = (bf16[384,256]{1,0:T(8,128)(2,1)S(1)}, bf16[384,256]{1,0:T(8,128)(2,1)S(1)}, u32[]{:S(2)}, u32[]{:S(2)}) collective-permute-start(bf16[384,256]{1,0:T(8,128)(2,1)S(1)} %get-tuple-element.22), channel_id=1, source_target_pairs={{0,1},{1,0},{2,3},{3,2},{4,5},{5,4},{6,7},{7,6},{8,9},{9,8},{10,11... | collective-permute-start | bytes 589832 | tf_op jit(solution)/shard_map/ppermute | solution.py:17
  134.5 14.1 %collective-permute-start.17 = (bf16[384,256]{1,0:T(8,128)(2,1)S(1)}, bf16[384,256]{1,0:T(8,128)(2,1)S(1)}, u32[]{:S(2)}, u32[]{:S(2)}) collective-permute-start(bf16[384,256]{1,0:T(8,128)(2,1)S(1)} %get-tuple-element.23), channel_id=1, source_target_pairs={{0,2},{1,3},{2,0},{3,1},{4,6},{5,7},{6,4},{7,5},{8,10},{9,11},{10,... | collective-permute-start | bytes 589832 | tf_op jit(solution)/shard_map/ppermute | solution.py:17
  136.5 18.0 %collective-permute-start.18 = (bf16[384,256]{1,0:T(8,128)(2,1)S(1)}, bf16[384,256]{1,0:T(8,128)(2,1)S(1)}, u32[]{:S(2)}, u32[]{:S(2)}) collective-permute-start(bf16[384,256]{1,0:T(8,128)(2,1)S(1)} %get-tuple-element.24), channel_id=1, source_target_pairs={{0,3},{1,2},{2,1},{3,0},{4,7},{5,6},{6,5},{7,4},{8,11},{9,10},{10,... | collective-permute-start | bytes 589832 | tf_op jit(solution)/shard_map/ppermute | solution.py:17

commit v3 on v2

--- a/solution.py
+++ b/solution.py
@@ -21,14 +21,17 @@
     return lax.ppermute(value, "dp", [(i, i ^ mask) for i in range(lax.axis_size("dp"))])
 
 
-def swapped(value, flip):
+def swapped(value, flip, back):
     experts = lax.axis_size("expert")
     pairs = []
     for d in range(lax.axis_size("dp")):
         for s in range(experts):
-            to_dp = (s & 1) * 4 + (d & 3)
-            to_expert = (s & ~3) + (((s >> 1) & 1) ^ flip) * 2 + (d >> 2)
+            high = d >> 2
+            to_dp = ((s & 1) ^ high) * 4 + (d & 3)
+            to_expert = (s & ~3) + (((s >> 1) & 1) ^ flip) * 2 + high
             pairs.append((d * experts + s, to_dp * experts + to_expert))
+    if back:
+        pairs = [(target, source) for source, target in pairs]
     return lax.ppermute(value, ("dp", "expert"), pairs)
 
 
@@ -92,7 +95,7 @@
 
 
 def product_body(s_ref, gate_ref, up_ref, out_ref):
-    group = s_ref[4]
+    group = s_ref[3]
     for t in range(4):
         gate = gate_ref[:, t].astype(F32)
         value = (gate * jax.nn.sigmoid(gate) * up_ref[:, t].astype(F32)).astype(BF)
@@ -113,13 +116,20 @@
     )(scalars, gate, up)
 
 
+def picked(near, far, r1, r0):
+    return jnp.where(r1 == 0, jnp.where(r0 == 0, *near), jnp.where(r0 == 0, *far))
+
+
 def slot_of(e, r1, r0):
-    near, far = ((4, 0), (1, 5)) if e == 0 else ((6, 7), (3, 2))
-    return jnp.where(r1 == 0, jnp.where(r0 == 0, *near), jnp.where(r0 == 0, *far))
+    return picked(*(((4, 0), (1, 5)) if e == 0 else ((6, 7), (3, 2))), r1, r0)
+
+
+def gathered_slot(e, r1, r0):
+    return picked(*(((0, 2), (5, 4)) if e == 0 else ((1, 6), (7, 3))), r1, r0)
 
 
 def weight_body(s_ref, recv_ref, p0, p1, p2, p3, rows_ref, keep_ref, send_ref):
-    core, k, a1, a0 = s_ref[0], s_ref[1], s_ref[2], s_ref[3]
+    core, a1, a0 = s_ref[0], s_ref[1], s_ref[2]
     sources = recv_ref.shape[0]
     block = keep_ref.shape[1]
     for b in range(2):
@@ -131,7 +141,7 @@
                 rows_ref[b], piece[...], (((0,), (0,)), ((), ())), preferred_element_type=F32
             ).astype(BF)
             low, high = grad[:block], grad[block:]
-            place = slot_of(q >> 1, (q & 1) ^ k ^ a1, b ^ a0)
+            place = slot_of(q >> 1, (q & 1) ^ a1, b ^ a0)
             keep_ref[place] = jnp.where(core == 0, low, high)
             send_ref[place] = jnp.where(core == 0, high, low)
 
@@ -153,12 +163,12 @@
 
 
 def upstream_body(s_ref, rows_ref, near_ref, far_ref, *out_refs):
-    core, k, a1, a0 = s_ref[0], s_ref[1], s_ref[2], s_ref[3]
+    core, a1, a0 = s_ref[0], s_ref[1], s_ref[2]
     for q in range(4):
         total = None
         for b in range(2):
-            near = near_ref[((q & 1) ^ k ^ a1) * 2 + (b ^ a0), q >> 1]
-            far = far_ref[((q & 1) ^ k ^ a1) * 2 + (b ^ a0), q >> 1]
+            near = near_ref[gathered_slot(q >> 1, (q & 1) ^ a1, b ^ a0)]
+            far = far_ref[gathered_slot(q >> 1, (q & 1) ^ a1, b ^ a0)]
             low = jnp.where(core == 0, near, far)
             high = jnp.where(core == 0, far, near)
             part = jnp.dot(
@@ -183,7 +193,7 @@
 
 
 def finish_body(s_ref, gate_ref, up_ref, c0, c1, c2, c3, gate_out, up_out):
-    group = s_ref[4]
+    group = s_ref[3]
     for side in range(2):
         for t in range(2):
             left, right = ((c0, c1), (c2, c3))[side]
@@ -229,20 +239,23 @@
     dp = lax.axis_index("dp")
     place = lax.axis_index("expert")
     group = ((place >> 2) ^ (place >> 1)) & 1
-    scalars = jnp.stack([dp & 1, place & 1, dp >> 2, (dp >> 1) & 1, group]).astype(jnp.int32)
+    scalars = jnp.stack([dp & 1, dp >> 2, (dp >> 1) & 1, group]).astype(jnp.int32)
     gate4 = gate_pre.reshape(ys, 4, PART, columns)
     up4 = up_pre.reshape(ys, 4, PART, columns)
 
-    own = [swapped(down_weight, flip) for flip in range(2)]
+    own = [swapped(down_weight, flip, False) for flip in range(2)]
     sent = products(scalars, gate4, up4).reshape(2, -1, columns)
+    pieces = [sent[0]] + [expert_xor(sent[q >> 1], q) for q in (1, 2, 3)]
     slots = slot_buffer(cotangent, expert_ids, route_weights, experts)
     recv = dispatched(slots.reshape(devices // 2, PART, slots.shape[3]))
-    pieces = [sent[0]] + [expert_xor(sent[q >> 1], q) for q in (1, 2, 3)]
-    own = jnp.stack(own)
-    near = jnp.stack([own] + [dp_xor(own, mask) for mask in (2, 4, 6)])
+    own = [value[None] for value in own]
+    ahead, behind = dp_xor(own[0], 2), dp_xor(own[1], 6)
+    low = dp_xor(jnp.concatenate([own[0], ahead]), 6)
+    high = dp_xor(jnp.concatenate([own[1], behind]), 2)
+    near = jnp.concatenate(own + [ahead, behind, low, high])
     far = dp_xor(near, 1)
 
-    recv, near, far = lax.optimization_barrier((recv, near, far))
+    recv, near = lax.optimization_barrier((recv, near))
     rows, keep, send = weight_partial(scalars, recv, pieces, block)
     crossed = dp_xor(send, 1)
     parts = upstream_partial(scalars, rows, near, far)
@@ -253,7 +266,7 @@
     first = [added(summed[4:6], first[0]), added(summed[6:8], first[1])]
     second = [dp_xor(first[0][1], 6), dp_xor(first[1][1], 2)]
     kept = [added(first[e][0], second[e]) for e in range(2)]
-    weight_grad = added(swapped(kept[0], 0), swapped(kept[1], 1))
+    weight_grad = added(swapped(kept[0], 0, True), swapped(kept[1], 1, True))
     gate_grad, up_grad = finish(scalars, gate4, up4, parts)
     return (
         weight_grad,

time: 158 us -> 165 us (1.044)
  the two profiles are of different devices: /device:TPU:64 before, /device:TPU:96 now
where the time goes in v3:
time: 165 us
  starting transfers between devices  75.3 us (46%)
  waiting for transfers between devices  69.4 us (42%)
  Pallas kernels  11.9 us (7%)
  local copies, waits for them, and re-layouts  5.23 us (3%)
  other arithmetic  1.81 us (1%)
    ppermute x10, waiting for transfers between devices, dp_xor(): lax.ppermute(value, 'dp', [(i, i ^ mask) for i in range(lax.axis_size('dp...  30.3 us
    ppermute x4, waiting for transfers between devices, swapped(): return lax.ppermute(value, ('dp', 'expert'), pairs)  26.1 us
    ppermute x10, starting transfers between devices, dp_xor(): lax.ppermute(value, 'dp', [(i, i ^ mask) for i in range(lax.axis_size('dp...  24.3 us
    ppermute x6, starting transfers between devices, expert_xor(): lax.ppermute(value, 'expert', [(i, i ^ mask) for i in range(lax.axis_size...  20.2 us
    ppermute x4, starting transfers between devices, swapped(): return lax.ppermute(value, ('dp', 'expert'), pairs)  15.7 us
    all_to_all x1, starting transfers between devices, dispatched(): lax.all_to_all(slots, 'expert', split_axis=0, concat_axis=0, tiled=True,...  15.1 us
    ppermute x6, waiting for transfers between devices, expert_xor(): lax.ppermute(value, 'expert', [(i, i ^ mask) for i in range(lax.axis_size...  13 us
    unnamed x9, local copies, waits for them, and re-layouts  3.62 us
  transfers between devices with their start and end apart: 21, of which 11 were waited for; matrix products, arithmetic and copies ran while one was open for 4% of the time, Pallas kernels for 4%

profile of v3, /device:TPU:96, one launch (start us, length us, event | category | flops | bytes accessed | tf_op | source)
XLA Modules:
  0.0 164.5 jit_solution(4104831303673114094)
XLA Ops:
  0.6 3.2 %slots.1 = bf16[16,2,24,896]{3,2,1,0:T(8,128)(2,1)} custom-call(s32[1,128]{1,0:T(1,128)} %bitcast.51, f32[1,128]{1,0:T(1,128)} %bitcast.52, bf16[128,3584]{1,0:T(8,128)(2,1)} %cot_ref.1), custom_call_target="tpu_custom_call" | custom-call | flops 704643072 | bytes 1835008 | tf_op jit(solution)/shard_map/slots/pallas_call | solution.py:72
  3.8 15.1 %all-to-all-start = ((bf16[32,24,896]{2,1,0:T(8,128)(2,1)}), bf16[32,24,896]{2,1,0:T(8,128)(2,1)S(1)}, u32[]{:S(2)}, u32[]{:S(2)}) async-start(bf16[32,24,896]{2,1,0:T(8,128)(2,1)} %bitcast.6), calls=%async_computation | async-start | bytes 2752512 | tf_op jit(solution)/shard_map/all_to_all | solution.py:228
  18.9 4.9 %collective-permute-start = (bf16[448,256]{1,0:T(8,128)(2,1)}, bf16[448,256]{1,0:T(8,128)(2,1)S(1)}, u32[]{:S(2)}, u32[]{:S(2)}) collective-permute-start(bf16[448,256]{1,0:T(8,128)(2,1)} %param.11), channel_id=1, source_target_pairs={{0,0},{1,256},{2,2},{3,258},{4,4},{5,260},{6,6},{7,262},{8,8},{9,2... | collective-permute-start | bytes 688136 | tf_op jit(solution)/shard_map/ppermute | solution.py:35
  23.8 3.4 %collective-permute-start.1 = (bf16[448,256]{1,0:T(8,128)(2,1)}, bf16[448,256]{1,0:T(8,128)(2,1)S(1)}, u32[]{:S(2)}, u32[]{:S(2)}) collective-permute-start(bf16[448,256]{1,0:T(8,128)(2,1)} %param.11), channel_id=1, source_target_pairs={{0,2},{1,258},{2,0},{3,256},{4,6},{5,262},{6,4},{7,260},{8,10},{9,... | collective-permute-start | bytes 688136 | tf_op jit(solution)/shard_map/ppermute | solution.py:35
  28.7 4.3 %collective-permute-start.7 = (bf16[384,256]{1,0:T(8,128)(2,1)}, bf16[384,256]{1,0:T(8,128)(2,1)S(1)}, u32[]{:S(2)}, u32[]{:S(2)}) collective-permute-start(bf16[384,256]{1,0:T(8,128)(2,1)} %bitcast.12), channel_id=1, source_target_pairs={{0,2},{1,3},{2,0},{3,1},{4,6},{5,7},{6,4},{7,5},{8,10},{9,11},{10,... | collective-permute-start | bytes 589832 | tf_op jit(solution)/shard_map/ppermute | solution.py:17
  34.9 3.9 %collective-permute-start.6 = (bf16[384,256]{1,0:T(8,128)(2,1)S(1)}, bf16[384,256]{1,0:T(8,128)(2,1)S(1)}, u32[]{:S(2)}, u32[]{:S(2)}) collective-permute-start(bf16[384,256]{1,0:T(8,128)(2,1)S(1)} %bitcast.39), channel_id=1, source_target_pairs={{0,1},{1,0},{2,3},{3,2},{4,5},{5,4},{6,7},{7,6},{8,9},{9,8},{10,11... | collective-permute-start | bytes 589832 | tf_op jit(solution)/shard_map/ppermute | solution.py:17
  38.8 26.1 %collective-permute-done = bf16[448,256]{1,0:T(8,128)(2,1)S(1)} collective-permute-done((bf16[448,256]{1,0:T(8,128)(2,1)}, bf16[448,256]{1,0:T(8,128)(2,1)S(1)}, u32[]{:S(2)}, u32[]{:S(2)}) %collective-permute-start) | collective-permute-done | bytes 229408 | tf_op jit(solution)/shard_map/ppermute | solution.py:35
  64.9 3.4 %collective-permute-start.2 = (bf16[1,448,256]{2,1,0:T(8,128)(2,1)S(1)}, bf16[1,448,256]{2,1,0:T(8,128)(2,1)S(1)}, u32[]{:S(2)}, u32[]{:S(2)}) collective-permute-start(bf16[1,448,256]{2,1,0:T(8,128)(2,1)S(1)} %bitcast.47), channel_id=1, source_target_pairs={{0,128},{64,192},{128,0},{192,64},{256,384},{320,448},{384,256},{4... | collective-permute-start | bytes 688136 | tf_op jit(solution)/shard_map/ppermute | solution.py:21
  68.3 1.9 %collective-permute-start.3 = (bf16[1,448,256]{2,1,0:T(8,128)(2,1)S(1)}, bf16[1,448,256]{2,1,0:T(8,128)(2,1)S(1)}, u32[]{:S(2)}, u32[]{:S(2)}) collective-permute-start(bf16[1,448,256]{2,1,0:T(8,128)(2,1)S(1)} %bitcast.45), channel_id=1, source_target_pairs={{0,384},{64,448},{128,256},{192,320},{256,128},{320,192},{384,0},{... | collective-permute-start | bytes 688136 | tf_op jit(solution)/shard_map/ppermute | solution.py:21
  71.0 3.3 %collective-permute-done.2 = bf16[1,448,256]{2,1,0:T(8,128)(2,1)S(1)} collective-permute-done((bf16[1,448,256]{2,1,0:T(8,128)(2,1)S(1)}, bf16[1,448,256]{2,1,0:T(8,128)(2,1)S(1)}, u32[]{:S(2)}, u32[]{:S(2)}) %collective-permute-start.2) | collective-permute-done | bytes 229408 | tf_op jit(solution)/shard_map/ppermute | solution.py:21
  74.3 1.9 %collective-permute-start.4 = (bf16[2,448,256]{2,1,0:T(8,128)(2,1)S(1)}, bf16[2,448,256]{2,1,0:T(8,128)(2,1)S(1)}, u32[]{:S(2)}, u32[]{:S(2)}) collective-permute-start(bf16[2,448,256]{2,1,0:T(8,128)(2,1)S(1)} %pad_maximum_fusion), channel_id=1, source_target_pairs={{0,384},{64,448},{128,256},{192,320},{256,128},{320,192},{384,0},{... | collective-permute-start | bytes 1376264 | tf_op jit(solution)/shard_map/ppermute | solution.py:21
  76.2 2.4 %collective-permute-done.3 = bf16[1,448,256]{2,1,0:T(8,128)(2,1)S(1)} collective-permute-done((bf16[1,448,256]{2,1,0:T(8,128)(2,1)S(1)}, bf16[1,448,256]{2,1,0:T(8,128)(2,1)S(1)}, u32[]{:S(2)}, u32[]{:S(2)}) %collective-permute-start.3) | collective-permute-done | bytes 229408 | tf_op jit(solution)/shard_map/ppermute | solution.py:21
  78.6 1.9 %collective-permute-start.5 = (bf16[2,448,256]{2,1,0:T(8,128)(2,1)S(1)}, bf16[2,448,256]{2,1,0:T(8,128)(2,1)S(1)}, u32[]{:S(2)}, u32[]{:S(2)}) collective-permute-start(bf16[2,448,256]{2,1,0:T(8,128)(2,1)S(1)} %pad_maximum_fusion.1), channel_id=1, source_target_pairs={{0,128},{64,192},{128,0},{192,64},{256,384},{320,448},{384,256},{4... | collective-permute-start | bytes 1376264 | tf_op jit(solution)/shard_map/ppermute | solution.py:21
  82.6 6.2 %collective-permute-done.4 = bf16[2,448,256]{2,1,0:T(8,128)(2,1)S(1)} collective-permute-done((bf16[2,448,256]{2,1,0:T(8,128)(2,1)S(1)}, bf16[2,448,256]{2,1,0:T(8,128)(2,1)S(1)}, u32[]{:S(2)}, u32[]{:S(2)}) %collective-permute-start.4) | collective-permute-done | bytes 458784 | tf_op jit(solution)/shard_map/ppermute | solution.py:21
  89.6 2.0 %collective-permute-done.5 = bf16[2,448,256]{2,1,0:T(8,128)(2,1)S(1)} collective-permute-done((bf16[2,448,256]{2,1,0:T(8,128)(2,1)S(1)}, bf16[2,448,256]{2,1,0:T(8,128)(2,1)S(1)}, u32[]{:S(2)}, u32[]{:S(2)}) %collective-permute-start.5) | collective-permute-done | bytes 458784 | tf_op jit(solution)/shard_map/ppermute | solution.py:21
  92.5 2.8 %weight_partial.1 = (bf16[2,384,896]{2,1,0:T(8,128)(2,1)S(1)}, bf16[8,448,256]{2,1,0:T(8,128)(2,1)S(1)}, bf16[8,448,256]{2,1,0:T(8,128)(2,1)S(1)}) custom-call(s32[4]{0:T(128)S(1)} %pad_add_fusion.s_ref, bf16[32,24,896]{2,1,0:T(8,128)(2,1)S(1)} %all-to-all-done.recv_ref, bf16[384,256]{1,0:T(8,128)(2,1)S(1)} %bitcast.40, ...), custom_call_target="tpu_custom_call" | custom-call | flops 1409286144 | bytes 2752512 | tf_op jit(solution)/shard_map/weight_partial/pallas_call | solution.py:154
  97.2 2.4 %collective-permute-start.16 = (bf16[8,448,256]{2,1,0:T(8,128)(2,1)}, bf16[8,448,256]{2,1,0:T(8,128)(2,1)S(1)}, u32[]{:S(2)}, u32[]{:S(2)}) collective-permute-start(bf16[8,448,256]{2,1,0:T(8,128)(2,1)} %constant_dynamic-update-slice_fusion.near_ref), channel_id=1, source_target_pairs={{0,64},{64,0},{128,192},{192,128},{256,320},{320,256},{384,448},{4... | collective-permute-start | bytes 5505032 | tf_op jit(solution)/shard_map/ppermute | solution.py:21
  101.5 2.2 %collective-permute-start.10 = (bf16[2,448,256]{2,1,0:T(8,128)(2,1)S(1)}, bf16[2,448,256]{2,1,0:T(8,128)(2,1)S(1)}, u32[]{:S(2)}, u32[]{:S(2)}) collective-permute-start(bf16[2,448,256]{2,1,0:T(8,128)(2,1)S(1)} %get-tuple-element.27), channel_id=1, source_target_pairs={{0,128},{64,192},{128,0},{192,64},{256,384},{320,448},{384,256},{4... | collective-permute-start | bytes 1376264 | tf_op jit(solution)/shard_map/ppermute | solution.py:21
  103.7 3.4 %collective-permute-start.13 = (bf16[2,448,256]{2,1,0:T(8,128)(2,1)S(1)}, bf16[2,448,256]{2,1,0:T(8,128)(2,1)S(1)}, u32[]{:S(2)}, u32[]{:S(2)}) collective-permute-start(bf16[2,448,256]{2,1,0:T(8,128)(2,1)S(1)} %get-tuple-element.28), channel_id=1, source_target_pairs={{0,384},{64,448},{128,256},{192,320},{256,128},{320,192},{384,0},{... | collective-permute-start | bytes 1376264 | tf_op jit(solution)/shard_map/ppermute | solution.py:21
  107.1 8.9 %collective-permute-done.10 = bf16[2,448,256]{2,1,0:T(8,128)(2,1)S(1)} collective-permute-done((bf16[2,448,256]{2,1,0:T(8,128)(2,1)S(1)}, bf16[2,448,256]{2,1,0:T(8,128)(2,1)S(1)}, u32[]{:S(2)}, u32[]{:S(2)}) %collective-permute-start.10) | collective-permute-done | bytes 458784 | tf_op jit(solution)/shard_map/ppermute | solution.py:21
  116.0 3.1 %collective-permute-done.13 = bf16[2,448,256]{2,1,0:T(8,128)(2,1)S(1)} collective-permute-done((bf16[2,448,256]{2,1,0:T(8,128)(2,1)S(1)}, bf16[2,448,256]{2,1,0:T(8,128)(2,1)S(1)}, u32[]{:S(2)}, u32[]{:S(2)}) %collective-permute-start.13) | collective-permute-done | bytes 458784 | tf_op jit(solution)/shard_map/ppermute | solution.py:21
  119.4 2.4 %collective-permute-start.14 = (bf16[448,256]{1,0:T(8,128)(2,1)S(1)}, bf16[448,256]{1,0:T(8,128)(2,1)S(1)}, u32[]{:S(2)}, u32[]{:S(2)}) collective-permute-start(bf16[448,256]{1,0:T(8,128)(2,1)S(1)} %slice_bitcast_fusion), channel_id=1, source_target_pairs={{0,128},{64,192},{128,0},{192,64},{256,384},{320,448},{384,256},{4... | collective-permute-start | bytes 688136 | tf_op jit(solution)/shard_map/ppermute | solution.py:21
  121.9 2.9 %collective-permute-start.11 = (bf16[448,256]{1,0:T(8,128)(2,1)S(1)}, bf16[448,256]{1,0:T(8,128)(2,1)S(1)}, u32[]{:S(2)}, u32[]{:S(2)}) collective-permute-start(bf16[448,256]{1,0:T(8,128)(2,1)S(1)} %slice_bitcast_fusion.2), channel_id=1, source_target_pairs={{0,384},{64,448},{128,256},{192,320},{256,128},{320,192},{384,0},{... | collective-permute-start | bytes 688136 | tf_op jit(solution)/shard_map/ppermute | solution.py:21
  124.8 3.1 %collective-permute-done.14 = bf16[448,256]{1,0:T(8,128)(2,1)S(1)} collective-permute-done((bf16[448,256]{1,0:T(8,128)(2,1)S(1)}, bf16[448,256]{1,0:T(8,128)(2,1)S(1)}, u32[]{:S(2)}, u32[]{:S(2)}) %collective-permute-start.14) | collective-permute-done | bytes 229408 | tf_op jit(solution)/shard_map/ppermute | solution.py:21
  127.9 5.5 %collective-permute-start.15 = (bf16[448,256]{1,0:T(8,128)(2,1)S(1)}, bf16[448,256]{1,0:T(8,128)(2,1)S(1)}, u32[]{:S(2)}, u32[]{:S(2)}) collective-permute-start(bf16[448,256]{1,0:T(8,128)(2,1)S(1)} %fusion), channel_id=1, source_target_pairs={{2,0},{258,1},{0,2},{256,3},{6,4},{262,5},{4,6},{260,7},{10,8},{26... | collective-permute-start | bytes 688136 | tf_op jit(solution)/shard_map/ppermute | solution.py:35
  133.4 1.9 %collective-permute-start.12 = (bf16[448,256]{1,0:T(8,128)(2,1)S(1)}, bf16[448,256]{1,0:T(8,128)(2,1)S(1)}, u32[]{:S(2)}, u32[]{:S(2)}) collective-permute-start(bf16[448,256]{1,0:T(8,128)(2,1)S(1)} %fusion.1), channel_id=1, source_target_pairs={{0,0},{256,1},{2,2},{258,3},{4,4},{260,5},{6,6},{262,7},{8,8},{264... | collective-permute-start | bytes 688136 | tf_op jit(solution)/shard_map/ppermute | solution.py:35
  135.4 3.4 %upstream_partial.1 = (bf16[384,256]{1,0:T(8,128)(2,1)S(1)}, bf16[384,256]{1,0:T(8,128)(2,1)S(1)}, bf16[384,256]{1,0:T(8,128)(2,1)S(1)}, bf16[384,256]{1,0:T(8,128)(2,1)S(1)}) custom-call(s32[4]{0:T(128)S(1)} %pad_add_fusion.s_ref, bf16[2,384,896]{2,1,0:T(8,128)(2,1)S(1)} %get-tuple-element.17.rows_ref, ...), custom_call_target="tpu_custom_call" | custom-call | flops 1409286144 | bytes 2752512 | tf_op jit(solution)/shard_map/upstream_partial/pallas_call | solution.py:184
  138.8 2.1 %collective-permute-start.17 = (bf16[384,256]{1,0:T(8,128)(2,1)S(1)}, bf16[384,256]{1,0:T(8,128)(2,1)S(1)}, u32[]{:S(2)}, u32[]{:S(2)}) collective-permute-start(bf16[384,256]{1,0:T(8,128)(2,1)S(1)} %get-tuple-element.20), channel_id=1, source_target_pairs={{0,1},{1,0},{2,3},{3,2},{4,5},{5,4},{6,7},{7,6},{8,9},{9,8},{10,11... | collective-permute-start | bytes 589832 | tf_op jit(solution)/shard_map/ppermute | solution.py:17
  140.9 5.5 %collective-permute-start.18 = (bf16[384,256]{1,0:T(8,128)(2,1)S(1)}, bf16[384,256]{1,0:T(8,128)(2,1)S(1)}, u32[]{:S(2)}, u32[]{:S(2)}) collective-permute-start(bf16[384,256]{1,0:T(8,128)(2,1)S(1)} %get-tuple-element.21), channel_id=1, source_target_pairs={{0,2},{1,3},{2,0},{3,1},{4,6},{5,7},{6,4},{7,5},{8,10},{9,11},{10,... | collective-permute-start | bytes 589832 | tf_op jit(solution)/shard_map/ppermute | solution.py:17
  146.5 2.5 %collective-permute-start.19 = (bf16[384,256]{1,0:T(8,128)(2,1)S(1)}, bf16[384,256]{1,0:T(8,128)(2,1)S(1)}, u32[]{:S(2)}, u32[]{:S(2)}) collective-permute-start(bf16[384,256]{1,0:T(8,128)(2,1)S(1)} %get-tuple-element.22), channel_id=1, source_target_pairs={{0,3},{1,2},{2,1},{3,0},{4,7},{5,6},{6,5},{7,4},{8,11},{9,10},{10,... | collective-permute-start | bytes 589832 | tf_op jit(solution)/shard_map/ppermute | solution.py:17
  149.0 9.1 %collective-permute-done.18 = bf16[384,256]{1,0:T(8,128)(2,1)S(1)} collective-permute-done((bf16[384,256]{1,0:T(8,128)(2,1)S(1)}, bf16[384,256]{1,0:T(8,128)(2,1)S(1)}, u32[]{:S(2)}, u32[]{:S(2)}) %collective-permute-start.18) | collective-permute-done | bytes 196640 | tf_op jit(solution)/shard_map/ppermute | solution.py:17
  158.1 3.8 %collective-permute-done.19 = bf16[384,256]{1,0:T(8,128)(2,1)S(1)} collective-permute-done((bf16[384,256]{1,0:T(8,128)(2,1)S(1)}, bf16[384,256]{1,0:T(8,128)(2,1)S(1)}, u32[]{:S(2)}, u32[]{:S(2)}) %collective-permute-start.19) | collective-permute-done | bytes 196640 | tf_op jit(solution)/shard_map/ppermute | solution.py:17
  (37 shorter events, 14.8 us)
Async XLA Ops:
  3.8 23.5 %copy-start = (bf16[768,256]{1,0:T(8,128)(2,1)S(1)}, bf16[768,256]{1,0:T(8,128)(2,1)}, u32[]{:S(2)}) copy-start(bf16[768,256]{1,0:T(8,128)(2,1)} %param.9) | copy-start | bytes 1179652
  3.8 23.5 %copy-start.1 = (bf16[768,256]{1,0:T(8,128)(2,1)S(1)}, bf16[768,256]{1,0:T(8,128)(2,1)}, u32[]{:S(2)}) copy-start(bf16[768,256]{1,0:T(8,128)(2,1)} %param.10) | copy-start | bytes 1179652
  3.8 88.7 %all-to-all-start = ((bf16[32,24,896]{2,1,0:T(8,128)(2,1)}), bf16[32,24,896]{2,1,0:T(8,128)(2,1)S(1)}, u32[]{:S(2)}, u32[]{:S(2)}) async-start(bf16[32,24,896]{2,1,0:T(8,128)(2,1)} %bitcast.6), calls=%async_computation | async-start | bytes 2752512 | tf_op jit(solution)/shard_map/all_to_all | solution.py:228
  18.9 46.1 %collective-permute-start = (bf16[448,256]{1,0:T(8,128)(2,1)}, bf16[448,256]{1,0:T(8,128)(2,1)S(1)}, u32[]{:S(2)}, u32[]{:S(2)}) collective-permute-start(bf16[448,256]{1,0:T(8,128)(2,1)} %param.11), channel_id=1, source_target_pairs={{0,0},{1,256},{2,2},{3,258},{4,4},{5,260},{6,6},{7,262},{8,8},{9,2... | collective-permute-start | bytes 688136 | tf_op jit(solution)/shard_map/ppermute | solution.py:35
  23.8 44.5 %collective-permute-start.1 = (bf16[448,256]{1,0:T(8,128)(2,1)}, bf16[448,256]{1,0:T(8,128)(2,1)S(1)}, u32[]{:S(2)}, u32[]{:S(2)}) collective-permute-start(bf16[448,256]{1,0:T(8,128)(2,1)} %param.11), channel_id=1, source_target_pairs={{0,2},{1,258},{2,0},{3,256},{4,6},{5,262},{6,4},{7,260},{8,10},{9,... | collective-permute-start | bytes 688136 | tf_op jit(solution)/shard_map/ppermute | solution.py:35
  28.7 63.8 %collective-permute-start.7 = (bf16[384,256]{1,0:T(8,128)(2,1)}, bf16[384,256]{1,0:T(8,128)(2,1)S(1)}, u32[]{:S(2)}, u32[]{:S(2)}) collective-permute-start(bf16[384,256]{1,0:T(8,128)(2,1)} %bitcast.12), channel_id=1, source_target_pairs={{0,2},{1,3},{2,0},{3,1},{4,6},{5,7},{6,4},{7,5},{8,10},{9,11},{10,... | collective-permute-start | bytes 589832 | tf_op jit(solution)/shard_map/ppermute | solution.py:17
  33.0 59.5 %collective-permute-start.8 = (bf16[384,256]{1,0:T(8,128)(2,1)}, bf16[384,256]{1,0:T(8,128)(2,1)S(1)}, u32[]{:S(2)}, u32[]{:S(2)}) collective-permute-start(bf16[384,256]{1,0:T(8,128)(2,1)} %bitcast.12), channel_id=1, source_target_pairs={{0,3},{1,2},{2,1},{3,0},{4,7},{5,6},{6,5},{7,4},{8,11},{9,10},{10,... | collective-permute-start | bytes 589832 | tf_op jit(solution)/shard_map/ppermute | solution.py:17
  34.9 57.6 %collective-permute-start.6 = (bf16[384,256]{1,0:T(8,128)(2,1)S(1)}, bf16[384,256]{1,0:T(8,128)(2,1)S(1)}, u32[]{:S(2)}, u32[]{:S(2)}) collective-permute-start(bf16[384,256]{1,0:T(8,128)(2,1)S(1)} %bitcast.39), channel_id=1, source_target_pairs={{0,1},{1,0},{2,3},{3,2},{4,5},{5,4},{6,7},{7,6},{8,9},{9,8},{10,11... | collective-permute-start | bytes 589832 | tf_op jit(solution)/shard_map/ppermute | solution.py:17
  64.9 9.3 %collective-permute-start.2 = (bf16[1,448,256]{2,1,0:T(8,128)(2,1)S(1)}, bf16[1,448,256]{2,1,0:T(8,128)(2,1)S(1)}, u32[]{:S(2)}, u32[]{:S(2)}) collective-permute-start(bf16[1,448,256]{2,1,0:T(8,128)(2,1)S(1)} %bitcast.47), channel_id=1, source_target_pairs={{0,128},{64,192},{128,0},{192,64},{256,384},{320,448},{384,256},{4... | collective-permute-start | bytes 688136 | tf_op jit(solution)/shard_map/ppermute | solution.py:21
  68.3 10.2 %collective-permute-start.3 = (bf16[1,448,256]{2,1,0:T(8,128)(2,1)S(1)}, bf16[1,448,256]{2,1,0:T(8,128)(2,1)S(1)}, u32[]{:S(2)}, u32[]{:S(2)}) collective-permute-start(bf16[1,448,256]{2,1,0:T(8,128)(2,1)S(1)} %bitcast.45), channel_id=1, source_target_pairs={{0,384},{64,448},{128,256},{192,320},{256,128},{320,192},{384,0},{... | collective-permute-start | bytes 688136 | tf_op jit(solution)/shard_map/ppermute | solution.py:21
  74.3 14.6 %collective-permute-start.4 = (bf16[2,448,256]{2,1,0:T(8,128)(2,1)S(1)}, bf16[2,448,256]{2,1,0:T(8,128)(2,1)S(1)}, u32[]{:S(2)}, u32[]{:S(2)}) collective-permute-start(bf16[2,448,256]{2,1,0:T(8,128)(2,1)S(1)} %pad_maximum_fusion), channel_id=1, source_target_pairs={{0,384},{64,448},{128,256},{192,320},{256,128},{320,192},{384,0},{... | collective-permute-start | bytes 1376264 | tf_op jit(solution)/shard_map/ppermute | solution.py:21
  78.6 13.1 %collective-permute-start.5 = (bf16[2,448,256]{2,1,0:T(8,128)(2,1)S(1)}, bf16[2,448,256]{2,1,0:T(8,128)(2,1)S(1)}, u32[]{:S(2)}, u32[]{:S(2)}) collective-permute-start(bf16[2,448,256]{2,1,0:T(8,128)(2,1)S(1)} %pad_maximum_fusion.1), channel_id=1, source_target_pairs={{0,128},{64,192},{128,0},{192,64},{256,384},{320,448},{384,256},{4... | collective-permute-start | bytes 1376264 | tf_op jit(solution)/shard_map/ppermute | solution.py:21
  95.3 5.7 %collective-permute-start.9 = (bf16[8,448,256]{2,1,0:T(8,128)(2,1)S(1)}, bf16[8,448,256]{2,1,0:T(8,128)(2,1)S(1)}, u32[]{:S(2)}, u32[]{:S(2)}) collective-permute-start(bf16[8,448,256]{2,1,0:T(8,128)(2,1)S(1)} %get-tuple-element.16), channel_id=1, source_target_pairs={{0,64},{64,0},{128,192},{192,128},{256,320},{320,256},{384,448},{4... | collective-permute-start | bytes 5505032 | tf_op jit(solution)/shard_map/ppermute | solution.py:21
  97.2 38.2 %collective-permute-start.16 = (bf16[8,448,256]{2,1,0:T(8,128)(2,1)}, bf16[8,448,256]{2,1,0:T(8,128)(2,1)S(1)}, u32[]{:S(2)}, u32[]{:S(2)}) collective-permute-start(bf16[8,448,256]{2,1,0:T(8,128)(2,1)} %constant_dynamic-update-slice_fusion.near_ref), channel_id=1, source_target_pairs={{0,64},{64,0},{128,192},{192,128},{256,320},{320,256},{384,448},{4... | collective-permute-start | bytes 5505032 | tf_op jit(solution)/shard_map/ppermute | solution.py:21
  101.5 14.5 %collective-permute-start.10 = (bf16[2,448,256]{2,1,0:T(8,128)(2,1)S(1)}, bf16[2,448,256]{2,1,0:T(8,128)(2,1)S(1)}, u32[]{:S(2)}, u32[]{:S(2)}) collective-permute-start(bf16[2,448,256]{2,1,0:T(8,128)(2,1)S(1)} %get-tuple-element.27), channel_id=1, source_target_pairs={{0,128},{64,192},{128,0},{192,64},{256,384},{320,448},{384,256},{4... | collective-permute-start | bytes 1376264 | tf_op jit(solution)/shard_map/ppermute | solution.py:21
  103.7 15.4 %collective-permute-start.13 = (bf16[2,448,256]{2,1,0:T(8,128)(2,1)S(1)}, bf16[2,448,256]{2,1,0:T(8,128)(2,1)S(1)}, u32[]{:S(2)}, u32[]{:S(2)}) collective-permute-start(bf16[2,448,256]{2,1,0:T(8,128)(2,1)S(1)} %get-tuple-element.28), channel_id=1, source_target_pairs={{0,384},{64,448},{128,256},{192,320},{256,128},{320,192},{384,0},{... | collective-permute-start | bytes 1376264 | tf_op jit(solution)/shard_map/ppermute | solution.py:21
  119.4 8.4 %collective-permute-start.14 = (bf16[448,256]{1,0:T(8,128)(2,1)S(1)}, bf16[448,256]{1,0:T(8,128)(2,1)S(1)}, u32[]{:S(2)}, u32[]{:S(2)}) collective-permute-start(bf16[448,256]{1,0:T(8,128)(2,1)S(1)} %slice_bitcast_fusion), channel_id=1, source_target_pairs={{0,128},{64,192},{128,0},{192,64},{256,384},{320,448},{384,256},{4... | collective-permute-start | bytes 688136 | tf_op jit(solution)/shard_map/ppermute | solution.py:21
  121.9 11.5 %collective-permute-start.11 = (bf16[448,256]{1,0:T(8,128)(2,1)S(1)}, bf16[448,256]{1,0:T(8,128)(2,1)S(1)}, u32[]{:S(2)}, u32[]{:S(2)}) collective-permute-start(bf16[448,256]{1,0:T(8,128)(2,1)S(1)} %slice_bitcast_fusion.2), channel_id=1, source_target_pairs={{0,384},{64,448},{128,256},{192,320},{256,128},{320,192},{384,0},{... | collective-permute-start | bytes 688136 | tf_op jit(solution)/shard_map/ppermute | solution.py:21
  127.9 35.9 %collective-permute-start.15 = (bf16[448,256]{1,0:T(8,128)(2,1)S(1)}, bf16[448,256]{1,0:T(8,128)(2,1)S(1)}, u32[]{:S(2)}, u32[]{:S(2)}) collective-permute-start(bf16[448,256]{1,0:T(8,128)(2,1)S(1)} %fusion), channel_id=1, source_target_pairs={{2,0},{258,1},{0,2},{256,3},{6,4},{262,5},{4,6},{260,7},{10,8},{26... | collective-permute-start | bytes 688136 | tf_op jit(solution)/shard_map/ppermute | solution.py:35
  133.4 30.3 %collective-permute-start.12 = (bf16[448,256]{1,0:T(8,128)(2,1)S(1)}, bf16[448,256]{1,0:T(8,128)(2,1)S(1)}, u32[]{:S(2)}, u32[]{:S(2)}) collective-permute-start(bf16[448,256]{1,0:T(8,128)(2,1)S(1)} %fusion.1), channel_id=1, source_target_pairs={{0,0},{256,1},{2,2},{258,3},{4,4},{260,5},{6,6},{262,7},{8,8},{264... | collective-permute-start | bytes 688136 | tf_op jit(solution)/shard_map/ppermute | solution.py:35
  138.8 10.1 %collective-permute-start.17 = (bf16[384,256]{1,0:T(8,128)(2,1)S(1)}, bf16[384,256]{1,0:T(8,128)(2,1)S(1)}, u32[]{:S(2)}, u32[]{:S(2)}) collective-permute-start(bf16[384,256]{1,0:T(8,128)(2,1)S(1)} %get-tuple-element.20), channel_id=1, source_target_pairs={{0,1},{1,0},{2,3},{3,2},{4,5},{5,4},{6,7},{7,6},{8,9},{9,8},{10,11... | collective-permute-start | bytes 589832 | tf_op jit(solution)/shard_map/ppermute | solution.py:17
  140.9 17.1 %collective-permute-start.18 = (bf16[384,256]{1,0:T(8,128)(2,1)S(1)}, bf16[384,256]{1,0:T(8,128)(2,1)S(1)}, u32[]{:S(2)}, u32[]{:S(2)}) collective-permute-start(bf16[384,256]{1,0:T(8,128)(2,1)S(1)} %get-tuple-element.21), channel_id=1, source_target_pairs={{0,2},{1,3},{2,0},{3,1},{4,6},{5,7},{6,4},{7,5},{8,10},{9,11},{10,... | collective-permute-start | bytes 589832 | tf_op jit(solution)/shard_map/ppermute | solution.py:17
  146.5 15.4 %collective-permute-start.19 = (bf16[384,256]{1,0:T(8,128)(2,1)S(1)}, bf16[384,256]{1,0:T(8,128)(2,1)S(1)}, u32[]{:S(2)}, u32[]{:S(2)}) collective-permute-start(bf16[384,256]{1,0:T(8,128)(2,1)S(1)} %get-tuple-element.22), channel_id=1, source_target_pairs={{0,3},{1,2},{2,1},{3,0},{4,7},{5,6},{6,5},{7,4},{8,11},{9,10},{10,... | collective-permute-start | bytes 589832 | tf_op jit(solution)/shard_map/ppermute | solution.py:17

commit v4 on v3

--- a/solution.py
+++ b/solution.py
@@ -27,7 +27,7 @@
     for d in range(lax.axis_size("dp")):
         for s in range(experts):
             high = d >> 2
-            to_dp = ((s & 1) ^ high) * 4 + (d & 3)
+            to_dp = ((s & 1) ^ high ^ (d & 1)) * 4 + (d & 3)
             to_expert = (s & ~3) + (((s >> 1) & 1) ^ flip) * 2 + high
             pairs.append((d * experts + s, to_dp * experts + to_expert))
     if back:
@@ -94,13 +94,15 @@
     )
 
 
-def product_body(s_ref, gate_ref, up_ref, out_ref):
-    group = s_ref[3]
-    for t in range(4):
-        gate = gate_ref[:, t].astype(F32)
-        value = (gate * jax.nn.sigmoid(gate) * up_ref[:, t].astype(F32)).astype(BF)
-        side = group ^ (0 if t in (0, 3) else 1)
-        out_ref[side, :, t >> 1] = value
+def product_body(s_ref, gate_ref, up_ref, mine_ref, theirs_ref):
+    outer = s_ref[3] == 0
+    for t, other in ((0, 1), (3, 2)):
+        values = []
+        for at in (t, other):
+            gate = gate_ref[:, at].astype(F32)
+            values.append(gate * jax.nn.sigmoid(gate) * up_ref[:, at].astype(F32))
+        mine_ref[:, t >> 1] = jnp.where(outer, *values).astype(BF)
+        theirs_ref[:, t >> 1] = jnp.where(outer, *values[::-1]).astype(BF)
 
 
 def products(scalars, gate, up):
@@ -108,8 +110,8 @@
     return pl.pallas_call(
         product_body,
         in_specs=[SCALARS, WHOLE, WHOLE],
-        out_specs=WHOLE,
-        out_shape=jax.ShapeDtypeStruct((2, ys, 2, part, columns), BF),
+        out_specs=[WHOLE] * 2,
+        out_shape=[jax.ShapeDtypeStruct((ys, 2, part, columns), BF)] * 2,
         compiler_params=PARAMS,
         cost_estimate=cost(gate.size * 200, gate.size * 8),
         name="products",
@@ -141,9 +143,10 @@
                 rows_ref[b], piece[...], (((0,), (0,)), ((), ())), preferred_element_type=F32
             ).astype(BF)
             low, high = grad[:block], grad[block:]
-            place = slot_of(q >> 1, (q & 1) ^ a1, b ^ a0)
-            keep_ref[place] = jnp.where(core == 0, low, high)
-            send_ref[place] = jnp.where(core == 0, high, low)
+            kept = slot_of(q >> 1, (q & 1) ^ core ^ a1, b ^ a0)
+            sent = slot_of(q >> 1, (q & 1) ^ core ^ a1 ^ 1, b ^ a0)
+            keep_ref[kept] = jnp.where(core == 0, low, high)
+            send_ref[sent] = jnp.where(core == 0, high, low)
 
 
 def weight_partial(scalars, recv, pieces, block):
@@ -167,8 +170,8 @@
     for q in range(4):
         total = None
         for b in range(2):
-            near = near_ref[gathered_slot(q >> 1, (q & 1) ^ a1, b ^ a0)]
-            far = far_ref[gathered_slot(q >> 1, (q & 1) ^ a1, b ^ a0)]
+            near = near_ref[gathered_slot(q >> 1, (q & 1) ^ core ^ a1, b ^ a0)]
+            far = far_ref[gathered_slot(q >> 1, (q & 1) ^ core ^ a1 ^ 1, b ^ a0)]
             low = jnp.where(core == 0, near, far)
             high = jnp.where(core == 0, far, near)
             part = jnp.dot(
@@ -244,7 +247,7 @@
     up4 = up_pre.reshape(ys, 4, PART, columns)
 
     own = [swapped(down_weight, flip, False) for flip in range(2)]
-    sent = products(scalars, gate4, up4).reshape(2, -1, columns)
+    sent = [rows.reshape(-1, columns) for rows in products(scalars, gate4, up4)]
     pieces = [sent[0]] + [expert_xor(sent[q >> 1], q) for q in (1, 2, 3)]
     slots = slot_buffer(cotangent, expert_ids, route_weights, experts)
     recv = dispatched(slots.reshape(devices // 2, PART, slots.shape[3]))

time: 165 us -> 167 us (1.012)
  starting transfers between devices: 75.3 us -> 77.5 us
  waiting for transfers between devices: 69.4 us -> 67.4 us
    ppermute x10, waiting for transfers between devices: 30.3 us -> 25.7 us  [dp_xor(): lax.ppermute(value, 'dp', [(i, i ^ mask) for i in range(lax.axis_size('dp...]
    ppermute x10, starting transfers between devices: 24.3 us -> 27.3 us  [dp_xor(): lax.ppermute(value, 'dp', [(i, i ^ mask) for i in range(lax.axis_size('dp...]
where the time goes in v4:
time: 167 us; the launch traced here: 166 us
  starting transfers between devices  77.5 us (46%)
  waiting for transfers between devices  67.4 us (40%)
  Pallas kernels  11.9 us (7%)
  local copies, waits for them, and re-layouts  5.47 us (3%)
  other arithmetic  2.75 us (2%)
    ppermute x10, starting transfers between devices, dp_xor(): lax.ppermute(value, 'dp', [(i, i ^ mask) for i in range(lax.axis_size('dp...  27.3 us
    ppermute x4, waiting for transfers between devices, swapped(): return lax.ppermute(value, ('dp', 'expert'), pairs)  27.1 us
    ppermute x10, waiting for transfers between devices, dp_xor(): lax.ppermute(value, 'dp', [(i, i ^ mask) for i in range(lax.axis_size('dp...  25.7 us
    ppermute x6, starting transfers between devices, expert_xor(): lax.ppermute(value, 'expert', [(i, i ^ mask) for i in range(lax.axis_size...  19.3 us
    ppermute x4, starting transfers between devices, swapped(): return lax.ppermute(value, ('dp', 'expert'), pairs)  15.8 us
    all_to_all x1, starting transfers between devices, dispatched(): lax.all_to_all(slots, 'expert', split_axis=0, concat_axis=0, tiled=True,...  15.1 us
    ppermute x6, waiting for transfers between devices, expert_xor(): lax.ppermute(value, 'expert', [(i, i ^ mask) for i in range(lax.axis_size...  14.5 us
    unnamed x9, local copies, waits for them, and re-layouts  4.56 us
  transfers between devices with their start and end apart: 21, of which 11 were waited for; matrix products, arithmetic and copies ran while one was open for 4% of the time, Pallas kernels for 4%

profile of v4, /device:TPU:96, one launch (start us, length us, event | category | flops | bytes accessed | tf_op | source)
XLA Modules:
  0.0 165.9 jit_solution(13643139327227020218)
XLA Ops:
  0.6 3.2 %slots.1 = bf16[16,2,24,896]{3,2,1,0:T(8,128)(2,1)} custom-call(s32[1,128]{1,0:T(1,128)} %bitcast.51, f32[1,128]{1,0:T(1,128)} %bitcast.52, bf16[128,3584]{1,0:T(8,128)(2,1)} %cot_ref.1), custom_call_target="tpu_custom_call" | custom-call | flops 704643072 | bytes 1835008 | tf_op jit(solution)/shard_map/slots/pallas_call | solution.py:72
  3.8 15.1 %all-to-all-start = ((bf16[32,24,896]{2,1,0:T(8,128)(2,1)}), bf16[32,24,896]{2,1,0:T(8,128)(2,1)S(1)}, u32[]{:S(2)}, u32[]{:S(2)}) async-start(bf16[32,24,896]{2,1,0:T(8,128)(2,1)} %bitcast.6), calls=%async_computation | async-start | bytes 2752512 | tf_op jit(solution)/shard_map/all_to_all | solution.py:231
  18.9 4.9 %collective-permute-start = (bf16[448,256]{1,0:T(8,128)(2,1)}, bf16[448,256]{1,0:T(8,128)(2,1)}, u32[]{:S(2)}, u32[]{:S(2)}) collective-permute-start(bf16[448,256]{1,0:T(8,128)(2,1)} %param.11), channel_id=1, source_target_pairs={{0,0},{1,256},{2,2},{3,258},{4,4},{5,260},{6,6},{7,262},{8,8},{9,2... | collective-permute-start | bytes 688136 | tf_op jit(solution)/shard_map/ppermute | solution.py:35
  23.8 3.4 %collective-permute-start.1 = (bf16[448,256]{1,0:T(8,128)(2,1)}, bf16[448,256]{1,0:T(8,128)(2,1)S(1)}, u32[]{:S(2)}, u32[]{:S(2)}) collective-permute-start(bf16[448,256]{1,0:T(8,128)(2,1)} %param.11), channel_id=1, source_target_pairs={{0,2},{1,258},{2,0},{3,256},{4,6},{5,262},{6,4},{7,260},{8,10},{9,... | collective-permute-start | bytes 688136 | tf_op jit(solution)/shard_map/ppermute | solution.py:35
  28.1 4.3 %collective-permute-start.7 = (bf16[384,256]{1,0:T(8,128)(2,1)S(1)}, bf16[384,256]{1,0:T(8,128)(2,1)S(1)}, u32[]{:S(2)}, u32[]{:S(2)}) collective-permute-start(bf16[384,256]{1,0:T(8,128)(2,1)S(1)} %bitcast.45), channel_id=1, source_target_pairs={{0,2},{1,3},{2,0},{3,1},{4,6},{5,7},{6,4},{7,5},{8,10},{9,11},{10,... | collective-permute-start | bytes 589832 | tf_op jit(solution)/shard_map/ppermute | solution.py:17
  32.4 1.9 %collective-permute-start.8 = (bf16[384,256]{1,0:T(8,128)(2,1)S(1)}, bf16[384,256]{1,0:T(8,128)(2,1)S(1)}, u32[]{:S(2)}, u32[]{:S(2)}) collective-permute-start(bf16[384,256]{1,0:T(8,128)(2,1)S(1)} %bitcast.46), channel_id=1, source_target_pairs={{0,3},{1,2},{2,1},{3,0},{4,7},{5,6},{6,5},{7,4},{8,11},{9,10},{10,... | collective-permute-start | bytes 589832 | tf_op jit(solution)/shard_map/ppermute | solution.py:17
  34.3 3.9 %collective-permute-start.6 = (bf16[384,256]{1,0:T(8,128)(2,1)S(1)}, bf16[384,256]{1,0:T(8,128)(2,1)S(1)}, u32[]{:S(2)}, u32[]{:S(2)}) collective-permute-start(bf16[384,256]{1,0:T(8,128)(2,1)S(1)} %bitcast.43), channel_id=1, source_target_pairs={{0,1},{1,0},{2,3},{3,2},{4,5},{5,4},{6,7},{7,6},{8,9},{9,8},{10,11... | collective-permute-start | bytes 589832 | tf_op jit(solution)/shard_map/ppermute | solution.py:17
  38.2 27.1 %collective-permute-done = bf16[448,256]{1,0:T(8,128)(2,1)} collective-permute-done((bf16[448,256]{1,0:T(8,128)(2,1)}, bf16[448,256]{1,0:T(8,128)(2,1)}, u32[]{:S(2)}, u32[]{:S(2)}) %collective-permute-start) | collective-permute-done | bytes 229408 | tf_op jit(solution)/shard_map/ppermute | solution.py:35
  65.3 3.4 %collective-permute-start.2 = (bf16[1,448,256]{2,1,0:T(8,128)(2,1)}, bf16[1,448,256]{2,1,0:T(8,128)(2,1)S(1)}, u32[]{:S(2)}, u32[]{:S(2)}) collective-permute-start(bf16[1,448,256]{2,1,0:T(8,128)(2,1)} %bitcast.7), channel_id=1, source_target_pairs={{0,128},{64,192},{128,0},{192,64},{256,384},{320,448},{384,256},{4... | collective-permute-start | bytes 688136 | tf_op jit(solution)/shard_map/ppermute | solution.py:21
  68.7 1.9 %collective-permute-start.3 = (bf16[1,448,256]{2,1,0:T(8,128)(2,1)S(1)}, bf16[1,448,256]{2,1,0:T(8,128)(2,1)S(1)}, u32[]{:S(2)}, u32[]{:S(2)}) collective-permute-start(bf16[1,448,256]{2,1,0:T(8,128)(2,1)S(1)} %bitcast.47), channel_id=1, source_target_pairs={{0,384},{64,448},{128,256},{192,320},{256,128},{320,192},{384,0},{... | collective-permute-start | bytes 688136 | tf_op jit(solution)/shard_map/ppermute | solution.py:21
  72.3 2.5 %collective-permute-done.2 = bf16[1,448,256]{2,1,0:T(8,128)(2,1)S(1)} collective-permute-done((bf16[1,448,256]{2,1,0:T(8,128)(2,1)}, bf16[1,448,256]{2,1,0:T(8,128)(2,1)S(1)}, u32[]{:S(2)}, u32[]{:S(2)}) %collective-permute-start.2) | collective-permute-done | bytes 229408 | tf_op jit(solution)/shard_map/ppermute | solution.py:21
  75.8 2.6 %collective-permute-start.4 = (bf16[2,448,256]{2,1,0:T(8,128)(2,1)S(1)}, bf16[2,448,256]{2,1,0:T(8,128)(2,1)S(1)}, u32[]{:S(2)}, u32[]{:S(2)}) collective-permute-start(bf16[2,448,256]{2,1,0:T(8,128)(2,1)S(1)} %pad_maximum_fusion), channel_id=1, source_target_pairs={{0,384},{64,448},{128,256},{192,320},{256,128},{320,192},{384,0},{... | collective-permute-start | bytes 1376264 | tf_op jit(solution)/shard_map/ppermute | solution.py:21
  79.0 2.2 %collective-permute-start.5 = (bf16[2,448,256]{2,1,0:T(8,128)(2,1)S(1)}, bf16[2,448,256]{2,1,0:T(8,128)(2,1)S(1)}, u32[]{:S(2)}, u32[]{:S(2)}) collective-permute-start(bf16[2,448,256]{2,1,0:T(8,128)(2,1)S(1)} %pad_maximum_fusion.1), channel_id=1, source_target_pairs={{0,128},{64,192},{128,0},{192,64},{256,384},{320,448},{384,256},{4... | collective-permute-start | bytes 1376264 | tf_op jit(solution)/shard_map/ppermute | solution.py:21
  83.3 7.1 %collective-permute-done.4 = bf16[2,448,256]{2,1,0:T(8,128)(2,1)S(1)} collective-permute-done((bf16[2,448,256]{2,1,0:T(8,128)(2,1)S(1)}, bf16[2,448,256]{2,1,0:T(8,128)(2,1)S(1)}, u32[]{:S(2)}, u32[]{:S(2)}) %collective-permute-start.4) | collective-permute-done | bytes 458784 | tf_op jit(solution)/shard_map/ppermute | solution.py:21
  92.9 2.8 %weight_partial.1 = (bf16[2,384,896]{2,1,0:T(8,128)(2,1)S(1)}, bf16[8,448,256]{2,1,0:T(8,128)(2,1)S(1)}, bf16[8,448,256]{2,1,0:T(8,128)(2,1)S(1)}) custom-call(s32[4]{0:T(128)S(1)} %pad_add_fusion.s_ref, bf16[32,24,896]{2,1,0:T(8,128)(2,1)S(1)} %all-to-all-done.recv_ref, bf16[384,256]{1,0:T(8,128)(2,1)S(1)} %bitcast.44, ...), custom_call_target="tpu_custom_call" | custom-call | flops 1409286144 | bytes 2752512 | tf_op jit(solution)/shard_map/weight_partial/pallas_call | solution.py:157
  95.7 1.9 %collective-permute-start.9 = (bf16[8,448,256]{2,1,0:T(8,128)(2,1)S(1)}, bf16[8,448,256]{2,1,0:T(8,128)(2,1)S(1)}, u32[]{:S(2)}, u32[]{:S(2)}) collective-permute-start(bf16[8,448,256]{2,1,0:T(8,128)(2,1)S(1)} %get-tuple-element.20), channel_id=1, source_target_pairs={{0,64},{64,0},{128,192},{192,128},{256,320},{320,256},{384,448},{4... | collective-permute-start | bytes 5505032 | tf_op jit(solution)/shard_map/ppermute | solution.py:21
  97.6 2.4 %collective-permute-start.16 = (bf16[8,448,256]{2,1,0:T(8,128)(2,1)}, bf16[8,448,256]{2,1,0:T(8,128)(2,1)S(1)}, u32[]{:S(2)}, u32[]{:S(2)}) collective-permute-start(bf16[8,448,256]{2,1,0:T(8,128)(2,1)} %constant_dynamic-update-slice_fusion.near_ref), channel_id=1, source_target_pairs={{0,64},{64,0},{128,192},{192,128},{256,320},{320,256},{384,448},{4... | collective-permute-start | bytes 5505032 | tf_op jit(solution)/shard_map/ppermute | solution.py:21
  101.9 2.5 %collective-permute-start.10 = (bf16[2,448,256]{2,1,0:T(8,128)(2,1)S(1)}, bf16[2,448,256]{2,1,0:T(8,128)(2,1)S(1)}, u32[]{:S(2)}, u32[]{:S(2)}) collective-permute-start(bf16[2,448,256]{2,1,0:T(8,128)(2,1)S(1)} %get-tuple-element.31), channel_id=1, source_target_pairs={{0,128},{64,192},{128,0},{192,64},{256,384},{320,448},{384,256},{4... | collective-permute-start | bytes 1376264 | tf_op jit(solution)/shard_map/ppermute | solution.py:21
  104.4 4.2 %collective-permute-start.13 = (bf16[2,448,256]{2,1,0:T(8,128)(2,1)S(1)}, bf16[2,448,256]{2,1,0:T(8,128)(2,1)S(1)}, u32[]{:S(2)}, u32[]{:S(2)}) collective-permute-start(bf16[2,448,256]{2,1,0:T(8,128)(2,1)S(1)} %get-tuple-element.32), channel_id=1, source_target_pairs={{0,384},{64,448},{128,256},{192,320},{256,128},{320,192},{384,0},{... | collective-permute-start | bytes 1376264 | tf_op jit(solution)/shard_map/ppermute | solution.py:21
  108.7 7.7 %collective-permute-done.10 = bf16[2,448,256]{2,1,0:T(8,128)(2,1)S(1)} collective-permute-done((bf16[2,448,256]{2,1,0:T(8,128)(2,1)S(1)}, bf16[2,448,256]{2,1,0:T(8,128)(2,1)S(1)}, u32[]{:S(2)}, u32[]{:S(2)}) %collective-permute-start.10) | collective-permute-done | bytes 458784 | tf_op jit(solution)/shard_map/ppermute | solution.py:21
  116.4 3.4 %collective-permute-done.13 = bf16[2,448,256]{2,1,0:T(8,128)(2,1)S(1)} collective-permute-done((bf16[2,448,256]{2,1,0:T(8,128)(2,1)S(1)}, bf16[2,448,256]{2,1,0:T(8,128)(2,1)S(1)}, u32[]{:S(2)}, u32[]{:S(2)}) %collective-permute-start.13) | collective-permute-done | bytes 458784 | tf_op jit(solution)/shard_map/ppermute | solution.py:21
  120.1 2.2 %collective-permute-start.14 = (bf16[448,256]{1,0:T(8,128)(2,1)S(1)}, bf16[448,256]{1,0:T(8,128)(2,1)S(1)}, u32[]{:S(2)}, u32[]{:S(2)}) collective-permute-start(bf16[448,256]{1,0:T(8,128)(2,1)S(1)} %slice_bitcast_fusion), channel_id=1, source_target_pairs={{0,128},{64,192},{128,0},{192,64},{256,384},{320,448},{384,256},{4... | collective-permute-start | bytes 688136 | tf_op jit(solution)/shard_map/ppermute | solution.py:21
  122.3 4.0 %collective-permute-start.11 = (bf16[448,256]{1,0:T(8,128)(2,1)S(1)}, bf16[448,256]{1,0:T(8,128)(2,1)S(1)}, u32[]{:S(2)}, u32[]{:S(2)}) collective-permute-start(bf16[448,256]{1,0:T(8,128)(2,1)S(1)} %slice_bitcast_fusion.2), channel_id=1, source_target_pairs={{0,384},{64,448},{128,256},{192,320},{256,128},{320,192},{384,0},{... | collective-permute-start | bytes 688136 | tf_op jit(solution)/shard_map/ppermute | solution.py:21
  126.3 2.2 %collective-permute-done.14 = bf16[448,256]{1,0:T(8,128)(2,1)S(1)} collective-permute-done((bf16[448,256]{1,0:T(8,128)(2,1)S(1)}, bf16[448,256]{1,0:T(8,128)(2,1)S(1)}, u32[]{:S(2)}, u32[]{:S(2)}) %collective-permute-start.14) | collective-permute-done | bytes 229408 | tf_op jit(solution)/shard_map/ppermute | solution.py:21
  128.5 5.6 %collective-permute-start.15 = (bf16[448,256]{1,0:T(8,128)(2,1)S(1)}, bf16[448,256]{1,0:T(8,128)(2,1)S(1)}, u32[]{:S(2)}, u32[]{:S(2)}) collective-permute-start(bf16[448,256]{1,0:T(8,128)(2,1)S(1)} %fusion), channel_id=1, source_target_pairs={{2,0},{258,1},{0,2},{256,3},{6,4},{262,5},{4,6},{260,7},{10,8},{26... | collective-permute-start | bytes 688136 | tf_op jit(solution)/shard_map/ppermute | solution.py:35
  134.2 1.9 %collective-permute-start.12 = (bf16[448,256]{1,0:T(8,128)(2,1)S(1)}, bf16[448,256]{1,0:T(8,128)(2,1)S(1)}, u32[]{:S(2)}, u32[]{:S(2)}) collective-permute-start(bf16[448,256]{1,0:T(8,128)(2,1)S(1)} %fusion.1), channel_id=1, source_target_pairs={{0,0},{256,1},{2,2},{258,3},{4,4},{260,5},{6,6},{262,7},{8,8},{264... | collective-permute-start | bytes 688136 | tf_op jit(solution)/shard_map/ppermute | solution.py:35
  136.1 3.4 %upstream_partial.1 = (bf16[384,256]{1,0:T(8,128)(2,1)S(1)}, bf16[384,256]{1,0:T(8,128)(2,1)S(1)}, bf16[384,256]{1,0:T(8,128)(2,1)S(1)}, bf16[384,256]{1,0:T(8,128)(2,1)S(1)}) custom-call(s32[4]{0:T(128)S(1)} %pad_add_fusion.s_ref, bf16[2,384,896]{2,1,0:T(8,128)(2,1)S(1)} %get-tuple-element.21.rows_ref, ...), custom_call_target="tpu_custom_call" | custom-call | flops 1409286144 | bytes 2752512 | tf_op jit(solution)/shard_map/upstream_partial/pallas_call | solution.py:187
  139.6 1.9 %collective-permute-start.17 = (bf16[384,256]{1,0:T(8,128)(2,1)S(1)}, bf16[384,256]{1,0:T(8,128)(2,1)S(1)}, u32[]{:S(2)}, u32[]{:S(2)}) collective-permute-start(bf16[384,256]{1,0:T(8,128)(2,1)S(1)} %get-tuple-element.24), channel_id=1, source_target_pairs={{0,1},{1,0},{2,3},{3,2},{4,5},{5,4},{6,7},{7,6},{8,9},{9,8},{10,11... | collective-permute-start | bytes 589832 | tf_op jit(solution)/shard_map/ppermute | solution.py:17
  141.5 4.5 %collective-permute-start.18 = (bf16[384,256]{1,0:T(8,128)(2,1)S(1)}, bf16[384,256]{1,0:T(8,128)(2,1)S(1)}, u32[]{:S(2)}, u32[]{:S(2)}) collective-permute-start(bf16[384,256]{1,0:T(8,128)(2,1)S(1)} %get-tuple-element.25), channel_id=1, source_target_pairs={{0,2},{1,3},{2,0},{3,1},{4,6},{5,7},{6,4},{7,5},{8,10},{9,11},{10,... | collective-permute-start | bytes 589832 | tf_op jit(solution)/shard_map/ppermute | solution.py:17
  146.0 2.8 %collective-permute-start.19 = (bf16[384,256]{1,0:T(8,128)(2,1)S(1)}, bf16[384,256]{1,0:T(8,128)(2,1)S(1)}, u32[]{:S(2)}, u32[]{:S(2)}) collective-permute-start(bf16[384,256]{1,0:T(8,128)(2,1)S(1)} %get-tuple-element.26), channel_id=1, source_target_pairs={{0,3},{1,2},{2,1},{3,0},{4,7},{5,6},{6,5},{7,4},{8,11},{9,10},{10,... | collective-permute-start | bytes 589832 | tf_op jit(solution)/shard_map/ppermute | solution.py:17
  148.8 10.6 %collective-permute-done.18 = bf16[384,256]{1,0:T(8,128)(2,1)S(1)} collective-permute-done((bf16[384,256]{1,0:T(8,128)(2,1)S(1)}, bf16[384,256]{1,0:T(8,128)(2,1)S(1)}, u32[]{:S(2)}, u32[]{:S(2)}) %collective-permute-start.18) | collective-permute-done | bytes 196640 | tf_op jit(solution)/shard_map/ppermute | solution.py:17
  159.4 4.0 %collective-permute-done.19 = bf16[384,256]{1,0:T(8,128)(2,1)S(1)} collective-permute-done((bf16[384,256]{1,0:T(8,128)(2,1)S(1)}, bf16[384,256]{1,0:T(8,128)(2,1)S(1)}, u32[]{:S(2)}, u32[]{:S(2)}) %collective-permute-start.19) | collective-permute-done | bytes 196640 | tf_op jit(solution)/shard_map/ppermute | solution.py:17
  (36 shorter events, 13.6 us)
Async XLA Ops:
  3.8 23.5 %copy-start = (bf16[768,256]{1,0:T(8,128)(2,1)S(1)}, bf16[768,256]{1,0:T(8,128)(2,1)}, u32[]{:S(2)}) copy-start(bf16[768,256]{1,0:T(8,128)(2,1)} %param.9) | copy-start | bytes 1179652
  3.8 23.5 %copy-start.1 = (bf16[768,256]{1,0:T(8,128)(2,1)S(1)}, bf16[768,256]{1,0:T(8,128)(2,1)}, u32[]{:S(2)}) copy-start(bf16[768,256]{1,0:T(8,128)(2,1)} %param.10) | copy-start | bytes 1179652
  3.8 89.1 %all-to-all-start = ((bf16[32,24,896]{2,1,0:T(8,128)(2,1)}), bf16[32,24,896]{2,1,0:T(8,128)(2,1)S(1)}, u32[]{:S(2)}, u32[]{:S(2)}) async-start(bf16[32,24,896]{2,1,0:T(8,128)(2,1)} %bitcast.6), calls=%async_computation | async-start | bytes 2752512 | tf_op jit(solution)/shard_map/all_to_all | solution.py:231
  18.9 46.4 %collective-permute-start = (bf16[448,256]{1,0:T(8,128)(2,1)}, bf16[448,256]{1,0:T(8,128)(2,1)}, u32[]{:S(2)}, u32[]{:S(2)}) collective-permute-start(bf16[448,256]{1,0:T(8,128)(2,1)} %param.11), channel_id=1, source_target_pairs={{0,0},{1,256},{2,2},{3,258},{4,4},{5,260},{6,6},{7,262},{8,8},{9,2... | collective-permute-start | bytes 688136 | tf_op jit(solution)/shard_map/ppermute | solution.py:35
  23.8 44.9 %collective-permute-start.1 = (bf16[448,256]{1,0:T(8,128)(2,1)}, bf16[448,256]{1,0:T(8,128)(2,1)S(1)}, u32[]{:S(2)}, u32[]{:S(2)}) collective-permute-start(bf16[448,256]{1,0:T(8,128)(2,1)} %param.11), channel_id=1, source_target_pairs={{0,2},{1,258},{2,0},{3,256},{4,6},{5,262},{6,4},{7,260},{8,10},{9,... | collective-permute-start | bytes 688136 | tf_op jit(solution)/shard_map/ppermute | solution.py:35
  28.1 64.8 %collective-permute-start.7 = (bf16[384,256]{1,0:T(8,128)(2,1)S(1)}, bf16[384,256]{1,0:T(8,128)(2,1)S(1)}, u32[]{:S(2)}, u32[]{:S(2)}) collective-permute-start(bf16[384,256]{1,0:T(8,128)(2,1)S(1)} %bitcast.45), channel_id=1, source_target_pairs={{0,2},{1,3},{2,0},{3,1},{4,6},{5,7},{6,4},{7,5},{8,10},{9,11},{10,... | collective-permute-start | bytes 589832 | tf_op jit(solution)/shard_map/ppermute | solution.py:17
  32.4 60.5 %collective-permute-start.8 = (bf16[384,256]{1,0:T(8,128)(2,1)S(1)}, bf16[384,256]{1,0:T(8,128)(2,1)S(1)}, u32[]{:S(2)}, u32[]{:S(2)}) collective-permute-start(bf16[384,256]{1,0:T(8,128)(2,1)S(1)} %bitcast.46), channel_id=1, source_target_pairs={{0,3},{1,2},{2,1},{3,0},{4,7},{5,6},{6,5},{7,4},{8,11},{9,10},{10,... | collective-permute-start | bytes 589832 | tf_op jit(solution)/shard_map/ppermute | solution.py:17
  34.3 58.6 %collective-permute-start.6 = (bf16[384,256]{1,0:T(8,128)(2,1)S(1)}, bf16[384,256]{1,0:T(8,128)(2,1)S(1)}, u32[]{:S(2)}, u32[]{:S(2)}) collective-permute-start(bf16[384,256]{1,0:T(8,128)(2,1)S(1)} %bitcast.43), channel_id=1, source_target_pairs={{0,1},{1,0},{2,3},{3,2},{4,5},{5,4},{6,7},{7,6},{8,9},{9,8},{10,11... | collective-permute-start | bytes 589832 | tf_op jit(solution)/shard_map/ppermute | solution.py:17
  65.3 9.5 %collective-permute-start.2 = (bf16[1,448,256]{2,1,0:T(8,128)(2,1)}, bf16[1,448,256]{2,1,0:T(8,128)(2,1)S(1)}, u32[]{:S(2)}, u32[]{:S(2)}) collective-permute-start(bf16[1,448,256]{2,1,0:T(8,128)(2,1)} %bitcast.7), channel_id=1, source_target_pairs={{0,128},{64,192},{128,0},{192,64},{256,384},{320,448},{384,256},{4... | collective-permute-start | bytes 688136 | tf_op jit(solution)/shard_map/ppermute | solution.py:21
  68.7 10.2 %collective-permute-start.3 = (bf16[1,448,256]{2,1,0:T(8,128)(2,1)S(1)}, bf16[1,448,256]{2,1,0:T(8,128)(2,1)S(1)}, u32[]{:S(2)}, u32[]{:S(2)}) collective-permute-start(bf16[1,448,256]{2,1,0:T(8,128)(2,1)S(1)} %bitcast.47), channel_id=1, source_target_pairs={{0,384},{64,448},{128,256},{192,320},{256,128},{320,192},{384,0},{... | collective-permute-start | bytes 688136 | tf_op jit(solution)/shard_map/ppermute | solution.py:21
  75.8 14.6 %collective-permute-start.4 = (bf16[2,448,256]{2,1,0:T(8,128)(2,1)S(1)}, bf16[2,448,256]{2,1,0:T(8,128)(2,1)S(1)}, u32[]{:S(2)}, u32[]{:S(2)}) collective-permute-start(bf16[2,448,256]{2,1,0:T(8,128)(2,1)S(1)} %pad_maximum_fusion), channel_id=1, source_target_pairs={{0,384},{64,448},{128,256},{192,320},{256,128},{320,192},{384,0},{... | collective-permute-start | bytes 1376264 | tf_op jit(solution)/shard_map/ppermute | solution.py:21
  79.0 13.1 %collective-permute-start.5 = (bf16[2,448,256]{2,1,0:T(8,128)(2,1)S(1)}, bf16[2,448,256]{2,1,0:T(8,128)(2,1)S(1)}, u32[]{:S(2)}, u32[]{:S(2)}) collective-permute-start(bf16[2,448,256]{2,1,0:T(8,128)(2,1)S(1)} %pad_maximum_fusion.1), channel_id=1, source_target_pairs={{0,128},{64,192},{128,0},{192,64},{256,384},{320,448},{384,256},{4... | collective-permute-start | bytes 1376264 | tf_op jit(solution)/shard_map/ppermute | solution.py:21
  95.7 5.7 %collective-permute-start.9 = (bf16[8,448,256]{2,1,0:T(8,128)(2,1)S(1)}, bf16[8,448,256]{2,1,0:T(8,128)(2,1)S(1)}, u32[]{:S(2)}, u32[]{:S(2)}) collective-permute-start(bf16[8,448,256]{2,1,0:T(8,128)(2,1)S(1)} %get-tuple-element.20), channel_id=1, source_target_pairs={{0,64},{64,0},{128,192},{192,128},{256,320},{320,256},{384,448},{4... | collective-permute-start | bytes 5505032 | tf_op jit(solution)/shard_map/ppermute | solution.py:21
  97.6 38.5 %collective-permute-start.16 = (bf16[8,448,256]{2,1,0:T(8,128)(2,1)}, bf16[8,448,256]{2,1,0:T(8,128)(2,1)S(1)}, u32[]{:S(2)}, u32[]{:S(2)}) collective-permute-start(bf16[8,448,256]{2,1,0:T(8,128)(2,1)} %constant_dynamic-update-slice_fusion.near_ref), channel_id=1, source_target_pairs={{0,64},{64,0},{128,192},{192,128},{256,320},{320,256},{384,448},{4... | collective-permute-start | bytes 5505032 | tf_op jit(solution)/shard_map/ppermute | solution.py:21
  101.9 14.5 %collective-permute-start.10 = (bf16[2,448,256]{2,1,0:T(8,128)(2,1)S(1)}, bf16[2,448,256]{2,1,0:T(8,128)(2,1)S(1)}, u32[]{:S(2)}, u32[]{:S(2)}) collective-permute-start(bf16[2,448,256]{2,1,0:T(8,128)(2,1)S(1)} %get-tuple-element.31), channel_id=1, source_target_pairs={{0,128},{64,192},{128,0},{192,64},{256,384},{320,448},{384,256},{4... | collective-permute-start | bytes 1376264 | tf_op jit(solution)/shard_map/ppermute | solution.py:21
  104.4 15.4 %collective-permute-start.13 = (bf16[2,448,256]{2,1,0:T(8,128)(2,1)S(1)}, bf16[2,448,256]{2,1,0:T(8,128)(2,1)S(1)}, u32[]{:S(2)}, u32[]{:S(2)}) collective-permute-start(bf16[2,448,256]{2,1,0:T(8,128)(2,1)S(1)} %get-tuple-element.32), channel_id=1, source_target_pairs={{0,384},{64,448},{128,256},{192,320},{256,128},{320,192},{384,0},{... | collective-permute-start | bytes 1376264 | tf_op jit(solution)/shard_map/ppermute | solution.py:21
  120.1 8.4 %collective-permute-start.14 = (bf16[448,256]{1,0:T(8,128)(2,1)S(1)}, bf16[448,256]{1,0:T(8,128)(2,1)S(1)}, u32[]{:S(2)}, u32[]{:S(2)}) collective-permute-start(bf16[448,256]{1,0:T(8,128)(2,1)S(1)} %slice_bitcast_fusion), channel_id=1, source_target_pairs={{0,128},{64,192},{128,0},{192,64},{256,384},{320,448},{384,256},{4... | collective-permute-start | bytes 688136 | tf_op jit(solution)/shard_map/ppermute | solution.py:21
  122.3 11.8 %collective-permute-start.11 = (bf16[448,256]{1,0:T(8,128)(2,1)S(1)}, bf16[448,256]{1,0:T(8,128)(2,1)S(1)}, u32[]{:S(2)}, u32[]{:S(2)}) collective-permute-start(bf16[448,256]{1,0:T(8,128)(2,1)S(1)} %slice_bitcast_fusion.2), channel_id=1, source_target_pairs={{0,384},{64,448},{128,256},{192,320},{256,128},{320,192},{384,0},{... | collective-permute-start | bytes 688136 | tf_op jit(solution)/shard_map/ppermute | solution.py:21
  128.5 36.6 %collective-permute-start.15 = (bf16[448,256]{1,0:T(8,128)(2,1)S(1)}, bf16[448,256]{1,0:T(8,128)(2,1)S(1)}, u32[]{:S(2)}, u32[]{:S(2)}) collective-permute-start(bf16[448,256]{1,0:T(8,128)(2,1)S(1)} %fusion), channel_id=1, source_target_pairs={{2,0},{258,1},{0,2},{256,3},{6,4},{262,5},{4,6},{260,7},{10,8},{26... | collective-permute-start | bytes 688136 | tf_op jit(solution)/shard_map/ppermute | solution.py:35
  134.2 31.0 %collective-permute-start.12 = (bf16[448,256]{1,0:T(8,128)(2,1)S(1)}, bf16[448,256]{1,0:T(8,128)(2,1)S(1)}, u32[]{:S(2)}, u32[]{:S(2)}) collective-permute-start(bf16[448,256]{1,0:T(8,128)(2,1)S(1)} %fusion.1), channel_id=1, source_target_pairs={{0,0},{256,1},{2,2},{258,3},{4,4},{260,5},{6,6},{262,7},{8,8},{264... | collective-permute-start | bytes 688136 | tf_op jit(solution)/shard_map/ppermute | solution.py:35
  139.6 9.2 %collective-permute-start.17 = (bf16[384,256]{1,0:T(8,128)(2,1)S(1)}, bf16[384,256]{1,0:T(8,128)(2,1)S(1)}, u32[]{:S(2)}, u32[]{:S(2)}) collective-permute-start(bf16[384,256]{1,0:T(8,128)(2,1)S(1)} %get-tuple-element.24), channel_id=1, source_target_pairs={{0,1},{1,0},{2,3},{3,2},{4,5},{5,4},{6,7},{7,6},{8,9},{9,8},{10,11... | collective-permute-start | bytes 589832 | tf_op jit(solution)/shard_map/ppermute | solution.py:17
  141.5 17.9 %collective-permute-start.18 = (bf16[384,256]{1,0:T(8,128)(2,1)S(1)}, bf16[384,256]{1,0:T(8,128)(2,1)S(1)}, u32[]{:S(2)}, u32[]{:S(2)}) collective-permute-start(bf16[384,256]{1,0:T(8,128)(2,1)S(1)} %get-tuple-element.25), channel_id=1, source_target_pairs={{0,2},{1,3},{2,0},{3,1},{4,6},{5,7},{6,4},{7,5},{8,10},{9,11},{10,... | collective-permute-start | bytes 589832 | tf_op jit(solution)/shard_map/ppermute | solution.py:17
  146.0 17.4 %collective-permute-start.19 = (bf16[384,256]{1,0:T(8,128)(2,1)S(1)}, bf16[384,256]{1,0:T(8,128)(2,1)S(1)}, u32[]{:S(2)}, u32[]{:S(2)}) collective-permute-start(bf16[384,256]{1,0:T(8,128)(2,1)S(1)} %get-tuple-element.26), channel_id=1, source_target_pairs={{0,3},{1,2},{2,1},{3,0},{4,7},{5,6},{6,5},{7,4},{8,11},{9,10},{10,... | collective-permute-start | bytes 589832 | tf_op jit(solution)/shard_map/ppermute | solution.py:17

commit v5 on v4

--- a/solution.py
+++ b/solution.py
@@ -263,13 +263,18 @@
     crossed = dp_xor(send, 1)
     parts = upstream_partial(scalars, rows, near, far)
     summed = added(keep, crossed)
-    first = [dp_xor(summed[0:2], 2), dp_xor(summed[2:4], 6)]
+    far_sum = dp_xor(summed[2:4], 6)
+    near_sum = dp_xor(summed[0:2], 2)
     parts = [parts[0]] + [expert_xor(parts[q], q) for q in (1, 2, 3)]
     parts = [part.reshape(ys, 2, PART, columns) for part in parts]
-    first = [added(summed[4:6], first[0]), added(summed[6:8], first[1])]
-    second = [dp_xor(first[0][1], 6), dp_xor(first[1][1], 2)]
-    kept = [added(first[e][0], second[e]) for e in range(2)]
-    weight_grad = added(swapped(kept[0], 0, True), swapped(kept[1], 1, True))
+    far_first = added(summed[6:8], far_sum)
+    near_sum, far_first = lax.optimization_barrier((near_sum, far_first))
+    near_first = added(summed[4:6], near_sum)
+    far_second = dp_xor(far_first[1], 2)
+    near_second = dp_xor(near_first[1], 6)
+    crossed = swapped(added(far_first[0], far_second), 1, True)
+    stayed = swapped(added(near_first[0], near_second), 0, True)
+    weight_grad = added(stayed, crossed)
     gate_grad, up_grad = finish(scalars, gate4, up4, parts)
     return (
         weight_grad,

time: 167 us -> 170 us (1.018)
  waiting for transfers between devices: 67.4 us -> 72.6 us
  starting transfers between devices: 77.5 us -> 75.6 us
    ppermute x10, waiting for transfers between devices: 25.7 us -> 30.8 us  [dp_xor(): lax.ppermute(value, 'dp', [(i, i ^ mask) for i in range(lax.axis_size('dp...]
    ppermute x10, starting transfers between devices: 27.3 us -> 25.4 us  [dp_xor(): lax.ppermute(value, 'dp', [(i, i ^ mask) for i in range(lax.axis_size('dp...]
where the time goes in v5:
time: 170 us; the launch traced here: 169 us
  starting transfers between devices  75.6 us (44%)
  waiting for transfers between devices  72.6 us (43%)
  Pallas kernels  12 us (7%)
  local copies, waits for them, and re-layouts  5.52 us (3%)
  other arithmetic  2.73 us (2%)
    ppermute x10, waiting for transfers between devices, dp_xor(): lax.ppermute(value, 'dp', [(i, i ^ mask) for i in range(lax.axis_size('dp...  30.8 us
    ppermute x4, waiting for transfers between devices, swapped(): return lax.ppermute(value, ('dp', 'expert'), pairs)  27.1 us
    ppermute x10, starting transfers between devices, dp_xor(): lax.ppermute(value, 'dp', [(i, i ^ mask) for i in range(lax.axis_size('dp...  25.4 us
    ppermute x6, starting transfers between devices, expert_xor(): lax.ppermute(value, 'expert', [(i, i ^ mask) for i in range(lax.axis_size...  19.3 us
    ppermute x4, starting transfers between devices, swapped(): return lax.ppermute(value, ('dp', 'expert'), pairs)  15.8 us
    all_to_all x1, starting transfers between devices, dispatched(): lax.all_to_all(slots, 'expert', split_axis=0, concat_axis=0, tiled=True,...  15.1 us
    ppermute x6, waiting for transfers between devices, expert_xor(): lax.ppermute(value, 'expert', [(i, i ^ mask) for i in range(lax.axis_size...  14.7 us
    unnamed x9, local copies, waits for them, and re-layouts  4.6 us
  transfers between devices with their start and end apart: 21, of which 11 were waited for; matrix products, arithmetic and copies ran while one was open for 4% of the time, Pallas kernels for 4%

profile of v5, /device:TPU:96, one launch (start us, length us, event | category | flops | bytes accessed | tf_op | source)
XLA Modules:
  0.0 169.3 jit_solution(10160923644551653880)
XLA Ops:
  0.6 3.2 %slots.1 = bf16[16,2,24,896]{3,2,1,0:T(8,128)(2,1)} custom-call(s32[1,128]{1,0:T(1,128)} %bitcast.49, f32[1,128]{1,0:T(1,128)} %bitcast.50, bf16[128,3584]{1,0:T(8,128)(2,1)} %cot_ref.1), custom_call_target="tpu_custom_call" | custom-call | flops 704643072 | bytes 1835008 | tf_op jit(solution)/shard_map/slots/pallas_call | solution.py:72
  3.8 15.1 %all-to-all-start = ((bf16[32,24,896]{2,1,0:T(8,128)(2,1)}), bf16[32,24,896]{2,1,0:T(8,128)(2,1)S(1)}, u32[]{:S(2)}, u32[]{:S(2)}) async-start(bf16[32,24,896]{2,1,0:T(8,128)(2,1)} %bitcast.6), calls=%async_computation | async-start | bytes 2752512 | tf_op jit(solution)/shard_map/all_to_all | solution.py:231
  18.9 4.9 %collective-permute-start = (bf16[448,256]{1,0:T(8,128)(2,1)}, bf16[448,256]{1,0:T(8,128)(2,1)}, u32[]{:S(2)}, u32[]{:S(2)}) collective-permute-start(bf16[448,256]{1,0:T(8,128)(2,1)} %param.11), channel_id=1, source_target_pairs={{0,0},{1,256},{2,2},{3,258},{4,4},{5,260},{6,6},{7,262},{8,8},{9,2... | collective-permute-start | bytes 688136 | tf_op jit(solution)/shard_map/ppermute | solution.py:35
  23.8 3.4 %collective-permute-start.1 = (bf16[448,256]{1,0:T(8,128)(2,1)}, bf16[448,256]{1,0:T(8,128)(2,1)S(1)}, u32[]{:S(2)}, u32[]{:S(2)}) collective-permute-start(bf16[448,256]{1,0:T(8,128)(2,1)} %param.11), channel_id=1, source_target_pairs={{0,2},{1,258},{2,0},{3,256},{4,6},{5,262},{6,4},{7,260},{8,10},{9,... | collective-permute-start | bytes 688136 | tf_op jit(solution)/shard_map/ppermute | solution.py:35
  28.1 4.3 %collective-permute-start.7 = (bf16[384,256]{1,0:T(8,128)(2,1)S(1)}, bf16[384,256]{1,0:T(8,128)(2,1)S(1)}, u32[]{:S(2)}, u32[]{:S(2)}) collective-permute-start(bf16[384,256]{1,0:T(8,128)(2,1)S(1)} %bitcast.43), channel_id=1, source_target_pairs={{0,2},{1,3},{2,0},{3,1},{4,6},{5,7},{6,4},{7,5},{8,10},{9,11},{10,... | collective-permute-start | bytes 589832 | tf_op jit(solution)/shard_map/ppermute | solution.py:17
  32.4 1.9 %collective-permute-start.8 = (bf16[384,256]{1,0:T(8,128)(2,1)S(1)}, bf16[384,256]{1,0:T(8,128)(2,1)S(1)}, u32[]{:S(2)}, u32[]{:S(2)}) collective-permute-start(bf16[384,256]{1,0:T(8,128)(2,1)S(1)} %bitcast.44), channel_id=1, source_target_pairs={{0,3},{1,2},{2,1},{3,0},{4,7},{5,6},{6,5},{7,4},{8,11},{9,10},{10,... | collective-permute-start | bytes 589832 | tf_op jit(solution)/shard_map/ppermute | solution.py:17
  34.3 3.9 %collective-permute-start.6 = (bf16[384,256]{1,0:T(8,128)(2,1)S(1)}, bf16[384,256]{1,0:T(8,128)(2,1)S(1)}, u32[]{:S(2)}, u32[]{:S(2)}) collective-permute-start(bf16[384,256]{1,0:T(8,128)(2,1)S(1)} %bitcast.41), channel_id=1, source_target_pairs={{0,1},{1,0},{2,3},{3,2},{4,5},{5,4},{6,7},{7,6},{8,9},{9,8},{10,11... | collective-permute-start | bytes 589832 | tf_op jit(solution)/shard_map/ppermute | solution.py:17
  38.2 27.1 %collective-permute-done = bf16[448,256]{1,0:T(8,128)(2,1)} collective-permute-done((bf16[448,256]{1,0:T(8,128)(2,1)}, bf16[448,256]{1,0:T(8,128)(2,1)}, u32[]{:S(2)}, u32[]{:S(2)}) %collective-permute-start) | collective-permute-done | bytes 229408 | tf_op jit(solution)/shard_map/ppermute | solution.py:35
  65.3 3.4 %collective-permute-start.2 = (bf16[1,448,256]{2,1,0:T(8,128)(2,1)}, bf16[1,448,256]{2,1,0:T(8,128)(2,1)S(1)}, u32[]{:S(2)}, u32[]{:S(2)}) collective-permute-start(bf16[1,448,256]{2,1,0:T(8,128)(2,1)} %bitcast.7), channel_id=1, source_target_pairs={{0,128},{64,192},{128,0},{192,64},{256,384},{320,448},{384,256},{4... | collective-permute-start | bytes 688136 | tf_op jit(solution)/shard_map/ppermute | solution.py:21
  68.7 1.9 %collective-permute-start.3 = (bf16[1,448,256]{2,1,0:T(8,128)(2,1)S(1)}, bf16[1,448,256]{2,1,0:T(8,128)(2,1)S(1)}, u32[]{:S(2)}, u32[]{:S(2)}) collective-permute-start(bf16[1,448,256]{2,1,0:T(8,128)(2,1)S(1)} %bitcast.45), channel_id=1, source_target_pairs={{0,384},{64,448},{128,256},{192,320},{256,128},{320,192},{384,0},{... | collective-permute-start | bytes 688136 | tf_op jit(solution)/shard_map/ppermute | solution.py:21
  72.3 2.5 %collective-permute-done.2 = bf16[1,448,256]{2,1,0:T(8,128)(2,1)S(1)} collective-permute-done((bf16[1,448,256]{2,1,0:T(8,128)(2,1)}, bf16[1,448,256]{2,1,0:T(8,128)(2,1)S(1)}, u32[]{:S(2)}, u32[]{:S(2)}) %collective-permute-start.2) | collective-permute-done | bytes 229408 | tf_op jit(solution)/shard_map/ppermute | solution.py:21
  75.8 2.6 %collective-permute-start.4 = (bf16[2,448,256]{2,1,0:T(8,128)(2,1)S(1)}, bf16[2,448,256]{2,1,0:T(8,128)(2,1)S(1)}, u32[]{:S(2)}, u32[]{:S(2)}) collective-permute-start(bf16[2,448,256]{2,1,0:T(8,128)(2,1)S(1)} %pad_maximum_fusion), channel_id=1, source_target_pairs={{0,384},{64,448},{128,256},{192,320},{256,128},{320,192},{384,0},{... | collective-permute-start | bytes 1376264 | tf_op jit(solution)/shard_map/ppermute | solution.py:21
  79.0 2.2 %collective-permute-start.5 = (bf16[2,448,256]{2,1,0:T(8,128)(2,1)S(1)}, bf16[2,448,256]{2,1,0:T(8,128)(2,1)S(1)}, u32[]{:S(2)}, u32[]{:S(2)}) collective-permute-start(bf16[2,448,256]{2,1,0:T(8,128)(2,1)S(1)} %pad_maximum_fusion.1), channel_id=1, source_target_pairs={{0,128},{64,192},{128,0},{192,64},{256,384},{320,448},{384,256},{4... | collective-permute-start | bytes 1376264 | tf_op jit(solution)/shard_map/ppermute | solution.py:21
  83.3 7.0 %collective-permute-done.4 = bf16[2,448,256]{2,1,0:T(8,128)(2,1)S(1)} collective-permute-done((bf16[2,448,256]{2,1,0:T(8,128)(2,1)S(1)}, bf16[2,448,256]{2,1,0:T(8,128)(2,1)S(1)}, u32[]{:S(2)}, u32[]{:S(2)}) %collective-permute-start.4) | collective-permute-done | bytes 458784 | tf_op jit(solution)/shard_map/ppermute | solution.py:21
  92.9 2.8 %weight_partial.1 = (bf16[2,384,896]{2,1,0:T(8,128)(2,1)S(1)}, bf16[8,448,256]{2,1,0:T(8,128)(2,1)S(1)}, bf16[8,448,256]{2,1,0:T(8,128)(2,1)S(1)}) custom-call(s32[4]{0:T(128)S(1)} %pad_add_fusion.s_ref, bf16[32,24,896]{2,1,0:T(8,128)(2,1)S(1)} %all-to-all-done.recv_ref, bf16[384,256]{1,0:T(8,128)(2,1)S(1)} %bitcast.42, ...), custom_call_target="tpu_custom_call" | custom-call | flops 1409286144 | bytes 2752512 | tf_op jit(solution)/shard_map/weight_partial/pallas_call | solution.py:157
  95.7 1.9 %collective-permute-start.9 = (bf16[8,448,256]{2,1,0:T(8,128)(2,1)S(1)}, bf16[8,448,256]{2,1,0:T(8,128)(2,1)S(1)}, u32[]{:S(2)}, u32[]{:S(2)}) collective-permute-start(bf16[8,448,256]{2,1,0:T(8,128)(2,1)S(1)} %get-tuple-element.22), channel_id=1, source_target_pairs={{0,64},{64,0},{128,192},{192,128},{256,320},{320,256},{384,448},{4... | collective-permute-start | bytes 5505032 | tf_op jit(solution)/shard_map/ppermute | solution.py:21
  97.6 3.8 %collective-permute-done.9 = bf16[8,448,256]{2,1,0:T(8,128)(2,1)S(1)} collective-permute-done((bf16[8,448,256]{2,1,0:T(8,128)(2,1)S(1)}, bf16[8,448,256]{2,1,0:T(8,128)(2,1)S(1)}, u32[]{:S(2)}, u32[]{:S(2)}) %collective-permute-start.9) | collective-permute-done | bytes 1835040 | tf_op jit(solution)/shard_map/ppermute | solution.py:21
  102.0 3.9 %collective-permute-start.11 = (bf16[2,448,256]{2,1,0:T(8,128)(2,1)S(1)}, bf16[2,448,256]{2,1,0:T(8,128)(2,1)S(1)}, u32[]{:S(2)}, u32[]{:S(2)}) collective-permute-start(bf16[2,448,256]{2,1,0:T(8,128)(2,1)S(1)} %get-tuple-element.33), channel_id=1, source_target_pairs={{0,384},{64,448},{128,256},{192,320},{256,128},{320,192},{384,0},{... | collective-permute-start | bytes 1376264 | tf_op jit(solution)/shard_map/ppermute | solution.py:21
  107.8 2.2 %collective-permute-start.10 = (bf16[2,448,256]{2,1,0:T(8,128)(2,1)S(1)}, bf16[2,448,256]{2,1,0:T(8,128)(2,1)S(1)}, u32[]{:S(2)}, u32[]{:S(2)}) collective-permute-start(bf16[2,448,256]{2,1,0:T(8,128)(2,1)S(1)} %get-tuple-element.34), channel_id=1, source_target_pairs={{0,128},{64,192},{128,0},{192,64},{256,384},{320,448},{384,256},{4... | collective-permute-start | bytes 1376264 | tf_op jit(solution)/shard_map/ppermute | solution.py:21
  110.0 7.6 %collective-permute-done.11 = bf16[2,448,256]{2,1,0:T(8,128)(2,1)S(1)} collective-permute-done((bf16[2,448,256]{2,1,0:T(8,128)(2,1)S(1)}, bf16[2,448,256]{2,1,0:T(8,128)(2,1)S(1)}, u32[]{:S(2)}, u32[]{:S(2)}) %collective-permute-start.11) | collective-permute-done | bytes 458784 | tf_op jit(solution)/shard_map/ppermute | solution.py:21
  117.7 4.9 %collective-permute-done.10 = bf16[2,448,256]{2,1,0:T(8,128)(2,1)S(1)} collective-permute-done((bf16[2,448,256]{2,1,0:T(8,128)(2,1)S(1)}, bf16[2,448,256]{2,1,0:T(8,128)(2,1)S(1)}, u32[]{:S(2)}, u32[]{:S(2)}) %collective-permute-start.10) | collective-permute-done | bytes 458784 | tf_op jit(solution)/shard_map/ppermute | solution.py:21
  122.7 2.2 %collective-permute-start.14 = (bf16[448,256]{1,0:T(8,128)(2,1)S(1)}, bf16[448,256]{1,0:T(8,128)(2,1)S(1)}, u32[]{:S(2)}, u32[]{:S(2)}) collective-permute-start(bf16[448,256]{1,0:T(8,128)(2,1)S(1)} %slice_bitcast_fusion.2), channel_id=1, source_target_pairs={{0,128},{64,192},{128,0},{192,64},{256,384},{320,448},{384,256},{4... | collective-permute-start | bytes 688136 | tf_op jit(solution)/shard_map/ppermute | solution.py:21
  125.0 3.1 %collective-permute-start.12 = (bf16[448,256]{1,0:T(8,128)(2,1)S(1)}, bf16[448,256]{1,0:T(8,128)(2,1)S(1)}, u32[]{:S(2)}, u32[]{:S(2)}) collective-permute-start(bf16[448,256]{1,0:T(8,128)(2,1)S(1)} %slice_bitcast_fusion), channel_id=1, source_target_pairs={{0,384},{64,448},{128,256},{192,320},{256,128},{320,192},{384,0},{... | collective-permute-start | bytes 688136 | tf_op jit(solution)/shard_map/ppermute | solution.py:21
  128.1 3.5 %collective-permute-done.14 = bf16[448,256]{1,0:T(8,128)(2,1)S(1)} collective-permute-done((bf16[448,256]{1,0:T(8,128)(2,1)S(1)}, bf16[448,256]{1,0:T(8,128)(2,1)S(1)}, u32[]{:S(2)}, u32[]{:S(2)}) %collective-permute-start.14) | collective-permute-done | bytes 229408 | tf_op jit(solution)/shard_map/ppermute | solution.py:21
  131.8 5.6 %collective-permute-start.15 = (bf16[448,256]{1,0:T(8,128)(2,1)S(1)}, bf16[448,256]{1,0:T(8,128)(2,1)S(1)}, u32[]{:S(2)}, u32[]{:S(2)}) collective-permute-start(bf16[448,256]{1,0:T(8,128)(2,1)S(1)} %fusion), channel_id=1, source_target_pairs={{2,0},{258,1},{0,2},{256,3},{6,4},{262,5},{4,6},{260,7},{10,8},{26... | collective-permute-start | bytes 688136 | tf_op jit(solution)/shard_map/ppermute | solution.py:35
  137.4 1.9 %collective-permute-start.13 = (bf16[448,256]{1,0:T(8,128)(2,1)S(1)}, bf16[448,256]{1,0:T(8,128)(2,1)S(1)}, u32[]{:S(2)}, u32[]{:S(2)}) collective-permute-start(bf16[448,256]{1,0:T(8,128)(2,1)S(1)} %fusion.1), channel_id=1, source_target_pairs={{0,0},{256,1},{2,2},{258,3},{4,4},{260,5},{6,6},{262,7},{8,8},{264... | collective-permute-start | bytes 688136 | tf_op jit(solution)/shard_map/ppermute | solution.py:35
  139.3 3.4 %upstream_partial.1 = (bf16[384,256]{1,0:T(8,128)(2,1)S(1)}, bf16[384,256]{1,0:T(8,128)(2,1)S(1)}, bf16[384,256]{1,0:T(8,128)(2,1)S(1)}, bf16[384,256]{1,0:T(8,128)(2,1)S(1)}) custom-call(s32[4]{0:T(128)S(1)} %pad_add_fusion.s_ref, bf16[2,384,896]{2,1,0:T(8,128)(2,1)S(1)} %get-tuple-element.25.rows_ref, ...), custom_call_target="tpu_custom_call" | custom-call | flops 1409286144 | bytes 2752512 | tf_op jit(solution)/shard_map/upstream_partial/pallas_call | solution.py:187
  142.8 1.9 %collective-permute-start.17 = (bf16[384,256]{1,0:T(8,128)(2,1)S(1)}, bf16[384,256]{1,0:T(8,128)(2,1)S(1)}, u32[]{:S(2)}, u32[]{:S(2)}) collective-permute-start(bf16[384,256]{1,0:T(8,128)(2,1)S(1)} %get-tuple-element.28), channel_id=1, source_target_pairs={{0,1},{1,0},{2,3},{3,2},{4,5},{5,4},{6,7},{7,6},{8,9},{9,8},{10,11... | collective-permute-start | bytes 589832 | tf_op jit(solution)/shard_map/ppermute | solution.py:17
  144.7 4.8 %collective-permute-start.18 = (bf16[384,256]{1,0:T(8,128)(2,1)S(1)}, bf16[384,256]{1,0:T(8,128)(2,1)S(1)}, u32[]{:S(2)}, u32[]{:S(2)}) collective-permute-start(bf16[384,256]{1,0:T(8,128)(2,1)S(1)} %get-tuple-element.29), channel_id=1, source_target_pairs={{0,2},{1,3},{2,0},{3,1},{4,6},{5,7},{6,4},{7,5},{8,10},{9,11},{10,... | collective-permute-start | bytes 589832 | tf_op jit(solution)/shard_map/ppermute | solution.py:17
  149.5 2.5 %collective-permute-start.19 = (bf16[384,256]{1,0:T(8,128)(2,1)S(1)}, bf16[384,256]{1,0:T(8,128)(2,1)S(1)}, u32[]{:S(2)}, u32[]{:S(2)}) collective-permute-start(bf16[384,256]{1,0:T(8,128)(2,1)S(1)} %get-tuple-element.30), channel_id=1, source_target_pairs={{0,3},{1,2},{2,1},{3,0},{4,7},{5,6},{6,5},{7,4},{8,11},{9,10},{10,... | collective-permute-start | bytes 589832 | tf_op jit(solution)/shard_map/ppermute | solution.py:17
  152.0 10.4 %collective-permute-done.18 = bf16[384,256]{1,0:T(8,128)(2,1)S(1)} collective-permute-done((bf16[384,256]{1,0:T(8,128)(2,1)S(1)}, bf16[384,256]{1,0:T(8,128)(2,1)S(1)}, u32[]{:S(2)}, u32[]{:S(2)}) %collective-permute-start.18) | collective-permute-done | bytes 196640 | tf_op jit(solution)/shard_map/ppermute | solution.py:17
  162.4 4.3 %collective-permute-done.19 = bf16[384,256]{1,0:T(8,128)(2,1)S(1)} collective-permute-done((bf16[384,256]{1,0:T(8,128)(2,1)S(1)}, bf16[384,256]{1,0:T(8,128)(2,1)S(1)}, u32[]{:S(2)}, u32[]{:S(2)}) %collective-permute-start.19) | collective-permute-done | bytes 196640 | tf_op jit(solution)/shard_map/ppermute | solution.py:17
  (37 shorter events, 14.2 us)
Async XLA Ops:
  3.8 23.5 %copy-start = (bf16[768,256]{1,0:T(8,128)(2,1)S(1)}, bf16[768,256]{1,0:T(8,128)(2,1)}, u32[]{:S(2)}) copy-start(bf16[768,256]{1,0:T(8,128)(2,1)} %param.9) | copy-start | bytes 1179652
  3.8 23.5 %copy-start.1 = (bf16[768,256]{1,0:T(8,128)(2,1)S(1)}, bf16[768,256]{1,0:T(8,128)(2,1)}, u32[]{:S(2)}) copy-start(bf16[768,256]{1,0:T(8,128)(2,1)} %param.10) | copy-start | bytes 1179652
  3.8 89.1 %all-to-all-start = ((bf16[32,24,896]{2,1,0:T(8,128)(2,1)}), bf16[32,24,896]{2,1,0:T(8,128)(2,1)S(1)}, u32[]{:S(2)}, u32[]{:S(2)}) async-start(bf16[32,24,896]{2,1,0:T(8,128)(2,1)} %bitcast.6), calls=%async_computation | async-start | bytes 2752512 | tf_op jit(solution)/shard_map/all_to_all | solution.py:231
  18.9 46.4 %collective-permute-start = (bf16[448,256]{1,0:T(8,128)(2,1)}, bf16[448,256]{1,0:T(8,128)(2,1)}, u32[]{:S(2)}, u32[]{:S(2)}) collective-permute-start(bf16[448,256]{1,0:T(8,128)(2,1)} %param.11), channel_id=1, source_target_pairs={{0,0},{1,256},{2,2},{3,258},{4,4},{5,260},{6,6},{7,262},{8,8},{9,2... | collective-permute-start | bytes 688136 | tf_op jit(solution)/shard_map/ppermute | solution.py:35
  23.8 44.9 %collective-permute-start.1 = (bf16[448,256]{1,0:T(8,128)(2,1)}, bf16[448,256]{1,0:T(8,128)(2,1)S(1)}, u32[]{:S(2)}, u32[]{:S(2)}) collective-permute-start(bf16[448,256]{1,0:T(8,128)(2,1)} %param.11), channel_id=1, source_target_pairs={{0,2},{1,258},{2,0},{3,256},{4,6},{5,262},{6,4},{7,260},{8,10},{9,... | collective-permute-start | bytes 688136 | tf_op jit(solution)/shard_map/ppermute | solution.py:35
  28.1 64.8 %collective-permute-start.7 = (bf16[384,256]{1,0:T(8,128)(2,1)S(1)}, bf16[384,256]{1,0:T(8,128)(2,1)S(1)}, u32[]{:S(2)}, u32[]{:S(2)}) collective-permute-start(bf16[384,256]{1,0:T(8,128)(2,1)S(1)} %bitcast.43), channel_id=1, source_target_pairs={{0,2},{1,3},{2,0},{3,1},{4,6},{5,7},{6,4},{7,5},{8,10},{9,11},{10,... | collective-permute-start | bytes 589832 | tf_op jit(solution)/shard_map/ppermute | solution.py:17
  32.4 60.5 %collective-permute-start.8 = (bf16[384,256]{1,0:T(8,128)(2,1)S(1)}, bf16[384,256]{1,0:T(8,128)(2,1)S(1)}, u32[]{:S(2)}, u32[]{:S(2)}) collective-permute-start(bf16[384,256]{1,0:T(8,128)(2,1)S(1)} %bitcast.44), channel_id=1, source_target_pairs={{0,3},{1,2},{2,1},{3,0},{4,7},{5,6},{6,5},{7,4},{8,11},{9,10},{10,... | collective-permute-start | bytes 589832 | tf_op jit(solution)/shard_map/ppermute | solution.py:17
  34.3 58.6 %collective-permute-start.6 = (bf16[384,256]{1,0:T(8,128)(2,1)S(1)}, bf16[384,256]{1,0:T(8,128)(2,1)S(1)}, u32[]{:S(2)}, u32[]{:S(2)}) collective-permute-start(bf16[384,256]{1,0:T(8,128)(2,1)S(1)} %bitcast.41), channel_id=1, source_target_pairs={{0,1},{1,0},{2,3},{3,2},{4,5},{5,4},{6,7},{7,6},{8,9},{9,8},{10,11... | collective-permute-start | bytes 589832 | tf_op jit(solution)/shard_map/ppermute | solution.py:17
  65.3 9.5 %collective-permute-start.2 = (bf16[1,448,256]{2,1,0:T(8,128)(2,1)}, bf16[1,448,256]{2,1,0:T(8,128)(2,1)S(1)}, u32[]{:S(2)}, u32[]{:S(2)}) collective-permute-start(bf16[1,448,256]{2,1,0:T(8,128)(2,1)} %bitcast.7), channel_id=1, source_target_pairs={{0,128},{64,192},{128,0},{192,64},{256,384},{320,448},{384,256},{4... | collective-permute-start | bytes 688136 | tf_op jit(solution)/shard_map/ppermute | solution.py:21
  68.7 10.2 %collective-permute-start.3 = (bf16[1,448,256]{2,1,0:T(8,128)(2,1)S(1)}, bf16[1,448,256]{2,1,0:T(8,128)(2,1)S(1)}, u32[]{:S(2)}, u32[]{:S(2)}) collective-permute-start(bf16[1,448,256]{2,1,0:T(8,128)(2,1)S(1)} %bitcast.45), channel_id=1, source_target_pairs={{0,384},{64,448},{128,256},{192,320},{256,128},{320,192},{384,0},{... | collective-permute-start | bytes 688136 | tf_op jit(solution)/shard_map/ppermute | solution.py:21
  75.8 14.6 %collective-permute-start.4 = (bf16[2,448,256]{2,1,0:T(8,128)(2,1)S(1)}, bf16[2,448,256]{2,1,0:T(8,128)(2,1)S(1)}, u32[]{:S(2)}, u32[]{:S(2)}) collective-permute-start(bf16[2,448,256]{2,1,0:T(8,128)(2,1)S(1)} %pad_maximum_fusion), channel_id=1, source_target_pairs={{0,384},{64,448},{128,256},{192,320},{256,128},{320,192},{384,0},{... | collective-permute-start | bytes 1376264 | tf_op jit(solution)/shard_map/ppermute | solution.py:21
  79.0 13.1 %collective-permute-start.5 = (bf16[2,448,256]{2,1,0:T(8,128)(2,1)S(1)}, bf16[2,448,256]{2,1,0:T(8,128)(2,1)S(1)}, u32[]{:S(2)}, u32[]{:S(2)}) collective-permute-start(bf16[2,448,256]{2,1,0:T(8,128)(2,1)S(1)} %pad_maximum_fusion.1), channel_id=1, source_target_pairs={{0,128},{64,192},{128,0},{192,64},{256,384},{320,448},{384,256},{4... | collective-permute-start | bytes 1376264 | tf_op jit(solution)/shard_map/ppermute | solution.py:21
  95.7 5.7 %collective-permute-start.9 = (bf16[8,448,256]{2,1,0:T(8,128)(2,1)S(1)}, bf16[8,448,256]{2,1,0:T(8,128)(2,1)S(1)}, u32[]{:S(2)}, u32[]{:S(2)}) collective-permute-start(bf16[8,448,256]{2,1,0:T(8,128)(2,1)S(1)} %get-tuple-element.22), channel_id=1, source_target_pairs={{0,64},{64,0},{128,192},{192,128},{256,320},{320,256},{384,448},{4... | collective-permute-start | bytes 5505032 | tf_op jit(solution)/shard_map/ppermute | solution.py:21
  102.0 15.7 %collective-permute-start.11 = (bf16[2,448,256]{2,1,0:T(8,128)(2,1)S(1)}, bf16[2,448,256]{2,1,0:T(8,128)(2,1)S(1)}, u32[]{:S(2)}, u32[]{:S(2)}) collective-permute-start(bf16[2,448,256]{2,1,0:T(8,128)(2,1)S(1)} %get-tuple-element.33), channel_id=1, source_target_pairs={{0,384},{64,448},{128,256},{192,320},{256,128},{320,192},{384,0},{... | collective-permute-start | bytes 1376264 | tf_op jit(solution)/shard_map/ppermute | solution.py:21
  105.9 33.4 %collective-permute-start.16 = (bf16[8,448,256]{2,1,0:T(8,128)(2,1)}, bf16[8,448,256]{2,1,0:T(8,128)(2,1)S(1)}, u32[]{:S(2)}, u32[]{:S(2)}) collective-permute-start(bf16[8,448,256]{2,1,0:T(8,128)(2,1)} %constant_dynamic-update-slice_fusion.near_ref), channel_id=1, source_target_pairs={{0,64},{64,0},{128,192},{192,128},{256,320},{320,256},{384,448},{4... | collective-permute-start | bytes 5505032 | tf_op jit(solution)/shard_map/ppermute | solution.py:21
  107.8 14.8 %collective-permute-start.10 = (bf16[2,448,256]{2,1,0:T(8,128)(2,1)S(1)}, bf16[2,448,256]{2,1,0:T(8,128)(2,1)S(1)}, u32[]{:S(2)}, u32[]{:S(2)}) collective-permute-start(bf16[2,448,256]{2,1,0:T(8,128)(2,1)S(1)} %get-tuple-element.34), channel_id=1, source_target_pairs={{0,128},{64,192},{128,0},{192,64},{256,384},{320,448},{384,256},{4... | collective-permute-start | bytes 1376264 | tf_op jit(solution)/shard_map/ppermute | solution.py:21
  122.7 9.0 %collective-permute-start.14 = (bf16[448,256]{1,0:T(8,128)(2,1)S(1)}, bf16[448,256]{1,0:T(8,128)(2,1)S(1)}, u32[]{:S(2)}, u32[]{:S(2)}) collective-permute-start(bf16[448,256]{1,0:T(8,128)(2,1)S(1)} %slice_bitcast_fusion.2), channel_id=1, source_target_pairs={{0,128},{64,192},{128,0},{192,64},{256,384},{320,448},{384,256},{4... | collective-permute-start | bytes 688136 | tf_op jit(solution)/shard_map/ppermute | solution.py:21
  125.0 12.3 %collective-permute-start.12 = (bf16[448,256]{1,0:T(8,128)(2,1)S(1)}, bf16[448,256]{1,0:T(8,128)(2,1)S(1)}, u32[]{:S(2)}, u32[]{:S(2)}) collective-permute-start(bf16[448,256]{1,0:T(8,128)(2,1)S(1)} %slice_bitcast_fusion), channel_id=1, source_target_pairs={{0,384},{64,448},{128,256},{192,320},{256,128},{320,192},{384,0},{... | collective-permute-start | bytes 688136 | tf_op jit(solution)/shard_map/ppermute | solution.py:21
  131.8 36.8 %collective-permute-start.15 = (bf16[448,256]{1,0:T(8,128)(2,1)S(1)}, bf16[448,256]{1,0:T(8,128)(2,1)S(1)}, u32[]{:S(2)}, u32[]{:S(2)}) collective-permute-start(bf16[448,256]{1,0:T(8,128)(2,1)S(1)} %fusion), channel_id=1, source_target_pairs={{2,0},{258,1},{0,2},{256,3},{6,4},{262,5},{4,6},{260,7},{10,8},{26... | collective-permute-start | bytes 688136 | tf_op jit(solution)/shard_map/ppermute | solution.py:35
  137.4 31.2 %collective-permute-start.13 = (bf16[448,256]{1,0:T(8,128)(2,1)S(1)}, bf16[448,256]{1,0:T(8,128)(2,1)S(1)}, u32[]{:S(2)}, u32[]{:S(2)}) collective-permute-start(bf16[448,256]{1,0:T(8,128)(2,1)S(1)} %fusion.1), channel_id=1, source_target_pairs={{0,0},{256,1},{2,2},{258,3},{4,4},{260,5},{6,6},{262,7},{8,8},{264... | collective-permute-start | bytes 688136 | tf_op jit(solution)/shard_map/ppermute | solution.py:35
  142.8 9.2 %collective-permute-start.17 = (bf16[384,256]{1,0:T(8,128)(2,1)S(1)}, bf16[384,256]{1,0:T(8,128)(2,1)S(1)}, u32[]{:S(2)}, u32[]{:S(2)}) collective-permute-start(bf16[384,256]{1,0:T(8,128)(2,1)S(1)} %get-tuple-element.28), channel_id=1, source_target_pairs={{0,1},{1,0},{2,3},{3,2},{4,5},{5,4},{6,7},{7,6},{8,9},{9,8},{10,11... | collective-permute-start | bytes 589832 | tf_op jit(solution)/shard_map/ppermute | solution.py:17
  144.7 17.7 %collective-permute-start.18 = (bf16[384,256]{1,0:T(8,128)(2,1)S(1)}, bf16[384,256]{1,0:T(8,128)(2,1)S(1)}, u32[]{:S(2)}, u32[]{:S(2)}) collective-permute-start(bf16[384,256]{1,0:T(8,128)(2,1)S(1)} %get-tuple-element.29), channel_id=1, source_target_pairs={{0,2},{1,3},{2,0},{3,1},{4,6},{5,7},{6,4},{7,5},{8,10},{9,11},{10,... | collective-permute-start | bytes 589832 | tf_op jit(solution)/shard_map/ppermute | solution.py:17
  149.5 17.2 %collective-permute-start.19 = (bf16[384,256]{1,0:T(8,128)(2,1)S(1)}, bf16[384,256]{1,0:T(8,128)(2,1)S(1)}, u32[]{:S(2)}, u32[]{:S(2)}) collective-permute-start(bf16[384,256]{1,0:T(8,128)(2,1)S(1)} %get-tuple-element.30), channel_id=1, source_target_pairs={{0,3},{1,2},{2,1},{3,0},{4,7},{5,6},{6,5},{7,4},{8,11},{9,10},{10,... | collective-permute-start | bytes 589832 | tf_op jit(solution)/shard_map/ppermute | solution.py:17

commit v6 on v4

--- a/solution.py
+++ b/solution.py
@@ -165,6 +165,26 @@
     )(scalars, recv, *pieces)
 
 
+def stacked_body(*refs):
+    at = 0
+    for ref in refs[:-1]:
+        refs[-1][at : at + ref.shape[0]] = ref[...]
+        at += ref.shape[0]
+
+
+def stacked(values):
+    total = sum(value.shape[0] for value in values)
+    return pl.pallas_call(
+        stacked_body,
+        in_specs=[WHOLE] * len(values),
+        out_specs=WHOLE,
+        out_shape=jax.ShapeDtypeStruct((total, *values[0].shape[1:]), BF),
+        compiler_params=pltpu.CompilerParams(vmem_limit_bytes=VMEM_LIMIT // 4),
+        cost_estimate=cost(values[0].size * 8, values[0].size * 32),
+        name="stacked",
+    )(*values)
+
+
 def upstream_body(s_ref, rows_ref, near_ref, far_ref, *out_refs):
     core, a1, a0 = s_ref[0], s_ref[1], s_ref[2]
     for q in range(4):
@@ -253,8 +273,8 @@
     recv = dispatched(slots.reshape(devices // 2, PART, slots.shape[3]))
     own = [value[None] for value in own]
     ahead, behind = dp_xor(own[0], 2), dp_xor(own[1], 6)
-    low = dp_xor(jnp.concatenate([own[0], ahead]), 6)
-    high = dp_xor(jnp.concatenate([own[1], behind]), 2)
+    low = dp_xor(stacked([own[0], ahead]), 6)
+    high = dp_xor(stacked([own[1], behind]), 2)
     near = jnp.concatenate(own + [ahead, behind, low, high])
     far = dp_xor(near, 1)
 

time: 167 us -> 167 us (level)
  the two profiles are of different devices: /device:TPU:96 before, /device:TPU:64 now
where the time goes in v6:
time: 167 us; the launch traced here: 166 us
  starting transfers between devices  80.5 us (48%)
  waiting for transfers between devices  66 us (40%)
  Pallas kernels  12.4 us (7%)
  local copies, waits for them, and re-layouts  4.53 us (3%)
  other arithmetic  1.71 us (1%)
    ppermute x4, waiting for transfers between devices, swapped(): return lax.ppermute(value, ('dp', 'expert'), pairs)  26.6 us
    ppermute x10, starting transfers between devices, dp_xor(): lax.ppermute(value, 'dp', [(i, i ^ mask) for i in range(lax.axis_size('dp...  26.5 us
    ppermute x10, waiting for transfers between devices, dp_xor(): lax.ppermute(value, 'dp', [(i, i ^ mask) for i in range(lax.axis_size('dp...  24.9 us
    ppermute x6, starting transfers between devices, expert_xor(): lax.ppermute(value, 'expert', [(i, i ^ mask) for i in range(lax.axis_size...  19.3 us
    ppermute x4, starting transfers between devices, swapped(): return lax.ppermute(value, ('dp', 'expert'), pairs)  19.1 us
    all_to_all x1, starting transfers between devices, dispatched(): lax.all_to_all(slots, 'expert', split_axis=0, concat_axis=0, tiled=True,...  15.5 us
    ppermute x6, waiting for transfers between devices, expert_xor(): lax.ppermute(value, 'expert', [(i, i ^ mask) for i in range(lax.axis_size...  14.4 us
    unnamed x9, local copies, waits for them, and re-layouts  3.62 us
  transfers between devices with their start and end apart: 21, of which 11 were waited for; matrix products, arithmetic and copies ran while one was open for 3% of the time, Pallas kernels for 4%

profile of v6, /device:TPU:64, one launch (start us, length us, event | category | flops | bytes accessed | tf_op | source)
XLA Modules:
  0.0 166.0 jit_solution(11028301073191001462)
XLA Ops:
  0.6 3.2 %slots.1 = bf16[16,2,24,896]{3,2,1,0:T(8,128)(2,1)} custom-call(s32[1,128]{1,0:T(1,128)} %bitcast.53, f32[1,128]{1,0:T(1,128)} %bitcast.54, bf16[128,3584]{1,0:T(8,128)(2,1)} %cot_ref.1), custom_call_target="tpu_custom_call" | custom-call | flops 704643072 | bytes 1835008 | tf_op jit(solution)/shard_map/slots/pallas_call | solution.py:72
  3.8 15.5 %all-to-all-start = ((bf16[32,24,896]{2,1,0:T(8,128)(2,1)}), bf16[32,24,896]{2,1,0:T(8,128)(2,1)S(1)}, u32[]{:S(2)}, u32[]{:S(2)}) async-start(bf16[32,24,896]{2,1,0:T(8,128)(2,1)} %bitcast.6), calls=%async_computation | async-start | bytes 2752512 | tf_op jit(solution)/shard_map/all_to_all | solution.py:251
  19.3 4.6 %collective-permute-start = (bf16[448,256]{1,0:T(8,128)(2,1)}, bf16[448,256]{1,0:T(8,128)(2,1)S(1)}, u32[]{:S(2)}, u32[]{:S(2)}) collective-permute-start(bf16[448,256]{1,0:T(8,128)(2,1)} %param.11), channel_id=1, source_target_pairs={{0,0},{1,256},{2,2},{3,258},{4,4},{5,260},{6,6},{7,262},{8,8},{9,2... | collective-permute-start | bytes 688136 | tf_op jit(solution)/shard_map/ppermute | solution.py:35
  23.9 3.7 %collective-permute-start.1 = (bf16[448,256]{1,0:T(8,128)(2,1)}, bf16[448,256]{1,0:T(8,128)(2,1)S(1)}, u32[]{:S(2)}, u32[]{:S(2)}) collective-permute-start(bf16[448,256]{1,0:T(8,128)(2,1)} %param.11), channel_id=1, source_target_pairs={{0,2},{1,258},{2,0},{3,256},{4,6},{5,262},{6,4},{7,260},{8,10},{9,... | collective-permute-start | bytes 688136 | tf_op jit(solution)/shard_map/ppermute | solution.py:35
  28.5 4.3 %collective-permute-start.7 = (bf16[384,256]{1,0:T(8,128)(2,1)S(1)}, bf16[384,256]{1,0:T(8,128)(2,1)S(1)}, u32[]{:S(2)}, u32[]{:S(2)}) collective-permute-start(bf16[384,256]{1,0:T(8,128)(2,1)S(1)} %bitcast.49), channel_id=1, source_target_pairs={{0,2},{1,3},{2,0},{3,1},{4,6},{5,7},{6,4},{7,5},{8,10},{9,11},{10,... | collective-permute-start | bytes 589832 | tf_op jit(solution)/shard_map/ppermute | solution.py:17
  32.8 1.9 %collective-permute-start.8 = (bf16[384,256]{1,0:T(8,128)(2,1)S(1)}, bf16[384,256]{1,0:T(8,128)(2,1)S(1)}, u32[]{:S(2)}, u32[]{:S(2)}) collective-permute-start(bf16[384,256]{1,0:T(8,128)(2,1)S(1)} %bitcast.50), channel_id=1, source_target_pairs={{0,3},{1,2},{2,1},{3,0},{4,7},{5,6},{6,5},{7,4},{8,11},{9,10},{10,... | collective-permute-start | bytes 589832 | tf_op jit(solution)/shard_map/ppermute | solution.py:17
  34.7 3.9 %collective-permute-start.6 = (bf16[384,256]{1,0:T(8,128)(2,1)S(1)}, bf16[384,256]{1,0:T(8,128)(2,1)}, u32[]{:S(2)}, u32[]{:S(2)}) collective-permute-start(bf16[384,256]{1,0:T(8,128)(2,1)S(1)} %bitcast.47), channel_id=1, source_target_pairs={{0,1},{1,0},{2,3},{3,2},{4,5},{5,4},{6,7},{7,6},{8,9},{9,8},{10,11... | collective-permute-start | bytes 589832 | tf_op jit(solution)/shard_map/ppermute | solution.py:17
  38.6 26.6 %collective-permute-done = bf16[448,256]{1,0:T(8,128)(2,1)S(1)} collective-permute-done((bf16[448,256]{1,0:T(8,128)(2,1)}, bf16[448,256]{1,0:T(8,128)(2,1)S(1)}, u32[]{:S(2)}, u32[]{:S(2)}) %collective-permute-start) | collective-permute-done | bytes 229408 | tf_op jit(solution)/shard_map/ppermute | solution.py:35
  65.3 3.4 %collective-permute-start.2 = (bf16[1,448,256]{2,1,0:T(8,128)(2,1)S(1)}, bf16[1,448,256]{2,1,0:T(8,128)(2,1)S(1)}, u32[]{:S(2)}, u32[]{:S(2)}) collective-permute-start(bf16[1,448,256]{2,1,0:T(8,128)(2,1)S(1)} %bitcast.41), channel_id=1, source_target_pairs={{0,128},{64,192},{128,0},{192,64},{256,384},{320,448},{384,256},{4... | collective-permute-start | bytes 688136 | tf_op jit(solution)/shard_map/ppermute | solution.py:21
  68.7 1.9 %collective-permute-start.3 = (bf16[1,448,256]{2,1,0:T(8,128)(2,1)S(1)}, bf16[1,448,256]{2,1,0:T(8,128)(2,1)S(1)}, u32[]{:S(2)}, u32[]{:S(2)}) collective-permute-start(bf16[1,448,256]{2,1,0:T(8,128)(2,1)S(1)} %bitcast.39), channel_id=1, source_target_pairs={{0,384},{64,448},{128,256},{192,320},{256,128},{320,192},{384,0},{... | collective-permute-start | bytes 688136 | tf_op jit(solution)/shard_map/ppermute | solution.py:21
  73.2 3.3 %collective-permute-start.4 = (bf16[2,448,256]{2,1,0:T(8,128)(2,1)S(1)}, bf16[2,448,256]{2,1,0:T(8,128)(2,1)S(1)}, u32[]{:S(2)}, u32[]{:S(2)}) collective-permute-start(bf16[2,448,256]{2,1,0:T(8,128)(2,1)S(1)} %stacked.2), channel_id=1, source_target_pairs={{0,384},{64,448},{128,256},{192,320},{256,128},{320,192},{384,0},{... | collective-permute-start | bytes 1376264 | tf_op jit(solution)/shard_map/ppermute | solution.py:21
  78.4 2.2 %collective-permute-start.5 = (bf16[2,448,256]{2,1,0:T(8,128)(2,1)S(1)}, bf16[2,448,256]{2,1,0:T(8,128)(2,1)S(1)}, u32[]{:S(2)}, u32[]{:S(2)}) collective-permute-start(bf16[2,448,256]{2,1,0:T(8,128)(2,1)S(1)} %stacked.3), channel_id=1, source_target_pairs={{0,128},{64,192},{128,0},{192,64},{256,384},{320,448},{384,256},{4... | collective-permute-start | bytes 1376264 | tf_op jit(solution)/shard_map/ppermute | solution.py:21
  82.7 2.1 %collective-permute-done.4 = bf16[2,448,256]{2,1,0:T(8,128)(2,1)S(1)} collective-permute-done((bf16[2,448,256]{2,1,0:T(8,128)(2,1)S(1)}, bf16[2,448,256]{2,1,0:T(8,128)(2,1)S(1)}, u32[]{:S(2)}, u32[]{:S(2)}) %collective-permute-start.4) | collective-permute-done | bytes 458784 | tf_op jit(solution)/shard_map/ppermute | solution.py:21
  85.6 3.2 %collective-permute-done.5 = bf16[2,448,256]{2,1,0:T(8,128)(2,1)S(1)} collective-permute-done((bf16[2,448,256]{2,1,0:T(8,128)(2,1)S(1)}, bf16[2,448,256]{2,1,0:T(8,128)(2,1)S(1)}, u32[]{:S(2)}, u32[]{:S(2)}) %collective-permute-start.5) | collective-permute-done | bytes 458784 | tf_op jit(solution)/shard_map/ppermute | solution.py:21
  89.6 3.2 %weight_partial.1 = (bf16[2,384,896]{2,1,0:T(8,128)(2,1)S(1)}, bf16[8,448,256]{2,1,0:T(8,128)(2,1)S(1)}, bf16[8,448,256]{2,1,0:T(8,128)(2,1)S(1)}) custom-call(s32[4]{0:T(128)S(1)} %pad_add_fusion.s_ref, bf16[32,24,896]{2,1,0:T(8,128)(2,1)S(1)} %all-to-all-done.recv_ref, bf16[384,256]{1,0:T(8,128)(2,1)S(1)} %bitcast.48, ...), custom_call_target="tpu_custom_call" | custom-call | flops 1409286144 | bytes 2752512 | tf_op jit(solution)/shard_map/weight_partial/pallas_call | solution.py:157
  92.8 1.9 %collective-permute-start.9 = (bf16[8,448,256]{2,1,0:T(8,128)(2,1)S(1)}, bf16[8,448,256]{2,1,0:T(8,128)(2,1)S(1)}, u32[]{:S(2)}, u32[]{:S(2)}) collective-permute-start(bf16[8,448,256]{2,1,0:T(8,128)(2,1)S(1)} %get-tuple-element.20), channel_id=1, source_target_pairs={{0,64},{64,0},{128,192},{192,128},{256,320},{320,256},{384,448},{4... | collective-permute-start | bytes 5505032 | tf_op jit(solution)/shard_map/ppermute | solution.py:21
  94.7 2.4 %collective-permute-start.16 = (bf16[8,448,256]{2,1,0:T(8,128)(2,1)}, bf16[8,448,256]{2,1,0:T(8,128)(2,1)S(1)}, u32[]{:S(2)}, u32[]{:S(2)}) collective-permute-start(bf16[8,448,256]{2,1,0:T(8,128)(2,1)} %constant_dynamic-update-slice_fusion.near_ref), channel_id=1, source_target_pairs={{0,64},{64,0},{128,192},{192,128},{256,320},{320,256},{384,448},{4... | collective-permute-start | bytes 5505032 | tf_op jit(solution)/shard_map/ppermute | solution.py:21
  99.0 2.2 %collective-permute-start.10 = (bf16[2,448,256]{2,1,0:T(8,128)(2,1)S(1)}, bf16[2,448,256]{2,1,0:T(8,128)(2,1)S(1)}, u32[]{:S(2)}, u32[]{:S(2)}) collective-permute-start(bf16[2,448,256]{2,1,0:T(8,128)(2,1)S(1)} %get-tuple-element.31), channel_id=1, source_target_pairs={{0,128},{64,192},{128,0},{192,64},{256,384},{320,448},{384,256},{4... | collective-permute-start | bytes 1376264 | tf_op jit(solution)/shard_map/ppermute | solution.py:21
  101.2 3.3 %collective-permute-start.13 = (bf16[2,448,256]{2,1,0:T(8,128)(2,1)S(1)}, bf16[2,448,256]{2,1,0:T(8,128)(2,1)S(1)}, u32[]{:S(2)}, u32[]{:S(2)}) collective-permute-start(bf16[2,448,256]{2,1,0:T(8,128)(2,1)S(1)} %get-tuple-element.32), channel_id=1, source_target_pairs={{0,384},{64,448},{128,256},{192,320},{256,128},{320,192},{384,0},{... | collective-permute-start | bytes 1376264 | tf_op jit(solution)/shard_map/ppermute | solution.py:21
  104.5 9.0 %collective-permute-done.10 = bf16[2,448,256]{2,1,0:T(8,128)(2,1)S(1)} collective-permute-done((bf16[2,448,256]{2,1,0:T(8,128)(2,1)S(1)}, bf16[2,448,256]{2,1,0:T(8,128)(2,1)S(1)}, u32[]{:S(2)}, u32[]{:S(2)}) %collective-permute-start.10) | collective-permute-done | bytes 458784 | tf_op jit(solution)/shard_map/ppermute | solution.py:21
  113.5 3.1 %collective-permute-done.13 = bf16[2,448,256]{2,1,0:T(8,128)(2,1)S(1)} collective-permute-done((bf16[2,448,256]{2,1,0:T(8,128)(2,1)S(1)}, bf16[2,448,256]{2,1,0:T(8,128)(2,1)S(1)}, u32[]{:S(2)}, u32[]{:S(2)}) %collective-permute-start.13) | collective-permute-done | bytes 458784 | tf_op jit(solution)/shard_map/ppermute | solution.py:21
  116.9 2.4 %collective-permute-start.14 = (bf16[448,256]{1,0:T(8,128)(2,1)S(1)}, bf16[448,256]{1,0:T(8,128)(2,1)S(1)}, u32[]{:S(2)}, u32[]{:S(2)}) collective-permute-start(bf16[448,256]{1,0:T(8,128)(2,1)S(1)} %slice_bitcast_fusion), channel_id=1, source_target_pairs={{0,128},{64,192},{128,0},{192,64},{256,384},{320,448},{384,256},{4... | collective-permute-start | bytes 688136 | tf_op jit(solution)/shard_map/ppermute | solution.py:21
  119.4 3.5 %collective-permute-start.11 = (bf16[448,256]{1,0:T(8,128)(2,1)S(1)}, bf16[448,256]{1,0:T(8,128)(2,1)S(1)}, u32[]{:S(2)}, u32[]{:S(2)}) collective-permute-start(bf16[448,256]{1,0:T(8,128)(2,1)S(1)} %slice_bitcast_fusion.2), channel_id=1, source_target_pairs={{0,384},{64,448},{128,256},{192,320},{256,128},{320,192},{384,0},{... | collective-permute-start | bytes 688136 | tf_op jit(solution)/shard_map/ppermute | solution.py:21
  122.9 2.4 %collective-permute-done.14 = bf16[448,256]{1,0:T(8,128)(2,1)S(1)} collective-permute-done((bf16[448,256]{1,0:T(8,128)(2,1)S(1)}, bf16[448,256]{1,0:T(8,128)(2,1)S(1)}, u32[]{:S(2)}, u32[]{:S(2)}) %collective-permute-start.14) | collective-permute-done | bytes 229408 | tf_op jit(solution)/shard_map/ppermute | solution.py:21
  125.4 8.9 %collective-permute-start.15 = (bf16[448,256]{1,0:T(8,128)(2,1)S(1)}, bf16[448,256]{1,0:T(8,128)(2,1)S(1)}, u32[]{:S(2)}, u32[]{:S(2)}) collective-permute-start(bf16[448,256]{1,0:T(8,128)(2,1)S(1)} %fusion), channel_id=1, source_target_pairs={{2,0},{258,1},{0,2},{256,3},{6,4},{262,5},{4,6},{260,7},{10,8},{26... | collective-permute-start | bytes 688136 | tf_op jit(solution)/shard_map/ppermute | solution.py:35
  134.4 1.9 %collective-permute-start.12 = (bf16[448,256]{1,0:T(8,128)(2,1)S(1)}, bf16[448,256]{1,0:T(8,128)(2,1)S(1)}, u32[]{:S(2)}, u32[]{:S(2)}) collective-permute-start(bf16[448,256]{1,0:T(8,128)(2,1)S(1)} %fusion.1), channel_id=1, source_target_pairs={{0,0},{256,1},{2,2},{258,3},{4,4},{260,5},{6,6},{262,7},{8,8},{264... | collective-permute-start | bytes 688136 | tf_op jit(solution)/shard_map/ppermute | solution.py:35
  136.4 3.4 %upstream_partial.1 = (bf16[384,256]{1,0:T(8,128)(2,1)S(1)}, bf16[384,256]{1,0:T(8,128)(2,1)S(1)}, bf16[384,256]{1,0:T(8,128)(2,1)S(1)}, bf16[384,256]{1,0:T(8,128)(2,1)S(1)}) custom-call(s32[4]{0:T(128)S(1)} %pad_add_fusion.s_ref, bf16[2,384,896]{2,1,0:T(8,128)(2,1)S(1)} %get-tuple-element.21.rows_ref, ...), custom_call_target="tpu_custom_call" | custom-call | flops 1409286144 | bytes 2752512 | tf_op jit(solution)/shard_map/upstream_partial/pallas_call | solution.py:207
  139.8 1.9 %collective-permute-start.17 = (bf16[384,256]{1,0:T(8,128)(2,1)S(1)}, bf16[384,256]{1,0:T(8,128)(2,1)S(1)}, u32[]{:S(2)}, u32[]{:S(2)}) collective-permute-start(bf16[384,256]{1,0:T(8,128)(2,1)S(1)} %get-tuple-element.24), channel_id=1, source_target_pairs={{0,1},{1,0},{2,3},{3,2},{4,5},{5,4},{6,7},{7,6},{8,9},{9,8},{10,11... | collective-permute-start | bytes 589832 | tf_op jit(solution)/shard_map/ppermute | solution.py:17
  141.7 4.1 %collective-permute-start.18 = (bf16[384,256]{1,0:T(8,128)(2,1)S(1)}, bf16[384,256]{1,0:T(8,128)(2,1)S(1)}, u32[]{:S(2)}, u32[]{:S(2)}) collective-permute-start(bf16[384,256]{1,0:T(8,128)(2,1)S(1)} %get-tuple-element.25), channel_id=1, source_target_pairs={{0,2},{1,3},{2,0},{3,1},{4,6},{5,7},{6,4},{7,5},{8,10},{9,11},{10,... | collective-permute-start | bytes 589832 | tf_op jit(solution)/shard_map/ppermute | solution.py:17
  145.8 3.2 %collective-permute-start.19 = (bf16[384,256]{1,0:T(8,128)(2,1)S(1)}, bf16[384,256]{1,0:T(8,128)(2,1)S(1)}, u32[]{:S(2)}, u32[]{:S(2)}) collective-permute-start(bf16[384,256]{1,0:T(8,128)(2,1)S(1)} %get-tuple-element.26), channel_id=1, source_target_pairs={{0,3},{1,2},{2,1},{3,0},{4,7},{5,6},{6,5},{7,4},{8,11},{9,10},{10,... | collective-permute-start | bytes 589832 | tf_op jit(solution)/shard_map/ppermute | solution.py:17
  149.0 10.4 %collective-permute-done.18 = bf16[384,256]{1,0:T(8,128)(2,1)S(1)} collective-permute-done((bf16[384,256]{1,0:T(8,128)(2,1)S(1)}, bf16[384,256]{1,0:T(8,128)(2,1)S(1)}, u32[]{:S(2)}, u32[]{:S(2)}) %collective-permute-start.18) | collective-permute-done | bytes 196640 | tf_op jit(solution)/shard_map/ppermute | solution.py:17
  159.4 4.0 %collective-permute-done.19 = bf16[384,256]{1,0:T(8,128)(2,1)S(1)} collective-permute-done((bf16[384,256]{1,0:T(8,128)(2,1)S(1)}, bf16[384,256]{1,0:T(8,128)(2,1)S(1)}, u32[]{:S(2)}, u32[]{:S(2)}) %collective-permute-start.19) | collective-permute-done | bytes 196640 | tf_op jit(solution)/shard_map/ppermute | solution.py:17
  (36 shorter events, 14.0 us)
Async XLA Ops:
  3.8 23.9 %copy-start = (bf16[768,256]{1,0:T(8,128)(2,1)S(1)}, bf16[768,256]{1,0:T(8,128)(2,1)}, u32[]{:S(2)}) copy-start(bf16[768,256]{1,0:T(8,128)(2,1)} %param.9) | copy-start | bytes 1179652
  3.8 23.9 %copy-start.1 = (bf16[768,256]{1,0:T(8,128)(2,1)S(1)}, bf16[768,256]{1,0:T(8,128)(2,1)}, u32[]{:S(2)}) copy-start(bf16[768,256]{1,0:T(8,128)(2,1)} %param.10) | copy-start | bytes 1179652
  3.8 85.8 %all-to-all-start = ((bf16[32,24,896]{2,1,0:T(8,128)(2,1)}), bf16[32,24,896]{2,1,0:T(8,128)(2,1)S(1)}, u32[]{:S(2)}, u32[]{:S(2)}) async-start(bf16[32,24,896]{2,1,0:T(8,128)(2,1)} %bitcast.6), calls=%async_computation | async-start | bytes 2752512 | tf_op jit(solution)/shard_map/all_to_all | solution.py:251
  19.3 45.9 %collective-permute-start = (bf16[448,256]{1,0:T(8,128)(2,1)}, bf16[448,256]{1,0:T(8,128)(2,1)S(1)}, u32[]{:S(2)}, u32[]{:S(2)}) collective-permute-start(bf16[448,256]{1,0:T(8,128)(2,1)} %param.11), channel_id=1, source_target_pairs={{0,0},{1,256},{2,2},{3,258},{4,4},{5,260},{6,6},{7,262},{8,8},{9,2... | collective-permute-start | bytes 688136 | tf_op jit(solution)/shard_map/ppermute | solution.py:35
  23.9 44.7 %collective-permute-start.1 = (bf16[448,256]{1,0:T(8,128)(2,1)}, bf16[448,256]{1,0:T(8,128)(2,1)S(1)}, u32[]{:S(2)}, u32[]{:S(2)}) collective-permute-start(bf16[448,256]{1,0:T(8,128)(2,1)} %param.11), channel_id=1, source_target_pairs={{0,2},{1,258},{2,0},{3,256},{4,6},{5,262},{6,4},{7,260},{8,10},{9,... | collective-permute-start | bytes 688136 | tf_op jit(solution)/shard_map/ppermute | solution.py:35
  28.5 61.1 %collective-permute-start.7 = (bf16[384,256]{1,0:T(8,128)(2,1)S(1)}, bf16[384,256]{1,0:T(8,128)(2,1)S(1)}, u32[]{:S(2)}, u32[]{:S(2)}) collective-permute-start(bf16[384,256]{1,0:T(8,128)(2,1)S(1)} %bitcast.49), channel_id=1, source_target_pairs={{0,2},{1,3},{2,0},{3,1},{4,6},{5,7},{6,4},{7,5},{8,10},{9,11},{10,... | collective-permute-start | bytes 589832 | tf_op jit(solution)/shard_map/ppermute | solution.py:17
  32.8 56.8 %collective-permute-start.8 = (bf16[384,256]{1,0:T(8,128)(2,1)S(1)}, bf16[384,256]{1,0:T(8,128)(2,1)S(1)}, u32[]{:S(2)}, u32[]{:S(2)}) collective-permute-start(bf16[384,256]{1,0:T(8,128)(2,1)S(1)} %bitcast.50), channel_id=1, source_target_pairs={{0,3},{1,2},{2,1},{3,0},{4,7},{5,6},{6,5},{7,4},{8,11},{9,10},{10,... | collective-permute-start | bytes 589832 | tf_op jit(solution)/shard_map/ppermute | solution.py:17
  34.7 54.9 %collective-permute-start.6 = (bf16[384,256]{1,0:T(8,128)(2,1)S(1)}, bf16[384,256]{1,0:T(8,128)(2,1)}, u32[]{:S(2)}, u32[]{:S(2)}) collective-permute-start(bf16[384,256]{1,0:T(8,128)(2,1)S(1)} %bitcast.47), channel_id=1, source_target_pairs={{0,1},{1,0},{2,3},{3,2},{4,5},{5,4},{6,7},{7,6},{8,9},{9,8},{10,11... | collective-permute-start | bytes 589832 | tf_op jit(solution)/shard_map/ppermute | solution.py:17
  65.3 7.9 %collective-permute-start.2 = (bf16[1,448,256]{2,1,0:T(8,128)(2,1)S(1)}, bf16[1,448,256]{2,1,0:T(8,128)(2,1)S(1)}, u32[]{:S(2)}, u32[]{:S(2)}) collective-permute-start(bf16[1,448,256]{2,1,0:T(8,128)(2,1)S(1)} %bitcast.41), channel_id=1, source_target_pairs={{0,128},{64,192},{128,0},{192,64},{256,384},{320,448},{384,256},{4... | collective-permute-start | bytes 688136 | tf_op jit(solution)/shard_map/ppermute | solution.py:21
  68.7 9.7 %collective-permute-start.3 = (bf16[1,448,256]{2,1,0:T(8,128)(2,1)S(1)}, bf16[1,448,256]{2,1,0:T(8,128)(2,1)S(1)}, u32[]{:S(2)}, u32[]{:S(2)}) collective-permute-start(bf16[1,448,256]{2,1,0:T(8,128)(2,1)S(1)} %bitcast.39), channel_id=1, source_target_pairs={{0,384},{64,448},{128,256},{192,320},{256,128},{320,192},{384,0},{... | collective-permute-start | bytes 688136 | tf_op jit(solution)/shard_map/ppermute | solution.py:21
  73.2 11.6 %collective-permute-start.4 = (bf16[2,448,256]{2,1,0:T(8,128)(2,1)S(1)}, bf16[2,448,256]{2,1,0:T(8,128)(2,1)S(1)}, u32[]{:S(2)}, u32[]{:S(2)}) collective-permute-start(bf16[2,448,256]{2,1,0:T(8,128)(2,1)S(1)} %stacked.2), channel_id=1, source_target_pairs={{0,384},{64,448},{128,256},{192,320},{256,128},{320,192},{384,0},{... | collective-permute-start | bytes 1376264 | tf_op jit(solution)/shard_map/ppermute | solution.py:21
  78.4 10.4 %collective-permute-start.5 = (bf16[2,448,256]{2,1,0:T(8,128)(2,1)S(1)}, bf16[2,448,256]{2,1,0:T(8,128)(2,1)S(1)}, u32[]{:S(2)}, u32[]{:S(2)}) collective-permute-start(bf16[2,448,256]{2,1,0:T(8,128)(2,1)S(1)} %stacked.3), channel_id=1, source_target_pairs={{0,128},{64,192},{128,0},{192,64},{256,384},{320,448},{384,256},{4... | collective-permute-start | bytes 1376264 | tf_op jit(solution)/shard_map/ppermute | solution.py:21
  92.8 5.7 %collective-permute-start.9 = (bf16[8,448,256]{2,1,0:T(8,128)(2,1)S(1)}, bf16[8,448,256]{2,1,0:T(8,128)(2,1)S(1)}, u32[]{:S(2)}, u32[]{:S(2)}) collective-permute-start(bf16[8,448,256]{2,1,0:T(8,128)(2,1)S(1)} %get-tuple-element.20), channel_id=1, source_target_pairs={{0,64},{64,0},{128,192},{192,128},{256,320},{320,256},{384,448},{4... | collective-permute-start | bytes 5505032 | tf_op jit(solution)/shard_map/ppermute | solution.py:21
  94.7 41.6 %collective-permute-start.16 = (bf16[8,448,256]{2,1,0:T(8,128)(2,1)}, bf16[8,448,256]{2,1,0:T(8,128)(2,1)S(1)}, u32[]{:S(2)}, u32[]{:S(2)}) collective-permute-start(bf16[8,448,256]{2,1,0:T(8,128)(2,1)} %constant_dynamic-update-slice_fusion.near_ref), channel_id=1, source_target_pairs={{0,64},{64,0},{128,192},{192,128},{256,320},{320,256},{384,448},{4... | collective-permute-start | bytes 5505032 | tf_op jit(solution)/shard_map/ppermute | solution.py:21
  99.0 14.5 %collective-permute-start.10 = (bf16[2,448,256]{2,1,0:T(8,128)(2,1)S(1)}, bf16[2,448,256]{2,1,0:T(8,128)(2,1)S(1)}, u32[]{:S(2)}, u32[]{:S(2)}) collective-permute-start(bf16[2,448,256]{2,1,0:T(8,128)(2,1)S(1)} %get-tuple-element.31), channel_id=1, source_target_pairs={{0,128},{64,192},{128,0},{192,64},{256,384},{320,448},{384,256},{4... | collective-permute-start | bytes 1376264 | tf_op jit(solution)/shard_map/ppermute | solution.py:21
  101.2 15.4 %collective-permute-start.13 = (bf16[2,448,256]{2,1,0:T(8,128)(2,1)S(1)}, bf16[2,448,256]{2,1,0:T(8,128)(2,1)S(1)}, u32[]{:S(2)}, u32[]{:S(2)}) collective-permute-start(bf16[2,448,256]{2,1,0:T(8,128)(2,1)S(1)} %get-tuple-element.32), channel_id=1, source_target_pairs={{0,384},{64,448},{128,256},{192,320},{256,128},{320,192},{384,0},{... | collective-permute-start | bytes 1376264 | tf_op jit(solution)/shard_map/ppermute | solution.py:21
  116.9 8.4 %collective-permute-start.14 = (bf16[448,256]{1,0:T(8,128)(2,1)S(1)}, bf16[448,256]{1,0:T(8,128)(2,1)S(1)}, u32[]{:S(2)}, u32[]{:S(2)}) collective-permute-start(bf16[448,256]{1,0:T(8,128)(2,1)S(1)} %slice_bitcast_fusion), channel_id=1, source_target_pairs={{0,128},{64,192},{128,0},{192,64},{256,384},{320,448},{384,256},{4... | collective-permute-start | bytes 688136 | tf_op jit(solution)/shard_map/ppermute | solution.py:21
  119.4 15.0 %collective-permute-start.11 = (bf16[448,256]{1,0:T(8,128)(2,1)S(1)}, bf16[448,256]{1,0:T(8,128)(2,1)S(1)}, u32[]{:S(2)}, u32[]{:S(2)}) collective-permute-start(bf16[448,256]{1,0:T(8,128)(2,1)S(1)} %slice_bitcast_fusion.2), channel_id=1, source_target_pairs={{0,384},{64,448},{128,256},{192,320},{256,128},{320,192},{384,0},{... | collective-permute-start | bytes 688136 | tf_op jit(solution)/shard_map/ppermute | solution.py:21
  125.4 39.8 %collective-permute-start.15 = (bf16[448,256]{1,0:T(8,128)(2,1)S(1)}, bf16[448,256]{1,0:T(8,128)(2,1)S(1)}, u32[]{:S(2)}, u32[]{:S(2)}) collective-permute-start(bf16[448,256]{1,0:T(8,128)(2,1)S(1)} %fusion), channel_id=1, source_target_pairs={{2,0},{258,1},{0,2},{256,3},{6,4},{262,5},{4,6},{260,7},{10,8},{26... | collective-permute-start | bytes 688136 | tf_op jit(solution)/shard_map/ppermute | solution.py:35
  134.4 30.8 %collective-permute-start.12 = (bf16[448,256]{1,0:T(8,128)(2,1)S(1)}, bf16[448,256]{1,0:T(8,128)(2,1)S(1)}, u32[]{:S(2)}, u32[]{:S(2)}) collective-permute-start(bf16[448,256]{1,0:T(8,128)(2,1)S(1)} %fusion.1), channel_id=1, source_target_pairs={{0,0},{256,1},{2,2},{258,3},{4,4},{260,5},{6,6},{262,7},{8,8},{264... | collective-permute-start | bytes 688136 | tf_op jit(solution)/shard_map/ppermute | solution.py:35
  139.8 9.2 %collective-permute-start.17 = (bf16[384,256]{1,0:T(8,128)(2,1)S(1)}, bf16[384,256]{1,0:T(8,128)(2,1)S(1)}, u32[]{:S(2)}, u32[]{:S(2)}) collective-permute-start(bf16[384,256]{1,0:T(8,128)(2,1)S(1)} %get-tuple-element.24), channel_id=1, source_target_pairs={{0,1},{1,0},{2,3},{3,2},{4,5},{5,4},{6,7},{7,6},{8,9},{9,8},{10,11... | collective-permute-start | bytes 589832 | tf_op jit(solution)/shard_map/ppermute | solution.py:17
  141.7 17.8 %collective-permute-start.18 = (bf16[384,256]{1,0:T(8,128)(2,1)S(1)}, bf16[384,256]{1,0:T(8,128)(2,1)S(1)}, u32[]{:S(2)}, u32[]{:S(2)}) collective-permute-start(bf16[384,256]{1,0:T(8,128)(2,1)S(1)} %get-tuple-element.25), channel_id=1, source_target_pairs={{0,2},{1,3},{2,0},{3,1},{4,6},{5,7},{6,4},{7,5},{8,10},{9,11},{10,... | collective-permute-start | bytes 589832 | tf_op jit(solution)/shard_map/ppermute | solution.py:17
  145.8 17.7 %collective-permute-start.19 = (bf16[384,256]{1,0:T(8,128)(2,1)S(1)}, bf16[384,256]{1,0:T(8,128)(2,1)S(1)}, u32[]{:S(2)}, u32[]{:S(2)}) collective-permute-start(bf16[384,256]{1,0:T(8,128)(2,1)S(1)} %get-tuple-element.26), channel_id=1, source_target_pairs={{0,3},{1,2},{2,1},{3,0},{4,7},{5,6},{6,5},{7,4},{8,11},{9,10},{10,... | collective-permute-start | bytes 589832 | tf_op jit(solution)/shard_map/ppermute | solution.py:17
